TPU v7x, 768 devices: a whole 4x8x12 slice. The times are simulated.
768 devices in a mesh: section: 2 (over core), mp: 8 (over y_lo, x), dp: 48 (over z, y_hi).
Axes of the slice: x: 4, y: 8 (y_hi: 4, y_lo: 2; y = y_hi * 2 + y_lo), z: 12, core: 2. Of those that a mesh axis runs over, the one named last changes fastest.
Arguments:
- value_grad: bfloat16 [2, 24576, 3072], P('section', 'dp', 'mp'), may hold values from -6 to 6
- stream: bfloat16 [2, 24576, 3072], P('section', 'dp'), may hold values from -300 to 300
- weights: bfloat16 [2, 3072, 3072], P('section', 'mp'), may hold values from -0.109375 to 0.109375
- gain: float32 [2, 3072], P('section'), may hold values from 0.25 to 1.75
- top_grad: bfloat16 [24576, 3072], P('dp'), may hold values from -6 to 6
- counts: int32 [48], P('dp'), may hold values from 1 to 2, as said below
Outputs:
- weight_grad: bfloat16 [2, 3072, 3072], P('section', ('mp', 'dp'))
- residual_grad: bfloat16 [2, 24576, 3072], P('section', 'dp', 'mp')
Inputs may be any that keep to these rules, and one draw needn't show every extreme that they name: counts[r] counts the live micro-batches of replica r; some replica has all 2.
All inputs are finite; a program needn't handle non-finite values.
Results may differ from a plain program's by a relative error of at most 0.009.
Values may be sent and summed in bfloat16 or wider, within the bound.
No kernel may reach another device: no remote copies, remote signals or barrier semaphores. Data moves between devices by JAX's collectives and lax.ppermute only.
A program may use at most 64 MiB of HBM per device.

v0:
```python
import jax
import jax.numpy as jnp
from jax import lax
from jax.sharding import Mesh
from jax.sharding import PartitionSpec as P

TOK_MB = 256
DP = ("dp_0", "dp_1")
MP_DP = ("mp", "dp_0", "dp_1")


def summed_rows(subtotal, axes):
    for axis in axes:
        subtotal = lax.psum_scatter(subtotal, axis, scatter_dimension=0, tiled=True)
    return subtotal


def split_up(value, dim, peers):
    shape = value.shape
    tiles = value.reshape(*shape[:dim], peers, shape[dim] // peers, *shape[dim + 1 :])
    return jnp.moveaxis(tiles, dim, 0)


def sum_at_owner(value, axis, dim):
    tiles = split_up(value, dim, lax.axis_size(axis))
    arrived = lax.all_to_all(tiles, axis, split_axis=0, concat_axis=0, tiled=True)
    return arrived.astype(jnp.float32).sum(axis=0)


def from_everyone(value, axis):
    copies = jnp.broadcast_to(value, (lax.axis_size(axis), *value.shape))
    return lax.all_to_all(copies, axis, split_axis=0, concat_axis=0, tiled=True)


def over_copies(value, axis):
    return from_everyone(value, axis).sum(axis=0)


def together(arrays, axis):
    ends = [0]
    for a in arrays:
        ends.append(ends[-1] + a.size)
    subtotal = over_copies(jnp.concatenate([a.ravel() for a in arrays]), axis)
    return tuple((subtotal[b:e].reshape(a.shape) for a, b, e in zip(arrays, ends, ends[1:])))


def shifted(value, axis, by):
    peers = lax.axis_size(axis)
    pairs = [(i, i + by) for i in range(peers) if 0 <= i + by < peers]
    return lax.ppermute(value, axis, pairs)


def normalize(stream_rows):
    values = stream_rows.astype(jnp.float32)
    average = jnp.mean(values, axis=-1, keepdims=True)
    centred = values - average
    variance = jnp.mean(centred * centred, axis=-1, keepdims=True)
    inv_scale = lax.rsqrt(variance + 1e-06)
    return (centred * inv_scale, inv_scale)


def shards(value_grad, stream, weights, gain, top_grad, counts):
    section_index = lax.axis_index("section")
    model_index = lax.axis_index("mp")
    row_total = stream.shape[1]
    whitened, inv_scale = normalize(stream[0])
    gain_row = gain[0]
    normed = (whitened * gain_row).astype(jnp.bfloat16)
    micro_index = jnp.arange(row_total, dtype=jnp.int32) // TOK_MB
    live_mask = (micro_index < counts[0]).astype(jnp.bfloat16)
    masked = value_grad[0] * live_mask[:, None]
    grad_rows = summed_rows(
        lax.dot_general(
            masked, normed, (((0,), (0,)), ((), ())), preferred_element_type=jnp.float32
        ),
        DP,
    )
    weight_grad = grad_rows.astype(jnp.bfloat16)[None]
    partial_sum = jnp.dot(value_grad[0], weights[0], preferred_element_type=jnp.float32)
    width = whitened.shape[1]
    share_width = width // lax.axis_size("mp")
    first_col = model_index * share_width
    norm_grad = sum_at_owner(partial_sum.astype(jnp.bfloat16), "mp", 1)
    white_share = lax.dynamic_slice_in_dim(whitened, first_col, share_width, 1)
    gain_share = lax.dynamic_slice_in_dim(gain_row, first_col, share_width, 0)
    scaled_grad = norm_grad * gain_share
    first_total, second_total = together(
        (jnp.sum(scaled_grad, axis=1), jnp.sum(scaled_grad * white_share, axis=1)), "mp"
    )
    norm_back = inv_scale * (
        scaled_grad - first_total[:, None] / width - white_share * (second_total[:, None] / width)
    )
    top_slice = lax.dynamic_slice_in_dim(top_grad, first_col, share_width, 1).astype(jnp.float32)
    above_grad = (top_slice + norm_back).astype(jnp.bfloat16)
    below_grad = shifted(above_grad, "section", -1)
    lower_grad = (below_grad.astype(jnp.float32) + norm_back).astype(jnp.bfloat16)
    result = jnp.where(section_index == 0, lower_grad, above_grad)
    return (weight_grad, result[None])


def solution(mesh):
    split = Mesh(
        mesh.devices.reshape(mesh.shape["section"], mesh.shape["mp"], 12, 4),
        ("section", "mp", "dp_0", "dp_1"),
    )
    placed = (
        P("section", DP, "mp"),
        P("section", DP, None),
        P("section", "mp", None),
        P("section", None),
        P(DP, None),
        P(DP),
    )
    return jax.shard_map(
        shards,
        mesh=split,
        in_specs=placed,
        out_specs=(P("section", MP_DP, None), P("section", DP, "mp")),
        check_vma=False,
    )
```

profile of v0, /device:TPU:16, one launch (start us, length us, event | category | flops | bytes accessed | tf_op | source)
XLA Modules:
  0.0 138.1 jit_solution(5752302302063429229)
XLA Ops:
  7.2 0.0 copy-start
  7.2 0.0 reduce-scatter.3.cloned.1.call-start
  7.2 0.0 copy-start.1
  8.1 2.7 %convert_reduce_fusion = f32[512]{0:T(512)S(1)} fusion(bf16[1,512,3072]{2,1,0:T(8,128)(2,1)} %param.7), kind=kLoop, calls=%fused_computation.2 | loop fusion | flops 3145216 | bytes 3147776 | tf_op jit(solution)/shard_map/reduce_sum | solution.py:55
  10.7 0.0 copy-done.1
  10.7 0.0 copy-start.2
  10.7 0.0 copy-start.3
  10.8 3.5 %fusion.3 = (f32[512,3072]{1,0:T(8,128)}, f32[512]{0:T(512)S(1)}) fusion(bf16[1,512,3072]{2,1,0:T(8,128)(2,1)S(1)} %copy-done.1, f32[512]{0:T(512)S(1)} %broadcast_multiply_fusion), kind=kLoop, calls=%fused_computation.6 | loop fusion | flops 6290944 | bytes 9441280 | tf_op jit(solution)/shard_map/sub | solution.py:56
  14.3 0.0 copy-done.2
  14.3 0.0 copy-done.3
  14.3 3.9 %fusion.5 = f32[384,3072]{1,0:T(8,128)} fusion(bf16[1,512,3072]{2,1,0:T(8,128)(2,1)S(1)} %copy-done.1, f32[3072]{0:T(1024)S(1)} %bitcast.34, f32[512]{0:T(512)S(1)} %add_rsqrt_fusion, f32[512]{0:T(512)S(1)} %broadcast_multiply_fusion, bf16[1,512,384]{2,1,0:T(8,128)(2,1)S(1)} %copy-done.2, bf16[512]{0:T(512)(128)(2,1)S(1)} %fusion.21), kind=kOutput, calls=%fused_computation.11 | convolution fusion | flops 1216020480 | bytes 8274944 | tf_op jit(solution)/shard_map/dot_general | solution.py:73
  18.2 0.0 reduce-scatter.3.cloned.1.call-update
  18.2 0.0 copy-done
  18.3 1.8 %convolution_convert_fusion = bf16[512,3072]{1,0:T(8,128)(2,1)S(1)} fusion(bf16[1,384,3072]{2,1,0:T(8,128)(2,1)S(1)} %copy-done, bf16[1,512,384]{2,1,0:T(8,128)(2,1)S(1)} %copy-done.2), kind=kOutput, calls=%fused_computation.9 | convolution fusion | flops 1209532416 | bytes 5898240 | tf_op jit(solution)/shard_map/dot_general | solution.py:79
  20.1 2.0 %copy.17 = bf16[64,8,8,384]{3,2,0,1:T(8,128)(2,1)} copy(bf16[64,8,8,384]{3,2,1,0:T(8,128)(2,1)S(1)} %bitcast.33) | data formatting | bytes 6291456 | tf_op jit(solution)/shard_map/reshape | solution.py:20
  22.0 5.3 %all-to-all-start = ((bf16[8,512,384]{2,1,0:T(8,128)(2,1)}), bf16[8,512,384]{2,1,0:T(8,128)(2,1)}, u32[]{:S(2)}, u32[]{:S(2)}) async-start(bf16[8,512,384]{2,1,0:T(8,128)(2,1)} %bitcast.32), calls=%async_computation.2 | async-start | bytes 6291456 | tf_op jit(solution)/shard_map/all_to_all | solution.py:26
  27.4 0.0 reduce-scatter.5.cloned.1.call-start
  27.4 37.3 %all-to-all-done = bf16[8,512,384]{2,1,0:T(8,128)(2,1)} async-done(((bf16[8,512,384]{2,1,0:T(8,128)(2,1)}), bf16[8,512,384]{2,1,0:T(8,128)(2,1)}, u32[]{:S(2)}, u32[]{:S(2)}) %all-to-all-start) | async-done | bytes 3145760 | tf_op jit(solution)/shard_map/all_to_all | solution.py:26
  64.7 2.4 %convert_reduce_fusion.1 = f32[512,384]{1,0:T(8,128)S(1)} fusion(bf16[8,512,384]{2,1,0:T(8,128)(2,1)} %all-to-all-done), kind=kLoop, calls=%fused_computation.7 | loop fusion | flops 2949120 | bytes 3932160 | tf_op jit(solution)/shard_map/reduce_sum | solution.py:27
  67.2 1.5 %multiply_reduce_fusion.2 = (f32[512]{0:T(512)S(1)}, f32[512]{0:T(512)S(1)}) fusion(f32[512,384]{1,0:T(8,128)S(1)} %convert_reduce_fusion.1, f32[384]{0:T(512)S(1)} %dynamic-slice_reduce_fusion, f32[512]{0:T(512)S(1)} %add_rsqrt_fusion, f32[512,3072]{1,0:T(8,128)} %get-tuple-element.4, s32[]{:T(128)S(6)} %select_n.24), kind=kLoop, calls=%fused_computation.22 | loop fusion | flops 982016 | bytes 1580548 | tf_op jit(solution)/shard_map/reduce_sum | solution.py:88
  68.7 9.7 %all_to_all.11 = f32[8,1,1024]{2,1,0:T(1,128)S(1)} all-to-all(f32[8,1,1024]{2,1,0:T(1,128)S(1)} %broadcast_in_dim.7), channel_id=1, replica_groups=mesh['section'=2,'mp'=8,'dp_0'=12,'dp_1'=4] {'mp'}, dimensions={0} | all-to-all | bytes 65536 | tf_op jit(solution)/shard_map/all_to_all | solution.py:32
  78.4 18.1 %reduce-scatter.3.cloned.1.call-done = f32[32,3072]{1,0:T(8,128)} async-done(((f32[384,3072]{1,0:T(8,128)}), f32[32,3072]{1,0:T(8,128)}) %reduce-scatter.3.cloned.1.call-update) | async-done | bytes 393232 | tf_op jit(solution)/shard_map/reduce_scatter | solution.py:14
  96.5 0.0 reduce-scatter.5.cloned.1.call-update
  96.5 1.6 %add_convert_fusion.1 = bf16[512,384]{1,0:T(8,128)(2,1)S(1)} fusion(bf16[512,3072]{1,0:T(8,128)(2,1)} %param.10, s32[]{:T(128)S(6)} %select_n.24, f32[512]{0:T(512)S(1)} %get-tuple-element.7, f32[512,3072]{1,0:T(8,128)} %get-tuple-element.4, f32[512]{0:T(512)S(1)} %get-tuple-element.6, f32[512,384]{1,0:T(8,128)S(1)} %convert_reduce_fusion.1, ...), kind=kLoop, calls=%fused_computation.19 | loop fusion | flops 1769472 | bytes 2366980 | tf_op jit(solution)/shard_map/convert_element_type | solution.py:94
  98.1 1.3 collective-permute-start
  99.4 2.4 %collective-permute-done = bf16[512,384]{1,0:T(8,128)(2,1)} collective-permute-done((bf16[512,384]{1,0:T(8,128)(2,1)S(1)}, bf16[512,384]{1,0:T(8,128)(2,1)}, u32[]{:S(2)}, u32[]{:S(2)}) %collective-permute-start) | collective-permute-done | bytes 393248 | tf_op jit(solution)/shard_map/ppermute | solution.py:50
  101.9 2.3 %fusion.12 = bf16[1,512,384]{2,1,0:T(8,128)(2,1)} fusion(bf16[512,384]{1,0:T(8,128)(2,1)S(1)} %add_convert_fusion.1, bf16[512,384]{1,0:T(8,128)(2,1)} %collective-permute-done, pred[]{:T(512)S(6)} %eq.3, f32[512]{0:T(512)S(1)} %get-tuple-element.7, f32[512,3072]{1,0:T(8,128)} %get-tuple-element.4, s32[]{:T(128)S(6)} %select_n.24, ...), kind=kLoop, calls=%fused_computation.24 | loop fusion | flops 1966080 | bytes 2760197 | tf_op jit(solution)/shard_map/broadcast_in_dim | solution.py:98
  104.2 25.6 %reduce-scatter.5.cloned.1.call-done = f32[8,3072]{1,0:T(8,128)} async-done(((f32[32,3072]{1,0:T(8,128)}), f32[8,3072]{1,0:T(8,128)}) %reduce-scatter.5.cloned.1.call-update) | async-done | bytes 98320 | tf_op jit(solution)/shard_map/reduce_scatter | solution.py:14
  129.8 1.5 %convert_bitcast_fusion.1 = bf16[1,8,3072]{2,1,0:T(8,128)(2,1)} fusion(f32[8,3072]{1,0:T(8,128)} %reduce-scatter.5.cloned.1.call-done), kind=kLoop, calls=%fused_computation.29 | loop fusion | flops 24576 | bytes 147456 | tf_op jit(solution)/shard_map/broadcast_in_dim | solution.py:78
  (8 shorter events, 0.1 us)
Async XLA Ops:
  7.2 11.1 %copy-start = (bf16[1,384,3072]{2,1,0:T(8,128)(2,1)S(1)}, bf16[1,384,3072]{2,1,0:T(8,128)(2,1)}, u32[]{:S(2)}) copy-start(bf16[1,384,3072]{2,1,0:T(8,128)(2,1)} %param.8) | copy-start | bytes 7077892
  7.2 89.3 %reduce-scatter.3.cloned.1.call-start = ((), (), s32[]{:S(2)}) async-start(), calls=%async_computation.4 | async-start | bytes 5111808 | tf_op jit(solution)/shard_map/reduce_scatter | solution.py:14
  7.2 3.5 %copy-start.1 = (bf16[1,512,3072]{2,1,0:T(8,128)(2,1)S(1)}, bf16[1,512,3072]{2,1,0:T(8,128)(2,1)}, u32[]{:S(2)}) copy-start(bf16[1,512,3072]{2,1,0:T(8,128)(2,1)} %param.7) | copy-start | bytes 9437188
  10.7 3.6 %copy-start.2 = (bf16[1,512,384]{2,1,0:T(8,128)(2,1)S(1)}, bf16[1,512,384]{2,1,0:T(8,128)(2,1)}, u32[]{:S(2)}) copy-start(bf16[1,512,384]{2,1,0:T(8,128)(2,1)} %param.6) | copy-start | bytes 1179652
  10.7 3.6 %copy-start.3 = (f32[1,3072]{1,0:T(1,128)S(1)}, f32[1,3072]{1,0:T(1,128)}, u32[]{:S(2)}) copy-start(f32[1,3072]{1,0:T(1,128)} %param.9) | copy-start | bytes 36868
  22.0 42.7 %all-to-all-start = ((bf16[8,512,384]{2,1,0:T(8,128)(2,1)}), bf16[8,512,384]{2,1,0:T(8,128)(2,1)}, u32[]{:S(2)}, u32[]{:S(2)}) async-start(bf16[8,512,384]{2,1,0:T(8,128)(2,1)} %bitcast.32), calls=%async_computation.2 | async-start | bytes 6291456 | tf_op jit(solution)/shard_map/all_to_all | solution.py:26
  27.4 102.4 %reduce-scatter.5.cloned.1.call-start = ((), (), s32[]{:S(2)}) async-start(), calls=%async_computation.5 | async-start | bytes 491520 | tf_op jit(solution)/shard_map/reduce_scatter | solution.py:14
  98.1 3.7 %collective-permute-start = (bf16[512,384]{1,0:T(8,128)(2,1)S(1)}, bf16[512,384]{1,0:T(8,128)(2,1)}, u32[]{:S(2)}, u32[]{:S(2)}) collective-permute-start(bf16[512,384]{1,0:T(8,128)(2,1)S(1)} %add_convert_fusion.1), channel_id=1, source_target_pairs={{384,0},{385,1},{386,2},{387,3},{388,4},{389,5},{390,6},{391,7},{3... | collective-permute-start | bytes 1179656 | tf_op jit(solution)/shard_map/ppermute | solution.py:50
Sparse Core Ops, SparseCore 0:
  18.4 78.0 reduce-scatter.2
  99.6 30.1 reduce-scatter.4
where the time goes:
time: 139 us; the launch traced here: 138 us
  waiting for transfers between devices  83.4 us (60%)
  other arithmetic  15.6 us (11%)
  between operations  15 us (11%)
  blocking collectives  9.68 us (7%)
  starting transfers between devices  6.68 us (5%)
  matrix products  5.72 us (4%)
  local copies, waits for them, and re-layouts  2.05 us (1%)
    reduce_scatter x2, waiting for transfers between devices, summed_rows(): subtotal = lax.psum_scatter(subtotal, axis, scatter_dimension=0, tiled=True)  43.6 us
    all_to_all x1, waiting for transfers between devices, sum_at_owner(): lax.all_to_all(tiles, axis, split_axis=0, concat_axis=0, tiled=True)  37.3 us
    all_to_all x1, blocking collectives, from_everyone(): return lax.all_to_all(copies, axis, split_axis=0, concat_axis=0, tiled=True)  9.68 us
    all_to_all x1, starting transfers between devices, sum_at_owner(): lax.all_to_all(tiles, axis, split_axis=0, concat_axis=0, tiled=True)  5.32 us
    dot_general x1, matrix products, shards(): lax.dot_general(masked, normed, (((0,), (0,)), ((), ())), preferred_eleme...  3.92 us
    sub x1, other arithmetic, normalize(): centred = values - average  3.53 us
  transfers between devices with their start and end apart: 4, of which 4 were waited for; matrix products, arithmetic and copies ran while one was open for 8% of the time, Pallas kernels for 0%

commit v1 on v0

v1 whole, which is shorter than its diff:
```python
import jax
import jax.numpy as jnp
from jax import lax
from jax.sharding import Mesh
from jax.sharding import PartitionSpec as P

TOK_MB = 256
DP = ("dz", "dy")
MP = ("my", "mx")
F32 = jnp.float32
BF16 = jnp.bfloat16


def turned(value, axis, by):
    peers = lax.axis_size(axis)
    return lax.ppermute(value, axis, [(i, (i + by) % peers) for i in range(peers)])


def normalize(stream_rows):
    values = stream_rows.astype(F32)
    average = jnp.mean(values, axis=-1, keepdims=True)
    centred = values - average
    variance = jnp.mean(centred * centred, axis=-1, keepdims=True)
    inv_scale = lax.rsqrt(variance + 1e-06)
    return (centred * inv_scale, inv_scale)


def joined(own, got):
    return own.astype(F32) + got.astype(F32)


def sum_over_z(grad):
    peers = lax.axis_size("dz")
    place = lax.axis_index("dz")
    rows = grad.shape[0] // peers
    half = grad.shape[1] // 2
    far = peers // 2

    def block(offset):
        return lax.dynamic_slice_in_dim(grad, ((place + offset) % peers) * rows, rows, 0)

    up = turned(block(far)[:, :half].astype(BF16), "dz", 1)
    down = turned(block(-far)[:, half:].astype(BF16), "dz", -1)
    for k in range(far - 1, 0, -1):
        mine_up = block(k)
        mine_down = block(-k)
        if k == far - 1:
            mine_up = jnp.concatenate([joined(mine_up[:, :half], up), mine_up[:, half:]], axis=1)
            mine_down = jnp.concatenate([mine_down[:, :half], joined(mine_down[:, half:], down)], axis=1)
        else:
            mine_up = joined(mine_up, up)
            mine_down = joined(mine_down, down)
        up = turned(mine_up.astype(BF16), "dz", 1)
        down = turned(mine_down.astype(BF16), "dz", -1)
    return block(0) + up.astype(F32) + down.astype(F32)


def sum_over_y(rows_sum):
    peers = lax.axis_size("dy")
    place = lax.axis_index("dy")
    rows = rows_sum.shape[0] // peers

    def block(offset):
        return lax.dynamic_slice_in_dim(rows_sum, ((place + offset) % peers) * rows, rows, 0)

    got = [turned(block(k).astype(BF16), "dy", k) for k in range(1, peers)]
    total = block(0)
    for g in got:
        total = total + g.astype(F32)
    return total


def sum_at_owner(partial, width):
    x = lax.axis_index("mx")
    y = lax.axis_index("my")

    def part(rx, ry):
        start = (((y + ry) % 2) * 4 + (x + rx) % 4) * width
        return lax.dynamic_slice_in_dim(partial, start, width, 1)

    far_up = turned(part(2, 1), "mx", 1)
    far_down = turned(part(2, 0), "mx", -1)
    near_up = turned(part(1, 0), "mx", 1)
    near_down = turned(part(3, 1), "mx", -1)
    sum_up = turned(joined(part(1, 1), far_up).astype(BF16), "mx", 1)
    sum_down = turned(joined(part(3, 0), far_down).astype(BF16), "mx", -1)
    other = part(0, 1).astype(F32) + near_down.astype(F32) + sum_up.astype(F32)
    across = turned(other.astype(BF16), "my", 1)
    return part(0, 0).astype(F32) + near_up.astype(F32) + sum_down.astype(F32) + across.astype(F32)


def sum_over_mp(value):
    got = [turned(value, "mx", k) for k in range(1, 4)]
    value = value + got[0] + got[1] + got[2]
    return value + turned(value, "my", 1)


def shards(value_grad, stream, weights, gain, top_grad, counts):
    section_index = lax.axis_index("section")
    model_index = lax.axis_index(MP)
    row_total = stream.shape[1]
    width = stream.shape[2]
    share_width = width // lax.axis_size(MP)
    first_col = model_index * share_width
    partial = jnp.dot(value_grad[0], weights[0], preferred_element_type=F32).astype(BF16)
    norm_grad = sum_at_owner(partial, share_width)
    whitened, inv_scale = normalize(stream[0])
    gain_row = gain[0]
    normed = (whitened * gain_row).astype(BF16)
    micro_index = jnp.arange(row_total, dtype=jnp.int32) // TOK_MB
    live_mask = (micro_index < counts[0]).astype(BF16)
    masked = value_grad[0] * live_mask[:, None]
    grad = lax.dot_general(masked, normed, (((0,), (0,)), ((), ())), preferred_element_type=F32)
    weight_grad = sum_over_y(sum_over_z(grad)).astype(BF16)[None]
    scaled_part = partial.astype(F32) * gain_row
    totals = sum_over_mp(jnp.stack([jnp.sum(scaled_part, axis=1), jnp.sum(scaled_part * whitened, axis=1)]))
    white_share = lax.dynamic_slice_in_dim(whitened, first_col, share_width, 1)
    gain_share = lax.dynamic_slice_in_dim(gain_row, first_col, share_width, 0)
    scaled_grad = norm_grad * gain_share
    norm_back = inv_scale * (
        scaled_grad - totals[0][:, None] / width - white_share * (totals[1][:, None] / width)
    )
    top_slice = lax.dynamic_slice_in_dim(top_grad, first_col, share_width, 1).astype(F32)
    above_grad = (top_slice + norm_back).astype(BF16)
    below_grad = lax.ppermute(above_grad, "section", [(1, 0)])
    lower_grad = (below_grad.astype(F32) + norm_back).astype(BF16)
    result = jnp.where(section_index == 0, lower_grad, above_grad)
    return (weight_grad, result[None])


def solution(mesh):
    split = Mesh(
        mesh.devices.reshape(mesh.shape["section"], 2, 4, 12, 4),
        ("section", "my", "mx", "dz", "dy"),
    )
    placed = (
        P("section", DP, MP),
        P("section", DP, None),
        P("section", MP, None),
        P("section", None),
        P(DP, None),
        P(DP),
    )
    return jax.shard_map(
        shards,
        mesh=split,
        in_specs=placed,
        out_specs=(P("section", MP + DP, None), P("section", DP, MP)),
        check_vma=False,
    )
```

time: 139 us -> 158 us (1.14)
  starting transfers between devices: 6.68 us -> 97.9 us
  waiting for transfers between devices: 83.4 us -> 22.8 us
  between operations: 15 us -> 2.31 us
  blocking collectives: 9.68 us -> 0 us
  other arithmetic: 15.6 us -> 21 us
  matrix products: 5.72 us -> 9 us
    ppermute x1 -> x27, starting transfers between devices: 1.29 us -> 97.9 us  [the longest x26 96.6 us: turned(): lax.ppermute(value, axis, [(i, (i + by) % peers) for i in range(peers)])]
    reduce_scatter x2 -> x0, waiting for transfers between devices: 43.6 us -> none  [summed_rows(): subtotal = lax.psum_scatter(subtotal, axis, scatter_dimension=0, tiled=True)]
    all_to_all x1 -> x0, waiting for transfers between devices: 37.3 us -> none  [sum_at_owner(): lax.all_to_all(tiles, axis, split_axis=0, concat_axis=0, tiled=True)]
    ppermute x1 -> x27, waiting for transfers between devices: 2.44 us -> 22.8 us  [the longest x26 22.8 us: turned(): lax.ppermute(value, axis, [(i, (i + by) % peers) for i in range(peers)])]
    convert_element_type x2 -> x11, other arithmetic: 1.6 us -> 12.9 us  [the longest x4 5.24 us: sum_over_z(): up = turned(mine_up.astype(BF16), 'dz', 1)]
    all_to_all x1 -> x0, blocking collectives: 9.68 us -> none  [from_everyone(): return lax.all_to_all(copies, axis, split_axis=0, concat_axis=0, tiled=True)]
    all_to_all x1 -> x0, starting transfers between devices: 5.32 us -> none  [sum_at_owner(): lax.all_to_all(tiles, axis, split_axis=0, concat_axis=0, tiled=True)]
    dot_general x1, matrix products: 1.8 us -> 5.33 us  [shards(): jnp.dot(value_grad[0], weights[0], preferred_element_type=F32).astype(BF16)]
  transfers between devices with their start and end apart: 4 -> 27, of which waited for: 4 -> 10; matrix products, arithmetic and copies ran while one was open for 8% -> 15% of each run, Pallas kernels for 0% -> 0%
where the time goes in v1:
time: 158 us; the launch traced here: 156 us
  starting transfers between devices  97.9 us (62%)
  waiting for transfers between devices  22.8 us (14%)
  other arithmetic  21 us (13%)
  matrix products  9 us (6%)
  local copies, waits for them, and re-layouts  3 us (2%)
  between operations  2.31 us (1%)
    ppermute x26, starting transfers between devices, turned(): lax.ppermute(value, axis, [(i, (i + by) % peers) for i in range(peers)])  96.6 us
    ppermute x26, waiting for transfers between devices, turned(): lax.ppermute(value, axis, [(i, (i + by) % peers) for i in range(peers)])  22.8 us
    dot_general x1, matrix products, shards(): jnp.dot(value_grad[0], weights[0], preferred_element_type=F32).astype(BF16)  5.33 us
    convert_element_type x4, other arithmetic, sum_over_z(): up = turned(mine_up.astype(BF16), 'dz', 1)  5.24 us
    dot_general x1, matrix products, shards(): lax.dot_general(masked, normed, (((0,), (0,)), ((), ())), preferred_eleme...  3.67 us
  transfers between devices with their start and end apart: 27, of which 10 were waited for; matrix products, arithmetic and copies ran while one was open for 15% of the time, Pallas kernels for 0%

profile of v1, /device:TPU:16, one launch (start us, length us, event | category | flops | bytes accessed | tf_op | source)
XLA Modules:
  0.0 156.0 jit_solution(5318891947689037465)
XLA Ops:
  0.8 2.5 %convert_reduce_fusion = f32[512]{0:T(512)S(1)} fusion(bf16[1,512,3072]{2,1,0:T(8,128)(2,1)} %param.7), kind=kLoop, calls=%fused_computation.2 | loop fusion | flops 3145216 | bytes 3147776 | tf_op jit(solution)/shard_map/reduce_sum | solution.py:21
  5.4 3.7 %fusion.9 = f32[384,3072]{1,0:T(8,128)S(1)} fusion(bf16[1,512,3072]{2,1,0:T(8,128)(2,1)} %param.7, f32[3072]{0:T(1024)S(1)} %bitcast.39, f32[512]{0:T(512)S(1)} %add_rsqrt_fusion, f32[512]{0:T(512)S(1)} %broadcast_multiply_fusion, bf16[1,512,384]{2,1,0:T(8,128)(2,1)S(1)} %copy-done.4, bf16[512]{0:T(512)(128)(2,1)S(1)} %fusion.28), kind=kOutput, calls=%fused_computation.15 | convolution fusion | flops 1216020480 | bytes 8274944 | tf_op jit(solution)/shard_map/dot_general | solution.py:113
  9.2 4.3 %collective-permute-start = (bf16[32,1536]{1,0:T(8,128)(2,1)S(1)}, bf16[32,1536]{1,0:T(8,128)(2,1)S(1)}, u32[]{:S(2)}, u32[]{:S(2)}) collective-permute-start(bf16[32,1536]{1,0:T(8,128)(2,1)S(1)} %get-tuple-element.10), channel_id=1, source_target_pairs={{0,4},{4,8},{8,12},{12,16},{16,20},{20,24},{24,28},{28,32},{32,36}... | collective-permute-start | bytes 294920 | tf_op jit(solution)/shard_map/ppermute | solution.py:16
  13.5 12.2 %collective-permute-start.6 = (bf16[32,1536]{1,0:T(8,128)(2,1)S(1)}, bf16[32,1536]{1,0:T(8,128)(2,1)S(1)}, u32[]{:S(2)}, u32[]{:S(2)}) collective-permute-start(bf16[32,1536]{1,0:T(8,128)(2,1)S(1)} %get-tuple-element.11), channel_id=1, source_target_pairs={{0,44},{4,0},{8,4},{12,8},{16,12},{20,16},{24,20},{28,24},{32,28},... | collective-permute-start | bytes 294920 | tf_op jit(solution)/shard_map/ppermute | solution.py:16
  26.5 1.3 collective-permute-done.6
  28.0 1.9 %collective-permute-start.1 = (bf16[32,3072]{1,0:T(8,128)(2,1)S(1)}, bf16[32,3072]{1,0:T(8,128)(2,1)S(1)}, u32[]{:S(2)}, u32[]{:S(2)}) collective-permute-start(bf16[32,3072]{1,0:T(8,128)(2,1)S(1)} %pad_maximum_fusion), channel_id=1, source_target_pairs={{0,4},{4,8},{8,12},{12,16},{16,20},{20,24},{24,28},{28,32},{32,36}... | collective-permute-start | bytes 589832 | tf_op jit(solution)/shard_map/ppermute | solution.py:16
  29.9 5.3 %fusion.7 = (f32[512]{0:T(512)}, f32[512]{0:T(512)}, f32[512,3072]{1,0:T(8,128)}, bf16[512,3072]{1,0:T(8,128)(2,1)}) fusion(f32[3072]{0:T(1024)S(1)} %bitcast.40, f32[512]{0:T(512)S(1)} %add_rsqrt_fusion, f32[512]{0:T(512)S(1)} %broadcast_multiply_fusion, bf16[1,512,3072]{2,1,0:T(8,128)(2,1)S(1)} %copy-done.2, bf16[1,384,3072]{2,1,0:T(8,128)(2,1)S(1)} %copy-done, ...), kind=kOutput, calls=%fused_computation.12 | convolution fusion | flops 1222114304 | bytes 15355904 | tf_op jit(solution)/shard_map/dot_general | solution.py:105
  35.2 2.0 %collective-permute-done.1 = bf16[32,3072]{1,0:T(8,128)(2,1)S(1)} collective-permute-done((bf16[32,3072]{1,0:T(8,128)(2,1)S(1)}, bf16[32,3072]{1,0:T(8,128)(2,1)S(1)}, u32[]{:S(2)}, u32[]{:S(2)}) %collective-permute-start.1) | collective-permute-done | bytes 196640 | tf_op jit(solution)/shard_map/ppermute | solution.py:16
  38.3 1.9 %collective-permute-start.2 = (bf16[32,3072]{1,0:T(8,128)(2,1)S(1)}, bf16[32,3072]{1,0:T(8,128)(2,1)}, u32[]{:S(2)}, u32[]{:S(2)}) collective-permute-start(bf16[32,3072]{1,0:T(8,128)(2,1)S(1)} %add_convert_fusion.12), channel_id=1, source_target_pairs={{0,4},{4,8},{8,12},{12,16},{16,20},{20,24},{24,28},{28,32},{32,36}... | collective-permute-start | bytes 589832 | tf_op jit(solution)/shard_map/ppermute | solution.py:16
  40.2 1.2 pad_maximum_fusion.2
  41.4 3.4 %collective-permute-start.22 = (f32[2,512]{1,0:T(2,128)}, f32[2,512]{1,0:T(2,128)}, u32[]{:S(2)}, u32[]{:S(2)}) collective-permute-start(f32[2,512]{1,0:T(2,128)} %pad_maximum_fusion.2), channel_id=1, source_target_pairs={{0,48},{48,96},{96,144},{144,0},{1,49},{49,97},{97,145},{145,1},{2... | collective-permute-start | bytes 12296 | tf_op jit(solution)/shard_map/ppermute | solution.py:16
  44.8 4.6 %collective-permute-start.23 = (f32[2,512]{1,0:T(2,128)}, f32[2,512]{1,0:T(2,128)}, u32[]{:S(2)}, u32[]{:S(2)}) collective-permute-start(f32[2,512]{1,0:T(2,128)} %pad_maximum_fusion.2), channel_id=1, source_target_pairs={{0,96},{48,144},{96,0},{144,48},{1,97},{49,145},{97,1},{145,49},{2... | collective-permute-start | bytes 12296 | tf_op jit(solution)/shard_map/ppermute | solution.py:16
  49.5 3.3 %collective-permute-start.24 = (f32[2,512]{1,0:T(2,128)}, f32[2,512]{1,0:T(2,128)}, u32[]{:S(2)}, u32[]{:S(2)}) collective-permute-start(f32[2,512]{1,0:T(2,128)} %pad_maximum_fusion.2), channel_id=1, source_target_pairs={{0,144},{48,0},{96,48},{144,96},{1,145},{49,1},{97,49},{145,97},{2... | collective-permute-start | bytes 12296 | tf_op jit(solution)/shard_map/ppermute | solution.py:16
  52.9 2.4 %constant_dynamic-slice_fusion.4 = (bf16[512,384]{1,0:T(8,128)(2,1)S(1)}, bf16[512,384]{1,0:T(8,128)(2,1)}, bf16[512,384]{1,0:T(8,128)(2,1)S(1)}, bf16[512,384]{1,0:T(8,128)(2,1)}) fusion(bf16[512,3072]{1,0:T(8,128)(2,1)} %get-tuple-element.26, s32[]{:T(128)S(6)} %select_n.253, s32[]{:T(128)S(6)} %select_n.262, s32[]{:T(128)S(6)} %select_n.260, s32[]{:T(128)S(6)} %select_n.257), kind=kLoop, calls=%fused_computation.60 | loop fusion | bytes 3145744 | tf_op jit(solution)/shard_map/dynamic_slice | solution.py:79
  55.3 1.9 %collective-permute-start.16 = (bf16[512,384]{1,0:T(8,128)(2,1)}, bf16[512,384]{1,0:T(8,128)(2,1)}, u32[]{:S(2)}, u32[]{:S(2)}) collective-permute-start(bf16[512,384]{1,0:T(8,128)(2,1)} %get-tuple-element.18), channel_id=1, source_target_pairs={{0,144},{48,0},{96,48},{144,96},{1,145},{49,1},{97,49},{145,97},{2... | collective-permute-start | bytes 1179656 | tf_op jit(solution)/shard_map/ppermute | solution.py:16
  57.4 1.1 add_convert_fusion.11
  58.6 1.9 %collective-permute-start.3 = (bf16[32,3072]{1,0:T(8,128)(2,1)S(1)}, bf16[32,3072]{1,0:T(8,128)(2,1)S(1)}, u32[]{:S(2)}, u32[]{:S(2)}) collective-permute-start(bf16[32,3072]{1,0:T(8,128)(2,1)S(1)} %add_convert_fusion.11), channel_id=1, source_target_pairs={{0,4},{4,8},{8,12},{12,16},{16,20},{20,24},{24,28},{28,32},{32,36}... | collective-permute-start | bytes 589832 | tf_op jit(solution)/shard_map/ppermute | solution.py:16
  60.5 6.8 %collective-permute-done.3 = bf16[32,3072]{1,0:T(8,128)(2,1)S(1)} collective-permute-done((bf16[32,3072]{1,0:T(8,128)(2,1)S(1)}, bf16[32,3072]{1,0:T(8,128)(2,1)S(1)}, u32[]{:S(2)}, u32[]{:S(2)}) %collective-permute-start.3) | collective-permute-done | bytes 196640 | tf_op jit(solution)/shard_map/ppermute | solution.py:16
  67.4 3.9 %collective-permute-start.19 = (bf16[512,384]{1,0:T(8,128)(2,1)}, bf16[512,384]{1,0:T(8,128)(2,1)}, u32[]{:S(2)}, u32[]{:S(2)}) collective-permute-start(bf16[512,384]{1,0:T(8,128)(2,1)} %get-tuple-element.16), channel_id=1, source_target_pairs={{0,48},{48,96},{96,144},{144,0},{1,49},{49,97},{97,145},{145,1},{2... | collective-permute-start | bytes 1179656 | tf_op jit(solution)/shard_map/ppermute | solution.py:16
  71.3 1.7 %add_convert_fusion.10 = bf16[32,3072]{1,0:T(8,128)(2,1)} fusion(bf16[32,3072]{1,0:T(8,128)(2,1)S(1)} %collective-permute-done.3, f32[384,3072]{1,0:T(8,128)} %copy-done.3, s32[]{:T(128)S(6)} %select_n.218), kind=kLoop, calls=%fused_computation.36 | loop fusion | flops 294912 | bytes 786436 | tf_op jit(solution)/shard_map/convert_element_type | solution.py:53
  73.0 3.9 %collective-permute-start.7 = (bf16[32,3072]{1,0:T(8,128)(2,1)S(1)}, bf16[32,3072]{1,0:T(8,128)(2,1)}, u32[]{:S(2)}, u32[]{:S(2)}) collective-permute-start(bf16[32,3072]{1,0:T(8,128)(2,1)S(1)} %pad_maximum_fusion.1), channel_id=1, source_target_pairs={{0,44},{4,0},{8,4},{12,8},{16,12},{20,16},{24,20},{28,24},{32,28},... | collective-permute-start | bytes 589832 | tf_op jit(solution)/shard_map/ppermute | solution.py:16
  76.9 1.9 %collective-permute-start.4 = (bf16[32,3072]{1,0:T(8,128)(2,1)}, bf16[32,3072]{1,0:T(8,128)(2,1)}, u32[]{:S(2)}, u32[]{:S(2)}) collective-permute-start(bf16[32,3072]{1,0:T(8,128)(2,1)} %add_convert_fusion.10), channel_id=1, source_target_pairs={{0,4},{4,8},{8,12},{12,16},{16,20},{20,24},{24,28},{28,32},{32,36}... | collective-permute-start | bytes 589832 | tf_op jit(solution)/shard_map/ppermute | solution.py:16
  79.6 3.5 %collective-permute-start.25 = (f32[2,512]{1,0:T(2,128)S(1)}, f32[2,512]{1,0:T(2,128)S(1)}, u32[]{:S(2)}, u32[]{:S(2)}) collective-permute-start(f32[2,512]{1,0:T(2,128)S(1)} %add_add_fusion), channel_id=1, source_target_pairs={{0,192},{192,0},{1,193},{193,1},{2,194},{194,2},{3,195},{195,3},{4... | collective-permute-start | bytes 12296 | tf_op jit(solution)/shard_map/ppermute | solution.py:16
  83.2 1.9 %collective-permute-done.25 = f32[2,512]{1,0:T(2,128)S(1)} collective-permute-done((f32[2,512]{1,0:T(2,128)S(1)}, f32[2,512]{1,0:T(2,128)S(1)}, u32[]{:S(2)}, u32[]{:S(2)}) %collective-permute-start.25) | collective-permute-done | bytes 4128 | tf_op jit(solution)/shard_map/ppermute | solution.py:16
  85.1 3.1 %collective-permute-start.18 = (bf16[512,384]{1,0:T(8,128)(2,1)S(1)}, bf16[512,384]{1,0:T(8,128)(2,1)S(1)}, u32[]{:S(2)}, u32[]{:S(2)}) collective-permute-start(bf16[512,384]{1,0:T(8,128)(2,1)S(1)} %get-tuple-element.17), channel_id=1, source_target_pairs={{0,144},{48,0},{96,48},{144,96},{1,145},{49,1},{97,49},{145,97},{2... | collective-permute-start | bytes 1179656 | tf_op jit(solution)/shard_map/ppermute | solution.py:16
  88.2 2.7 %collective-permute-start.15 = (bf16[512,384]{1,0:T(8,128)(2,1)S(1)}, bf16[512,384]{1,0:T(8,128)(2,1)S(1)}, u32[]{:S(2)}, u32[]{:S(2)}) collective-permute-start(bf16[512,384]{1,0:T(8,128)(2,1)S(1)} %get-tuple-element.15), channel_id=1, source_target_pairs={{0,48},{48,96},{96,144},{144,0},{1,49},{49,97},{97,145},{145,1},{2... | collective-permute-start | bytes 1179656 | tf_op jit(solution)/shard_map/ppermute | solution.py:16
  91.0 1.3 add_convert_fusion.9
  92.3 5.1 %collective-permute-start.8 = (bf16[32,3072]{1,0:T(8,128)(2,1)S(1)}, bf16[32,3072]{1,0:T(8,128)(2,1)S(1)}, u32[]{:S(2)}, u32[]{:S(2)}) collective-permute-start(bf16[32,3072]{1,0:T(8,128)(2,1)S(1)} %get-tuple-element.7), channel_id=1, source_target_pairs={{0,44},{4,0},{8,4},{12,8},{16,12},{20,16},{24,20},{28,24},{32,28},... | collective-permute-start | bytes 589832 | tf_op jit(solution)/shard_map/ppermute | solution.py:16
  97.5 3.8 %collective-permute-done.8 = bf16[32,3072]{1,0:T(8,128)(2,1)S(1)} collective-permute-done((bf16[32,3072]{1,0:T(8,128)(2,1)S(1)}, bf16[32,3072]{1,0:T(8,128)(2,1)S(1)}, u32[]{:S(2)}, u32[]{:S(2)}) %collective-permute-start.8) | collective-permute-done | bytes 196640 | tf_op jit(solution)/shard_map/ppermute | solution.py:16
  102.3 5.6 %collective-permute-start.9 = (bf16[32,3072]{1,0:T(8,128)(2,1)S(1)}, bf16[32,3072]{1,0:T(8,128)(2,1)S(1)}, u32[]{:S(2)}, u32[]{:S(2)}) collective-permute-start(bf16[32,3072]{1,0:T(8,128)(2,1)S(1)} %add_convert_fusion.7), channel_id=1, source_target_pairs={{0,44},{4,0},{8,4},{12,8},{16,12},{20,16},{24,20},{28,24},{32,28},... | collective-permute-start | bytes 589832 | tf_op jit(solution)/shard_map/ppermute | solution.py:16
  107.9 1.6 %add_convert_fusion.4 = (bf16[512,384]{1,0:T(8,128)(2,1)S(1)}, bf16[512,384]{1,0:T(8,128)(2,1)S(1)}) fusion(bf16[512,384]{1,0:T(8,128)(2,1)} %collective-permute-done.16, bf16[512,3072]{1,0:T(8,128)(2,1)} %get-tuple-element.26, s32[]{:T(128)S(6)} %select_n.255, bf16[512,384]{1,0:T(8,128)(2,1)} %collective-permute-done.19, s32[]{:T(128)S(6)} %select_n.261), kind=kLoop, calls=%fused_computation.25 | loop fusion | flops 1572864 | bytes 2359304 | tf_op jit(solution)/shard_map/convert_element_type | solution.py:86
  109.5 2.5 %collective-permute-start.20 = (bf16[512,384]{1,0:T(8,128)(2,1)S(1)}, bf16[512,384]{1,0:T(8,128)(2,1)S(1)}, u32[]{:S(2)}, u32[]{:S(2)}) collective-permute-start(bf16[512,384]{1,0:T(8,128)(2,1)S(1)} %get-tuple-element.20), channel_id=1, source_target_pairs={{0,48},{48,96},{96,144},{144,0},{1,49},{49,97},{97,145},{145,1},{2... | collective-permute-start | bytes 1179656 | tf_op jit(solution)/shard_map/ppermute | solution.py:16
  112.0 4.6 %collective-permute-start.17 = (bf16[512,384]{1,0:T(8,128)(2,1)S(1)}, bf16[512,384]{1,0:T(8,128)(2,1)S(1)}, u32[]{:S(2)}, u32[]{:S(2)}) collective-permute-start(bf16[512,384]{1,0:T(8,128)(2,1)S(1)} %get-tuple-element.19), channel_id=1, source_target_pairs={{0,144},{48,0},{96,48},{144,96},{1,145},{49,1},{97,49},{145,97},{2... | collective-permute-start | bytes 1179656 | tf_op jit(solution)/shard_map/ppermute | solution.py:16
  116.5 1.0 add_convert_fusion.6
  117.6 1.9 %collective-permute-start.10 = (bf16[32,3072]{1,0:T(8,128)(2,1)S(1)}, bf16[32,3072]{1,0:T(8,128)(2,1)S(1)}, u32[]{:S(2)}, u32[]{:S(2)}) collective-permute-start(bf16[32,3072]{1,0:T(8,128)(2,1)S(1)} %add_convert_fusion.6), channel_id=1, source_target_pairs={{0,44},{4,0},{8,4},{12,8},{16,12},{20,16},{24,20},{28,24},{32,28},... | collective-permute-start | bytes 589832 | tf_op jit(solution)/shard_map/ppermute | solution.py:16
  120.3 1.1 add_convert_fusion.2
  121.5 3.5 %collective-permute-start.21 = (bf16[512,384]{1,0:T(8,128)(2,1)S(1)}, bf16[512,384]{1,0:T(8,128)(2,1)S(1)}, u32[]{:S(2)}, u32[]{:S(2)}) collective-permute-start(bf16[512,384]{1,0:T(8,128)(2,1)S(1)} %add_convert_fusion.2), channel_id=1, source_target_pairs={{0,192},{192,0},{1,193},{193,1},{2,194},{194,2},{3,195},{195,3},{4... | collective-permute-start | bytes 1179656 | tf_op jit(solution)/shard_map/ppermute | solution.py:16
  125.0 3.1 %collective-permute-start.5 = (bf16[32,3072]{1,0:T(8,128)(2,1)S(1)}, bf16[32,3072]{1,0:T(8,128)(2,1)S(1)}, u32[]{:S(2)}, u32[]{:S(2)}) collective-permute-start(bf16[32,3072]{1,0:T(8,128)(2,1)S(1)} %get-tuple-element.6), channel_id=1, source_target_pairs={{0,4},{4,8},{8,12},{12,16},{16,20},{20,24},{24,28},{28,32},{32,36}... | collective-permute-start | bytes 589832 | tf_op jit(solution)/shard_map/ppermute | solution.py:16
  128.1 1.0 add_convert_fusion.5
  129.2 3.9 %collective-permute-start.11 = (bf16[32,3072]{1,0:T(8,128)(2,1)S(1)}, bf16[32,3072]{1,0:T(8,128)(2,1)S(1)}, u32[]{:S(2)}, u32[]{:S(2)}) collective-permute-start(bf16[32,3072]{1,0:T(8,128)(2,1)S(1)} %add_convert_fusion.5), channel_id=1, source_target_pairs={{0,44},{4,0},{8,4},{12,8},{16,12},{20,16},{24,20},{28,24},{32,28},... | collective-permute-start | bytes 589832 | tf_op jit(solution)/shard_map/ppermute | solution.py:16
  133.1 1.8 %add_convert_fusion.1 = (bf16[512,384]{1,0:T(8,128)(2,1)S(1)}, f32[512,384]{1,0:T(8,128)S(1)}) fusion(bf16[512,3072]{1,0:T(8,128)(2,1)} %param.10, s32[]{:T(128)S(6)} %select_n.248, f32[512]{0:T(512)S(1)} %bitcast.42, f32[512,3072]{1,0:T(8,128)} %get-tuple-element.14, f32[512]{0:T(512)S(1)} %bitcast.41, f32[384]{0:T(512)S(1)} %fusion.29, ...), kind=kLoop, calls=%fused_computation.21 | loop fusion | flops 2949120 | bytes 3939848 | tf_op jit(solution)/shard_map/convert_element_type | solution.py:124
  134.9 1.3 collective-permute-start.26
  136.7 1.1 convert_add_fusion
  137.8 4.8 %collective-permute-start.12 = (bf16[8,3072]{1,0:T(8,128)(2,1)S(1)}, bf16[8,3072]{1,0:T(8,128)(2,1)S(1)}, u32[]{:S(2)}, u32[]{:S(2)}) collective-permute-start(bf16[8,3072]{1,0:T(8,128)(2,1)S(1)} %get-tuple-element.21), channel_id=1, source_target_pairs={{0,1},{1,2},{2,3},{3,0},{4,5},{5,6},{6,7},{7,4},{8,9},{9,10},{10,1... | collective-permute-start | bytes 147464 | tf_op jit(solution)/shard_map/ppermute | solution.py:16
  142.6 2.9 %collective-permute-start.13 = (bf16[8,3072]{1,0:T(8,128)(2,1)S(1)}, bf16[8,3072]{1,0:T(8,128)(2,1)S(1)}, u32[]{:S(2)}, u32[]{:S(2)}) collective-permute-start(bf16[8,3072]{1,0:T(8,128)(2,1)S(1)} %get-tuple-element.23), channel_id=1, source_target_pairs={{0,2},{1,3},{2,0},{3,1},{4,6},{5,7},{6,4},{7,5},{8,10},{9,11},{10,... | collective-permute-start | bytes 147464 | tf_op jit(solution)/shard_map/ppermute | solution.py:16
  145.6 4.1 %collective-permute-start.14 = (bf16[8,3072]{1,0:T(8,128)(2,1)S(1)}, bf16[8,3072]{1,0:T(8,128)(2,1)S(1)}, u32[]{:S(2)}, u32[]{:S(2)}) collective-permute-start(bf16[8,3072]{1,0:T(8,128)(2,1)S(1)} %get-tuple-element.22), channel_id=1, source_target_pairs={{0,3},{1,0},{2,1},{3,2},{4,7},{5,4},{6,5},{7,6},{8,11},{9,8},{10,9... | collective-permute-start | bytes 147464 | tf_op jit(solution)/shard_map/ppermute | solution.py:16
  150.5 2.5 %collective-permute-done.13 = bf16[8,3072]{1,0:T(8,128)(2,1)S(1)} collective-permute-done((bf16[8,3072]{1,0:T(8,128)(2,1)S(1)}, bf16[8,3072]{1,0:T(8,128)(2,1)S(1)}, u32[]{:S(2)}, u32[]{:S(2)}) %collective-permute-start.13) | collective-permute-done | bytes 49184 | tf_op jit(solution)/shard_map/ppermute | solution.py:16
  153.0 2.3 %collective-permute-done.14 = bf16[8,3072]{1,0:T(8,128)(2,1)S(1)} collective-permute-done((bf16[8,3072]{1,0:T(8,128)(2,1)S(1)}, bf16[8,3072]{1,0:T(8,128)(2,1)S(1)}, u32[]{:S(2)}, u32[]{:S(2)}) %collective-permute-start.14) | collective-permute-done | bytes 49184 | tf_op jit(solution)/shard_map/ppermute | solution.py:16
  (49 shorter events, 8.1 us)
Async XLA Ops:
  0.6 29.3 %copy-start = (bf16[1,384,3072]{2,1,0:T(8,128)(2,1)S(1)}, bf16[1,384,3072]{2,1,0:T(8,128)(2,1)}, u32[]{:S(2)}) copy-start(bf16[1,384,3072]{2,1,0:T(8,128)(2,1)} %param.8) | copy-start | bytes 7077892
  0.6 4.7 %copy-start.5 = (f32[1,3072]{1,0:T(1,128)S(1)}, f32[1,3072]{1,0:T(1,128)}, u32[]{:S(2)}) copy-start(f32[1,3072]{1,0:T(1,128)} %param.9) | copy-start | bytes 36868
  0.7 3.0 %copy-start.1 = (bf16[1,512,3072]{2,1,0:T(8,128)(2,1)S(1)}, bf16[1,512,3072]{2,1,0:T(8,128)(2,1)}, u32[]{:S(2)}) copy-start(bf16[1,512,3072]{2,1,0:T(8,128)(2,1)} %param.7) | copy-start | bytes 9437188
  0.8 4.6 %copy-start.4 = (bf16[1,512,384]{2,1,0:T(8,128)(2,1)S(1)}, bf16[1,512,384]{2,1,0:T(8,128)(2,1)}, u32[]{:S(2)}) copy-start(bf16[1,512,384]{2,1,0:T(8,128)(2,1)} %param.6) | copy-start | bytes 1179652
  5.4 24.5 %copy-start.2 = (bf16[1,512,3072]{2,1,0:T(8,128)(2,1)S(1)}, bf16[1,512,3072]{2,1,0:T(8,128)(2,1)}, u32[]{:S(2)}) copy-start(bf16[1,512,3072]{2,1,0:T(8,128)(2,1)} %param.7) | copy-start | bytes 9437188
  9.1 18.8 %copy-start.3 = (f32[384,3072]{1,0:T(8,128)}, f32[384,3072]{1,0:T(8,128)S(1)}, u32[]{:S(2)}) copy-start(f32[384,3072]{1,0:T(8,128)S(1)} %fusion.9) | copy-start | bytes 14155780
  9.2 17.4 %collective-permute-start = (bf16[32,1536]{1,0:T(8,128)(2,1)S(1)}, bf16[32,1536]{1,0:T(8,128)(2,1)S(1)}, u32[]{:S(2)}, u32[]{:S(2)}) collective-permute-start(bf16[32,1536]{1,0:T(8,128)(2,1)S(1)} %get-tuple-element.10), channel_id=1, source_target_pairs={{0,4},{4,8},{8,12},{12,16},{16,20},{20,24},{24,28},{28,32},{32,36}... | collective-permute-start | bytes 294920 | tf_op jit(solution)/shard_map/ppermute | solution.py:16
  13.5 14.4 %collective-permute-start.6 = (bf16[32,1536]{1,0:T(8,128)(2,1)S(1)}, bf16[32,1536]{1,0:T(8,128)(2,1)S(1)}, u32[]{:S(2)}, u32[]{:S(2)}) collective-permute-start(bf16[32,1536]{1,0:T(8,128)(2,1)S(1)} %get-tuple-element.11), channel_id=1, source_target_pairs={{0,44},{4,0},{8,4},{12,8},{16,12},{20,16},{24,20},{28,24},{32,28},... | collective-permute-start | bytes 294920 | tf_op jit(solution)/shard_map/ppermute | solution.py:16
  28.0 9.3 %collective-permute-start.1 = (bf16[32,3072]{1,0:T(8,128)(2,1)S(1)}, bf16[32,3072]{1,0:T(8,128)(2,1)S(1)}, u32[]{:S(2)}, u32[]{:S(2)}) collective-permute-start(bf16[32,3072]{1,0:T(8,128)(2,1)S(1)} %pad_maximum_fusion), channel_id=1, source_target_pairs={{0,4},{4,8},{8,12},{12,16},{16,20},{20,24},{24,28},{28,32},{32,36}... | collective-permute-start | bytes 589832 | tf_op jit(solution)/shard_map/ppermute | solution.py:16
  38.3 19.2 %collective-permute-start.2 = (bf16[32,3072]{1,0:T(8,128)(2,1)S(1)}, bf16[32,3072]{1,0:T(8,128)(2,1)}, u32[]{:S(2)}, u32[]{:S(2)}) collective-permute-start(bf16[32,3072]{1,0:T(8,128)(2,1)S(1)} %add_convert_fusion.12), channel_id=1, source_target_pairs={{0,4},{4,8},{8,12},{12,16},{16,20},{20,24},{24,28},{28,32},{32,36}... | collective-permute-start | bytes 589832 | tf_op jit(solution)/shard_map/ppermute | solution.py:16
  41.4 31.6 %collective-permute-start.22 = (f32[2,512]{1,0:T(2,128)}, f32[2,512]{1,0:T(2,128)}, u32[]{:S(2)}, u32[]{:S(2)}) collective-permute-start(f32[2,512]{1,0:T(2,128)} %pad_maximum_fusion.2), channel_id=1, source_target_pairs={{0,48},{48,96},{96,144},{144,0},{1,49},{49,97},{97,145},{145,1},{2... | collective-permute-start | bytes 12296 | tf_op jit(solution)/shard_map/ppermute | solution.py:16
  44.8 32.1 %collective-permute-start.23 = (f32[2,512]{1,0:T(2,128)}, f32[2,512]{1,0:T(2,128)}, u32[]{:S(2)}, u32[]{:S(2)}) collective-permute-start(f32[2,512]{1,0:T(2,128)} %pad_maximum_fusion.2), channel_id=1, source_target_pairs={{0,96},{48,144},{96,0},{144,48},{1,97},{49,145},{97,1},{145,49},{2... | collective-permute-start | bytes 12296 | tf_op jit(solution)/shard_map/ppermute | solution.py:16
  49.5 29.4 %collective-permute-start.24 = (f32[2,512]{1,0:T(2,128)}, f32[2,512]{1,0:T(2,128)}, u32[]{:S(2)}, u32[]{:S(2)}) collective-permute-start(f32[2,512]{1,0:T(2,128)} %pad_maximum_fusion.2), channel_id=1, source_target_pairs={{0,144},{48,0},{96,48},{144,96},{1,145},{49,1},{97,49},{145,97},{2... | collective-permute-start | bytes 12296 | tf_op jit(solution)/shard_map/ppermute | solution.py:16
  55.3 52.6 %collective-permute-start.16 = (bf16[512,384]{1,0:T(8,128)(2,1)}, bf16[512,384]{1,0:T(8,128)(2,1)}, u32[]{:S(2)}, u32[]{:S(2)}) collective-permute-start(bf16[512,384]{1,0:T(8,128)(2,1)} %get-tuple-element.18), channel_id=1, source_target_pairs={{0,144},{48,0},{96,48},{144,96},{1,145},{49,1},{97,49},{145,97},{2... | collective-permute-start | bytes 1179656 | tf_op jit(solution)/shard_map/ppermute | solution.py:16
  58.6 8.8 %collective-permute-start.3 = (bf16[32,3072]{1,0:T(8,128)(2,1)S(1)}, bf16[32,3072]{1,0:T(8,128)(2,1)S(1)}, u32[]{:S(2)}, u32[]{:S(2)}) collective-permute-start(bf16[32,3072]{1,0:T(8,128)(2,1)S(1)} %add_convert_fusion.11), channel_id=1, source_target_pairs={{0,4},{4,8},{8,12},{12,16},{16,20},{20,24},{24,28},{28,32},{32,36}... | collective-permute-start | bytes 589832 | tf_op jit(solution)/shard_map/ppermute | solution.py:16
  67.4 40.5 %collective-permute-start.19 = (bf16[512,384]{1,0:T(8,128)(2,1)}, bf16[512,384]{1,0:T(8,128)(2,1)}, u32[]{:S(2)}, u32[]{:S(2)}) collective-permute-start(bf16[512,384]{1,0:T(8,128)(2,1)} %get-tuple-element.16), channel_id=1, source_target_pairs={{0,48},{48,96},{96,144},{144,0},{1,49},{49,97},{97,145},{145,1},{2... | collective-permute-start | bytes 1179656 | tf_op jit(solution)/shard_map/ppermute | solution.py:16
  73.0 15.2 %collective-permute-start.7 = (bf16[32,3072]{1,0:T(8,128)(2,1)S(1)}, bf16[32,3072]{1,0:T(8,128)(2,1)}, u32[]{:S(2)}, u32[]{:S(2)}) collective-permute-start(bf16[32,3072]{1,0:T(8,128)(2,1)S(1)} %pad_maximum_fusion.1), channel_id=1, source_target_pairs={{0,44},{4,0},{8,4},{12,8},{16,12},{20,16},{24,20},{28,24},{32,28},... | collective-permute-start | bytes 589832 | tf_op jit(solution)/shard_map/ppermute | solution.py:16
  76.9 14.0 %collective-permute-start.4 = (bf16[32,3072]{1,0:T(8,128)(2,1)}, bf16[32,3072]{1,0:T(8,128)(2,1)}, u32[]{:S(2)}, u32[]{:S(2)}) collective-permute-start(bf16[32,3072]{1,0:T(8,128)(2,1)} %add_convert_fusion.10), channel_id=1, source_target_pairs={{0,4},{4,8},{8,12},{12,16},{16,20},{20,24},{24,28},{28,32},{32,36}... | collective-permute-start | bytes 589832 | tf_op jit(solution)/shard_map/ppermute | solution.py:16
  79.6 5.5 %collective-permute-start.25 = (f32[2,512]{1,0:T(2,128)S(1)}, f32[2,512]{1,0:T(2,128)S(1)}, u32[]{:S(2)}, u32[]{:S(2)}) collective-permute-start(f32[2,512]{1,0:T(2,128)S(1)} %add_add_fusion), channel_id=1, source_target_pairs={{0,192},{192,0},{1,193},{193,1},{2,194},{194,2},{3,195},{195,3},{4... | collective-permute-start | bytes 12296 | tf_op jit(solution)/shard_map/ppermute | solution.py:16
  85.1 34.4 %collective-permute-start.18 = (bf16[512,384]{1,0:T(8,128)(2,1)S(1)}, bf16[512,384]{1,0:T(8,128)(2,1)S(1)}, u32[]{:S(2)}, u32[]{:S(2)}) collective-permute-start(bf16[512,384]{1,0:T(8,128)(2,1)S(1)} %get-tuple-element.17), channel_id=1, source_target_pairs={{0,144},{48,0},{96,48},{144,96},{1,145},{49,1},{97,49},{145,97},{2... | collective-permute-start | bytes 1179656 | tf_op jit(solution)/shard_map/ppermute | solution.py:16
  88.2 44.9 %collective-permute-start.15 = (bf16[512,384]{1,0:T(8,128)(2,1)S(1)}, bf16[512,384]{1,0:T(8,128)(2,1)S(1)}, u32[]{:S(2)}, u32[]{:S(2)}) collective-permute-start(bf16[512,384]{1,0:T(8,128)(2,1)S(1)} %get-tuple-element.15), channel_id=1, source_target_pairs={{0,48},{48,96},{96,144},{144,0},{1,49},{49,97},{97,145},{145,1},{2... | collective-permute-start | bytes 1179656 | tf_op jit(solution)/shard_map/ppermute | solution.py:16
  92.3 8.9 %collective-permute-start.8 = (bf16[32,3072]{1,0:T(8,128)(2,1)S(1)}, bf16[32,3072]{1,0:T(8,128)(2,1)S(1)}, u32[]{:S(2)}, u32[]{:S(2)}) collective-permute-start(bf16[32,3072]{1,0:T(8,128)(2,1)S(1)} %get-tuple-element.7), channel_id=1, source_target_pairs={{0,44},{4,0},{8,4},{12,8},{16,12},{20,16},{24,20},{28,24},{32,28},... | collective-permute-start | bytes 589832 | tf_op jit(solution)/shard_map/ppermute | solution.py:16
  102.3 14.3 %collective-permute-start.9 = (bf16[32,3072]{1,0:T(8,128)(2,1)S(1)}, bf16[32,3072]{1,0:T(8,128)(2,1)S(1)}, u32[]{:S(2)}, u32[]{:S(2)}) collective-permute-start(bf16[32,3072]{1,0:T(8,128)(2,1)S(1)} %add_convert_fusion.7), channel_id=1, source_target_pairs={{0,44},{4,0},{8,4},{12,8},{16,12},{20,16},{24,20},{28,24},{32,28},... | collective-permute-start | bytes 589832 | tf_op jit(solution)/shard_map/ppermute | solution.py:16
  109.5 10.9 %collective-permute-start.20 = (bf16[512,384]{1,0:T(8,128)(2,1)S(1)}, bf16[512,384]{1,0:T(8,128)(2,1)S(1)}, u32[]{:S(2)}, u32[]{:S(2)}) collective-permute-start(bf16[512,384]{1,0:T(8,128)(2,1)S(1)} %get-tuple-element.20), channel_id=1, source_target_pairs={{0,48},{48,96},{96,144},{144,0},{1,49},{49,97},{97,145},{145,1},{2... | collective-permute-start | bytes 1179656 | tf_op jit(solution)/shard_map/ppermute | solution.py:16
  112.0 21.1 %collective-permute-start.17 = (bf16[512,384]{1,0:T(8,128)(2,1)S(1)}, bf16[512,384]{1,0:T(8,128)(2,1)S(1)}, u32[]{:S(2)}, u32[]{:S(2)}) collective-permute-start(bf16[512,384]{1,0:T(8,128)(2,1)S(1)} %get-tuple-element.19), channel_id=1, source_target_pairs={{0,144},{48,0},{96,48},{144,96},{1,145},{49,1},{97,49},{145,97},{2... | collective-permute-start | bytes 1179656 | tf_op jit(solution)/shard_map/ppermute | solution.py:16
  117.6 10.5 %collective-permute-start.10 = (bf16[32,3072]{1,0:T(8,128)(2,1)S(1)}, bf16[32,3072]{1,0:T(8,128)(2,1)S(1)}, u32[]{:S(2)}, u32[]{:S(2)}) collective-permute-start(bf16[32,3072]{1,0:T(8,128)(2,1)S(1)} %add_convert_fusion.6), channel_id=1, source_target_pairs={{0,44},{4,0},{8,4},{12,8},{16,12},{20,16},{24,20},{28,24},{32,28},... | collective-permute-start | bytes 589832 | tf_op jit(solution)/shard_map/ppermute | solution.py:16
  121.5 11.6 %collective-permute-start.21 = (bf16[512,384]{1,0:T(8,128)(2,1)S(1)}, bf16[512,384]{1,0:T(8,128)(2,1)S(1)}, u32[]{:S(2)}, u32[]{:S(2)}) collective-permute-start(bf16[512,384]{1,0:T(8,128)(2,1)S(1)} %add_convert_fusion.2), channel_id=1, source_target_pairs={{0,192},{192,0},{1,193},{193,1},{2,194},{194,2},{3,195},{195,3},{4... | collective-permute-start | bytes 1179656 | tf_op jit(solution)/shard_map/ppermute | solution.py:16
  125.0 11.2 %collective-permute-start.5 = (bf16[32,3072]{1,0:T(8,128)(2,1)S(1)}, bf16[32,3072]{1,0:T(8,128)(2,1)S(1)}, u32[]{:S(2)}, u32[]{:S(2)}) collective-permute-start(bf16[32,3072]{1,0:T(8,128)(2,1)S(1)} %get-tuple-element.6), channel_id=1, source_target_pairs={{0,4},{4,8},{8,12},{12,16},{16,20},{20,24},{24,28},{28,32},{32,36}... | collective-permute-start | bytes 589832 | tf_op jit(solution)/shard_map/ppermute | solution.py:16
  129.2 7.6 %collective-permute-start.11 = (bf16[32,3072]{1,0:T(8,128)(2,1)S(1)}, bf16[32,3072]{1,0:T(8,128)(2,1)S(1)}, u32[]{:S(2)}, u32[]{:S(2)}) collective-permute-start(bf16[32,3072]{1,0:T(8,128)(2,1)S(1)} %add_convert_fusion.5), channel_id=1, source_target_pairs={{0,44},{4,0},{8,4},{12,8},{16,12},{20,16},{24,20},{28,24},{32,28},... | collective-permute-start | bytes 589832 | tf_op jit(solution)/shard_map/ppermute | solution.py:16
  134.9 14.7 %collective-permute-start.26 = (bf16[512,384]{1,0:T(8,128)(2,1)S(1)}, bf16[512,384]{1,0:T(8,128)(2,1)S(1)}, u32[]{:S(2)}, u32[]{:S(2)}) collective-permute-start(bf16[512,384]{1,0:T(8,128)(2,1)S(1)} %get-tuple-element.4), channel_id=1, source_target_pairs={{384,0},{385,1},{386,2},{387,3},{388,4},{389,5},{390,6},{391,7},{3... | collective-permute-start | bytes 1179656 | tf_op jit(solution)/shard_map/ppermute | solution.py:125
  137.8 12.7 %collective-permute-start.12 = (bf16[8,3072]{1,0:T(8,128)(2,1)S(1)}, bf16[8,3072]{1,0:T(8,128)(2,1)S(1)}, u32[]{:S(2)}, u32[]{:S(2)}) collective-permute-start(bf16[8,3072]{1,0:T(8,128)(2,1)S(1)} %get-tuple-element.21), channel_id=1, source_target_pairs={{0,1},{1,2},{2,3},{3,0},{4,5},{5,6},{6,7},{7,4},{8,9},{9,10},{10,1... | collective-permute-start | bytes 147464 | tf_op jit(solution)/shard_map/ppermute | solution.py:16
  142.6 10.4 %collective-permute-start.13 = (bf16[8,3072]{1,0:T(8,128)(2,1)S(1)}, bf16[8,3072]{1,0:T(8,128)(2,1)S(1)}, u32[]{:S(2)}, u32[]{:S(2)}) collective-permute-start(bf16[8,3072]{1,0:T(8,128)(2,1)S(1)} %get-tuple-element.23), channel_id=1, source_target_pairs={{0,2},{1,3},{2,0},{3,1},{4,6},{5,7},{6,4},{7,5},{8,10},{9,11},{10,... | collective-permute-start | bytes 147464 | tf_op jit(solution)/shard_map/ppermute | solution.py:16
  145.6 9.8 %collective-permute-start.14 = (bf16[8,3072]{1,0:T(8,128)(2,1)S(1)}, bf16[8,3072]{1,0:T(8,128)(2,1)S(1)}, u32[]{:S(2)}, u32[]{:S(2)}) collective-permute-start(bf16[8,3072]{1,0:T(8,128)(2,1)S(1)} %get-tuple-element.22), channel_id=1, source_target_pairs={{0,3},{1,0},{2,1},{3,2},{4,7},{5,4},{6,5},{7,6},{8,11},{9,8},{10,9... | collective-permute-start | bytes 147464 | tf_op jit(solution)/shard_map/ppermute | solution.py:16

commit v2 on v1

v2 whole, which is shorter than its diff:
```python
import jax
import jax.numpy as jnp
from jax import lax
from jax.sharding import Mesh
from jax.sharding import PartitionSpec as P

TOK_MB = 256
DP = ("dz", "dy")
MP = ("my", "mx")
F32 = jnp.float32
BF16 = jnp.bfloat16


def turned(value, axis, by):
    peers = lax.axis_size(axis)
    return lax.ppermute(value, axis, [(i, (i + by) % peers) for i in range(peers)])


def normalize(stream_rows):
    values = stream_rows.astype(F32)
    average = jnp.mean(values, axis=-1, keepdims=True)
    centred = values - average
    variance = jnp.mean(centred * centred, axis=-1, keepdims=True)
    inv_scale = lax.rsqrt(variance + 1e-06)
    return (centred * inv_scale, inv_scale)


def joined(own, got):
    return own.astype(F32) + got.astype(F32)


def tied(value, *others):
    return lax.optimization_barrier((value, *others))[0]


def sum_over_z(grad, start_between):
    peers = lax.axis_size("dz")
    place = lax.axis_index("dz")
    rows = grad.shape[0] // peers
    far = peers // 2

    def block(offset):
        return lax.dynamic_slice_in_dim(grad, ((place + offset) % peers) * rows, rows, 0)

    with jax.named_scope("up6"):
        up = turned(block(far).astype(BF16), "dz", 1)
    down = None
    for k in range(far - 1, 0, -1):
        if down is not None:
            up, down = lax.optimization_barrier((up, down))
        mine = joined(block(k), up).astype(BF16)
        with jax.named_scope(f"up{k}"):
            up = turned(mine, "dz", 1)
        mine = block(-k).astype(BF16) if down is None else joined(block(-k), down).astype(BF16)
        with jax.named_scope(f"down{k}"):
            down = turned(mine, "dz", -1)
    return block(0) + up.astype(F32) + down.astype(F32)


def sum_over_y(rows_sum):
    peers = lax.axis_size("dy")
    tiles = rows_sum.astype(BF16).reshape(peers, rows_sum.shape[0] // peers, rows_sum.shape[1])
    arrived = lax.all_to_all(tiles, "dy", split_axis=0, concat_axis=0, tiled=True)
    return arrived.astype(F32).sum(axis=0)


def halves(value):
    high = value.astype(BF16)
    return (high, (value - high.astype(F32)).astype(BF16))


def shards(value_grad, stream, weights, gain, top_grad, counts):
    section_index = lax.axis_index("section")
    model_index = lax.axis_index(MP)
    row_total = stream.shape[1]
    width = stream.shape[2]
    share_width = width // lax.axis_size(MP)
    first_col = model_index * share_width
    whitened, inv_scale = normalize(stream[0])
    gain_row = gain[0]
    normed = (whitened * gain_row).astype(BF16)
    micro_index = jnp.arange(row_total, dtype=jnp.int32) // TOK_MB
    live_mask = (micro_index < counts[0]).astype(BF16)
    masked = value_grad[0] * live_mask[:, None]
    grad = lax.dot_general(masked, normed, (((0,), (0,)), ((), ())), preferred_element_type=F32)
    weight_grad = sum_over_y(sum_over_z(grad, None)).astype(BF16)[None]
    partial = jnp.dot(value_grad[0], weights[0], preferred_element_type=F32).astype(BF16)
    scaled_part = partial.astype(F32) * gain_row
    first = jnp.sum(scaled_part, axis=1)
    second = jnp.sum(scaled_part * whitened, axis=1)
    extra = jnp.stack(halves(first) + halves(second))
    extra = jnp.concatenate([extra[:, :384], jnp.pad(extra[:, 384:], ((0, 0), (0, 256)))], axis=0)
    tiles = jnp.moveaxis(partial.reshape(row_total, 8, share_width), 1, 0)
    tiles = jnp.concatenate([tiles, jnp.broadcast_to(extra, (8, 8, share_width))], axis=1)
    with jax.named_scope("parts"):
        arrived = lax.all_to_all(tiles, MP, split_axis=0, concat_axis=0, tiled=True)
    norm_grad = arrived[:, :row_total].astype(F32).sum(axis=0)
    sums = arrived[:, row_total:].astype(F32).sum(axis=0)
    sums = jnp.concatenate([sums[:4], sums[4:, :128]], axis=1)
    totals = (sums[0] + sums[1], sums[2] + sums[3])
    white_share = lax.dynamic_slice_in_dim(whitened, first_col, share_width, 1)
    gain_share = lax.dynamic_slice_in_dim(gain_row, first_col, share_width, 0)
    scaled_grad = norm_grad * gain_share
    norm_back = inv_scale * (
        scaled_grad - totals[0][:, None] / width - white_share * (totals[1][:, None] / width)
    )
    top_slice = lax.dynamic_slice_in_dim(top_grad, first_col, share_width, 1).astype(F32)
    above_grad = (top_slice + norm_back).astype(BF16)
    below_grad = lax.ppermute(above_grad, "section", [(1, 0)])
    lower_grad = (below_grad.astype(F32) + norm_back).astype(BF16)
    result = jnp.where(section_index == 0, lower_grad, above_grad)
    return (weight_grad, result[None])


def solution(mesh):
    split = Mesh(
        mesh.devices.reshape(mesh.shape["section"], 2, 4, 12, 4),
        ("section", "my", "mx", "dz", "dy"),
    )
    placed = (
        P("section", DP, MP),
        P("section", DP, None),
        P("section", MP, None),
        P("section", None),
        P(DP, None),
        P(DP),
    )
    return jax.shard_map(
        shards,
        mesh=split,
        in_specs=placed,
        out_specs=(P("section", MP + DP, None), P("section", DP, MP)),
        check_vma=False,
    )
```

time: 158 us -> 129 us (0.82)
  the two profiles are of different devices: /device:TPU:16 before, /device:TPU:6 now
where the time goes in v2:
time: 129 us; the launch traced here: 128 us
  starting transfers between devices  61.7 us (48%)
  waiting for transfers between devices  30.4 us (24%)
  other arithmetic  22.8 us (18%)
  matrix products  7.83 us (6%)
  local copies, waits for them, and re-layouts  3.06 us (2%)
  between operations  1.81 us (1%)
    ppermute x11, starting transfers between devices, turned(): lax.ppermute(value, axis, [(i, (i + by) % peers) for i in range(peers)])  40 us
    ppermute x11, waiting for transfers between devices, turned(): lax.ppermute(value, axis, [(i, (i + by) % peers) for i in range(peers)])  19.5 us
    all_to_all x1, starting transfers between devices, shards(): arrived = lax.all_to_all(tiles, MP, split_axis=0, concat_axis=0, tiled=True)  13.8 us
    all_to_all x1, waiting for transfers between devices, sum_over_y(): lax.all_to_all(tiles, 'dy', split_axis=0, concat_axis=0, tiled=True)  10.9 us
    all_to_all x1, starting transfers between devices, sum_over_y(): lax.all_to_all(tiles, 'dy', split_axis=0, concat_axis=0, tiled=True)  6.61 us
    dot_general x1, matrix products, shards(): jnp.dot(value_grad[0], weights[0], preferred_element_type=F32).astype(BF16)  4.29 us
    convert_element_type x3, other arithmetic, sum_over_z(): joined(block(-k), down).astype(BF16)  3.55 us
    dot_general x1, matrix products, shards(): lax.dot_general(masked, normed, (((0,), (0,)), ((), ())), preferred_eleme...  3.54 us
  transfers between devices with their start and end apart: 14, of which 10 were waited for; matrix products, arithmetic and copies ran while one was open for 14% of the time, Pallas kernels for 0%

profile of v2, /device:TPU:6, one launch (start us, length us, event | category | flops | bytes accessed | tf_op | source)
XLA Modules:
  0.0 127.6 jit_solution(4663445680670170273)
XLA Ops:
  0.6 0.0 copy-start
  0.6 0.0 copy-start.1
  0.7 2.6 %convert_reduce_fusion = f32[512]{0:T(512)S(1)} fusion(bf16[1,512,3072]{2,1,0:T(8,128)(2,1)} %param.7), kind=kLoop, calls=%fused_computation.2 | loop fusion | flops 3145216 | bytes 3147776 | tf_op jit(solution)/shard_map/reduce_sum | solution.py:21
  3.2 0.4 copy-done.1
  3.6 1.0 fusion.6
  4.6 4.3 %fusion.7 = (f32[512]{0:T(512)S(1)}, f32[512]{0:T(512)S(1)}, f32[512,3072]{1,0:T(8,128)}, bf16[512,3072]{1,0:T(8,128)(2,1)S(1)}) fusion(f32[3072]{0:T(1024)S(1)} %bitcast.54, f32[512]{0:T(512)S(1)} %add_rsqrt_fusion, f32[512]{0:T(512)S(1)} %broadcast_multiply_fusion, bf16[1,512,3072]{2,1,0:T(8,128)(2,1)S(1)} %copy-done.1, ...), kind=kOutput, calls=%fused_computation.13 | convolution fusion | flops 1222114304 | bytes 15355904 | tf_op jit(solution)/shard_map/dot_general | solution.py:87
  9.0 0.3 copy.11
  9.4 1.9 %pad_maximum_fusion = bf16[8,520,384]{2,1,0:T(8,128)(2,1)} fusion(bf16[8,8,384]{2,1,0:T(8,128)(2,1)S(1)} %broadcast_in_dim.7, bf16[8,512,384]{2,1,0:T(8,128)(2,1)S(1)} %bitcast.47), kind=kLoop, calls=%fused_computation.15 | loop fusion | flops 6389760 | bytes 6389760 | tf_op jit(solution)/shard_map/concatenate | solution.py:94
  11.3 13.8 %all-to-all-start.1 = ((bf16[8,520,384]{2,1,0:T(8,128)(2,1)}), bf16[8,520,384]{2,1,0:T(8,128)(2,1)}, u32[]{:S(2)}, u32[]{:S(2)}) async-start(bf16[8,520,384]{2,1,0:T(8,128)(2,1)} %pad_maximum_fusion), calls=%async_computation.1 | async-start | bytes 6389760 | tf_op jit(solution)/shard_map/parts/all_to_all | solution.py:96
  25.8 3.5 %fusion.9 = f32[384,3072]{1,0:T(8,128)S(1)} fusion(bf16[1,512,3072]{2,1,0:T(8,128)(2,1)} %param.7, f32[3072]{0:T(1024)S(1)} %bitcast.55, f32[512]{0:T(512)S(1)} %add_rsqrt_fusion, f32[512]{0:T(512)S(1)} %broadcast_multiply_fusion, bf16[1,512,384]{2,1,0:T(8,128)(2,1)S(1)} %copy-done.3, bf16[512]{0:T(512)(128)(2,1)S(1)} %fusion.38), kind=kOutput, calls=%fused_computation.17 | convolution fusion | flops 1216020480 | bytes 8274944 | tf_op jit(solution)/shard_map/dot_general | solution.py:85
  29.4 2.2 %copy-done.2 = f32[384,3072]{1,0:T(8,128)} copy-done((f32[384,3072]{1,0:T(8,128)}, f32[384,3072]{1,0:T(8,128)S(1)}, u32[]{:S(2)}) %copy-start.2) | copy-done | bytes 4718616
  31.6 1.9 %collective-permute-start = (bf16[32,3072]{1,0:T(8,128)(2,1)S(1)}, bf16[32,3072]{1,0:T(8,128)(2,1)S(1)}, u32[]{:S(2)}, u32[]{:S(2)}) collective-permute-start(bf16[32,3072]{1,0:T(8,128)(2,1)S(1)} %get-tuple-element.29), channel_id=1, source_target_pairs={{0,4},{4,8},{8,12},{12,16},{16,20},{20,24},{24,28},{28,32},{32,36}... | collective-permute-start | bytes 589832 | tf_op jit(solution)/shard_map/up6/ppermute | solution.py:16
  33.6 6.5 %collective-permute-start.2 = (bf16[32,3072]{1,0:T(8,128)(2,1)S(1)}, bf16[32,3072]{1,0:T(8,128)(2,1)S(1)}, u32[]{:S(2)}, u32[]{:S(2)}) collective-permute-start(bf16[32,3072]{1,0:T(8,128)(2,1)S(1)} %get-tuple-element.28), channel_id=1, source_target_pairs={{0,44},{4,0},{8,4},{12,8},{16,12},{20,16},{24,20},{28,24},{32,28},... | collective-permute-start | bytes 589832 | tf_op jit(solution)/shard_map/down5/ppermute | solution.py:16
  40.1 2.4 %collective-permute-done = bf16[32,3072]{1,0:T(8,128)(2,1)S(1)} collective-permute-done((bf16[32,3072]{1,0:T(8,128)(2,1)S(1)}, bf16[32,3072]{1,0:T(8,128)(2,1)S(1)}, u32[]{:S(2)}, u32[]{:S(2)}) %collective-permute-start) | collective-permute-done | bytes 196640 | tf_op jit(solution)/shard_map/up6/ppermute | solution.py:16
  42.5 1.0 add_convert_fusion.11
  43.6 1.9 %collective-permute-start.1 = (bf16[32,3072]{1,0:T(8,128)(2,1)S(1)}, bf16[32,3072]{1,0:T(8,128)(2,1)S(1)}, u32[]{:S(2)}, u32[]{:S(2)}) collective-permute-start(bf16[32,3072]{1,0:T(8,128)(2,1)S(1)} %add_convert_fusion.11), channel_id=1, source_target_pairs={{0,4},{4,8},{8,12},{12,16},{16,20},{20,24},{24,28},{28,32},{32,36}... | collective-permute-start | bytes 589832 | tf_op jit(solution)/shard_map/up5/ppermute | solution.py:16
  45.5 0.0 collective-permute-done.2
  45.5 6.8 %collective-permute-done.1 = bf16[32,3072]{1,0:T(8,128)(2,1)S(1)} collective-permute-done((bf16[32,3072]{1,0:T(8,128)(2,1)S(1)}, bf16[32,3072]{1,0:T(8,128)(2,1)S(1)}, u32[]{:S(2)}, u32[]{:S(2)}) %collective-permute-start.1) | collective-permute-done | bytes 196640 | tf_op jit(solution)/shard_map/up5/ppermute | solution.py:16
  52.3 1.2 add_convert_fusion.9
  53.5 1.9 %collective-permute-start.3 = (bf16[32,3072]{1,0:T(8,128)(2,1)S(1)}, bf16[32,3072]{1,0:T(8,128)(2,1)S(1)}, u32[]{:S(2)}, u32[]{:S(2)}) collective-permute-start(bf16[32,3072]{1,0:T(8,128)(2,1)S(1)} %get-tuple-element.27), channel_id=1, source_target_pairs={{0,4},{4,8},{8,12},{12,16},{16,20},{20,24},{24,28},{28,32},{32,36}... | collective-permute-start | bytes 589832 | tf_op jit(solution)/shard_map/up4/ppermute | solution.py:16
  55.4 5.1 %collective-permute-start.4 = (bf16[32,3072]{1,0:T(8,128)(2,1)S(1)}, bf16[32,3072]{1,0:T(8,128)(2,1)S(1)}, u32[]{:S(2)}, u32[]{:S(2)}) collective-permute-start(bf16[32,3072]{1,0:T(8,128)(2,1)S(1)} %get-tuple-element.26), channel_id=1, source_target_pairs={{0,44},{4,0},{8,4},{12,8},{16,12},{20,16},{24,20},{28,24},{32,28},... | collective-permute-start | bytes 589832 | tf_op jit(solution)/shard_map/down4/ppermute | solution.py:16
  60.6 1.7 %collective-permute-done.3 = bf16[32,3072]{1,0:T(8,128)(2,1)S(1)} collective-permute-done((bf16[32,3072]{1,0:T(8,128)(2,1)S(1)}, bf16[32,3072]{1,0:T(8,128)(2,1)S(1)}, u32[]{:S(2)}, u32[]{:S(2)}) %collective-permute-start.3) | collective-permute-done | bytes 196640 | tf_op jit(solution)/shard_map/up4/ppermute | solution.py:16
  62.3 1.5 %collective-permute-done.4 = bf16[32,3072]{1,0:T(8,128)(2,1)S(1)} collective-permute-done((bf16[32,3072]{1,0:T(8,128)(2,1)S(1)}, bf16[32,3072]{1,0:T(8,128)(2,1)S(1)}, u32[]{:S(2)}, u32[]{:S(2)}) %collective-permute-start.4) | collective-permute-done | bytes 196640 | tf_op jit(solution)/shard_map/down4/ppermute | solution.py:16
  63.8 1.2 add_convert_fusion.7
  64.9 1.9 %collective-permute-start.5 = (bf16[32,3072]{1,0:T(8,128)(2,1)S(1)}, bf16[32,3072]{1,0:T(8,128)(2,1)S(1)}, u32[]{:S(2)}, u32[]{:S(2)}) collective-permute-start(bf16[32,3072]{1,0:T(8,128)(2,1)S(1)} %get-tuple-element.25), channel_id=1, source_target_pairs={{0,4},{4,8},{8,12},{12,16},{16,20},{20,24},{24,28},{28,32},{32,36}... | collective-permute-start | bytes 589832 | tf_op jit(solution)/shard_map/up3/ppermute | solution.py:16
  66.9 5.6 %collective-permute-start.6 = (bf16[32,3072]{1,0:T(8,128)(2,1)S(1)}, bf16[32,3072]{1,0:T(8,128)(2,1)S(1)}, u32[]{:S(2)}, u32[]{:S(2)}) collective-permute-start(bf16[32,3072]{1,0:T(8,128)(2,1)S(1)} %get-tuple-element.24), channel_id=1, source_target_pairs={{0,44},{4,0},{8,4},{12,8},{16,12},{20,16},{24,20},{28,24},{32,28},... | collective-permute-start | bytes 589832 | tf_op jit(solution)/shard_map/down3/ppermute | solution.py:16
  72.5 1.7 %collective-permute-done.5 = bf16[32,3072]{1,0:T(8,128)(2,1)S(1)} collective-permute-done((bf16[32,3072]{1,0:T(8,128)(2,1)S(1)}, bf16[32,3072]{1,0:T(8,128)(2,1)S(1)}, u32[]{:S(2)}, u32[]{:S(2)}) %collective-permute-start.5) | collective-permute-done | bytes 196640 | tf_op jit(solution)/shard_map/up3/ppermute | solution.py:16
  74.2 1.5 %collective-permute-done.6 = bf16[32,3072]{1,0:T(8,128)(2,1)S(1)} collective-permute-done((bf16[32,3072]{1,0:T(8,128)(2,1)S(1)}, bf16[32,3072]{1,0:T(8,128)(2,1)S(1)}, u32[]{:S(2)}, u32[]{:S(2)}) %collective-permute-start.6) | collective-permute-done | bytes 196640 | tf_op jit(solution)/shard_map/down3/ppermute | solution.py:16
  75.6 1.2 add_convert_fusion.5
  76.8 1.9 %collective-permute-start.7 = (bf16[32,3072]{1,0:T(8,128)(2,1)S(1)}, bf16[32,3072]{1,0:T(8,128)(2,1)S(1)}, u32[]{:S(2)}, u32[]{:S(2)}) collective-permute-start(bf16[32,3072]{1,0:T(8,128)(2,1)S(1)} %get-tuple-element.23), channel_id=1, source_target_pairs={{0,4},{4,8},{8,12},{12,16},{16,20},{20,24},{24,28},{28,32},{32,36}... | collective-permute-start | bytes 589832 | tf_op jit(solution)/shard_map/up2/ppermute | solution.py:16
  78.8 5.6 %collective-permute-start.8 = (bf16[32,3072]{1,0:T(8,128)(2,1)S(1)}, bf16[32,3072]{1,0:T(8,128)(2,1)S(1)}, u32[]{:S(2)}, u32[]{:S(2)}) collective-permute-start(bf16[32,3072]{1,0:T(8,128)(2,1)S(1)} %get-tuple-element.22), channel_id=1, source_target_pairs={{0,44},{4,0},{8,4},{12,8},{16,12},{20,16},{24,20},{28,24},{32,28},... | collective-permute-start | bytes 589832 | tf_op jit(solution)/shard_map/down2/ppermute | solution.py:16
  84.5 1.6 %collective-permute-done.7 = bf16[32,3072]{1,0:T(8,128)(2,1)S(1)} collective-permute-done((bf16[32,3072]{1,0:T(8,128)(2,1)S(1)}, bf16[32,3072]{1,0:T(8,128)(2,1)S(1)}, u32[]{:S(2)}, u32[]{:S(2)}) %collective-permute-start.7) | collective-permute-done | bytes 196640 | tf_op jit(solution)/shard_map/up2/ppermute | solution.py:16
  86.1 1.5 %collective-permute-done.8 = bf16[32,3072]{1,0:T(8,128)(2,1)S(1)} collective-permute-done((bf16[32,3072]{1,0:T(8,128)(2,1)S(1)}, bf16[32,3072]{1,0:T(8,128)(2,1)S(1)}, u32[]{:S(2)}, u32[]{:S(2)}) %collective-permute-start.8) | collective-permute-done | bytes 196640 | tf_op jit(solution)/shard_map/down2/ppermute | solution.py:16
  87.5 1.9 %add_convert_fusion.4 = (bf16[32,3072]{1,0:T(8,128)(2,1)}, bf16[32,3072]{1,0:T(8,128)(2,1)}) fusion(bf16[32,3072]{1,0:T(8,128)(2,1)S(1)} %collective-permute-done.7, f32[384,3072]{1,0:T(8,128)} %copy-done.2, s32[]{:T(128)S(6)} %select_n.113, bf16[32,3072]{1,0:T(8,128)(2,1)S(1)} %collective-permute-done.8, s32[]{:T(128)S(6)} %select_n.133), kind=kLoop, calls=%fused_computation.32 | loop fusion | flops 589824 | bytes 1572872 | tf_op jit(solution)/shard_map/convert_element_type | solution.py:51
  89.5 5.6 %collective-permute-start.10 = (bf16[32,3072]{1,0:T(8,128)(2,1)}, bf16[32,3072]{1,0:T(8,128)(2,1)}, u32[]{:S(2)}, u32[]{:S(2)}) collective-permute-start(bf16[32,3072]{1,0:T(8,128)(2,1)} %get-tuple-element.21), channel_id=1, source_target_pairs={{0,44},{4,0},{8,4},{12,8},{16,12},{20,16},{24,20},{28,24},{32,28},... | collective-permute-start | bytes 589832 | tf_op jit(solution)/shard_map/down1/ppermute | solution.py:16
  95.1 1.9 %collective-permute-start.9 = (bf16[32,3072]{1,0:T(8,128)(2,1)}, bf16[32,3072]{1,0:T(8,128)(2,1)}, u32[]{:S(2)}, u32[]{:S(2)}) collective-permute-start(bf16[32,3072]{1,0:T(8,128)(2,1)} %get-tuple-element.20), channel_id=1, source_target_pairs={{0,4},{4,8},{8,12},{12,16},{16,20},{20,24},{24,28},{28,32},{32,36}... | collective-permute-start | bytes 589832 | tf_op jit(solution)/shard_map/up1/ppermute | solution.py:16
  97.0 0.0 all-to-all-done.1
  97.0 0.8 convert_reduce_fusion.2
  97.9 2.4 %convert_reduce_fusion.1 = f32[512,384]{1,0:T(8,128)S(1)} fusion(bf16[8,520,384]{2,1,0:T(8,128)(2,1)} %all-to-all-done.1), kind=kLoop, calls=%fused_computation.10 | loop fusion | flops 2949120 | bytes 3932160 | tf_op jit(solution)/shard_map/reduce_sum | solution.py:97
  100.3 1.5 %add_convert_fusion.1 = bf16[512,384]{1,0:T(8,128)(2,1)S(1)} fusion(bf16[512,3072]{1,0:T(8,128)(2,1)} %param.10, s32[]{:T(128)S(6)} %select_n.135, f32[512]{0:T(512)S(1)} %bitcast.52, f32[512,3072]{1,0:T(8,128)} %get-tuple-element.30, f32[512]{0:T(512)S(1)} %bitcast.50, f32[512,384]{1,0:T(8,128)S(1)} %convert_reduce_fusion.1, f32[384]{0:T(512)S(1)} %fusion.41, ...), kind=kLoop, calls=%fused_computation.24 | loop fusion | flops 1572864 | bytes 2366980 | tf_op jit(solution)/shard_map/convert_element_type | solution.py:108
  101.8 1.3 %collective-permute-start.11 = (bf16[512,384]{1,0:T(8,128)(2,1)S(1)}, bf16[512,384]{1,0:T(8,128)(2,1)}, u32[]{:S(2)}, u32[]{:S(2)}) collective-permute-start(bf16[512,384]{1,0:T(8,128)(2,1)S(1)} %add_convert_fusion.1), channel_id=1, source_target_pairs={{384,0},{385,1},{386,2},{387,3},{388,4},{389,5},{390,6},{391,7},{3... | collective-permute-start | bytes 1179656 | tf_op jit(solution)/shard_map/ppermute | solution.py:109
  103.1 0.0 collective-permute-done.10
  103.1 1.0 collective-permute-done.9
  104.2 1.9 %fusion.20 = bf16[4,8,3072]{2,1,0:T(8,128)(2,1)} fusion(bf16[32,3072]{1,0:T(8,128)(2,1)} %collective-permute-done.10, bf16[32,3072]{1,0:T(8,128)(2,1)} %collective-permute-done.9, f32[384,3072]{1,0:T(8,128)} %copy-done.2, s32[]{:T(128)S(6)} %select_n.111), kind=kLoop, calls=%fused_computation.43 | loop fusion | flops 491520 | bytes 983044 | tf_op jit(solution)/shard_map/reshape | solution.py:62
  106.1 6.6 %all-to-all-start = ((bf16[4,8,3072]{2,1,0:T(8,128)(2,1)}), bf16[4,8,3072]{2,1,0:T(8,128)(2,1)}, u32[]{:S(2)}, u32[]{:S(2)}) async-start(bf16[4,8,3072]{2,1,0:T(8,128)(2,1)} %fusion.20), calls=%async_computation | async-start | bytes 393216 | tf_op jit(solution)/shard_map/all_to_all | solution.py:63
  112.7 10.9 %all-to-all-done = bf16[4,8,3072]{2,1,0:T(8,128)(2,1)} async-done(((bf16[4,8,3072]{2,1,0:T(8,128)(2,1)}), bf16[4,8,3072]{2,1,0:T(8,128)(2,1)}, u32[]{:S(2)}, u32[]{:S(2)}) %all-to-all-start) | async-done | bytes 196640 | tf_op jit(solution)/shard_map/all_to_all | solution.py:63
  123.6 1.6 %reduce_sum.72 = bf16[8,3072]{1,0:T(8,128)(2,1)} reduce(bf16[4,8,3072]{2,1,0:T(8,128)(2,1)} %all-to-all-done, bf16[]{:T(256)} %constant.100.clone.1), dimensions={0}, to_apply=%region_2.3 | reduce | flops 73728 | bytes 245762 | tf_op jit(solution)/shard_map/reduce_sum | solution.py:64
  125.2 2.4 %fusion.16 = bf16[1,512,384]{2,1,0:T(8,128)(2,1)} fusion(bf16[512,384]{1,0:T(8,128)(2,1)S(1)} %add_convert_fusion.1, bf16[512,384]{1,0:T(8,128)(2,1)} %collective-permute-done.11, pred[]{:T(512)S(6)} %eq.16, f32[512]{0:T(512)S(1)} %bitcast.53, f32[512,3072]{1,0:T(8,128)} %get-tuple-element.30, s32[]{:T(128)S(6)} %select_n.135, f32[512]{0:T(512)S(1)} %bitcast.51, ...), kind=kLoop, calls=%fused_computation.27 | loop fusion | flops 1769472 | bytes 2760197 | tf_op jit(solution)/shard_map/broadcast_in_dim | solution.py:112
  (23 shorter events, 0.2 us)
Async XLA Ops:
  0.6 4.0 %copy-start = (bf16[1,384,3072]{2,1,0:T(8,128)(2,1)S(1)}, bf16[1,384,3072]{2,1,0:T(8,128)(2,1)}, u32[]{:S(2)}) copy-start(bf16[1,384,3072]{2,1,0:T(8,128)(2,1)} %param.8) | copy-start | bytes 7077892
  0.6 3.0 %copy-start.1 = (bf16[1,512,3072]{2,1,0:T(8,128)(2,1)S(1)}, bf16[1,512,3072]{2,1,0:T(8,128)(2,1)}, u32[]{:S(2)}) copy-start(bf16[1,512,3072]{2,1,0:T(8,128)(2,1)} %param.7) | copy-start | bytes 9437188
  0.7 4.0 %copy-start.4 = (f32[1,3072]{1,0:T(1,128)S(1)}, f32[1,3072]{1,0:T(1,128)}, u32[]{:S(2)}) copy-start(f32[1,3072]{1,0:T(1,128)} %param.9) | copy-start | bytes 36868
  0.7 4.0 %copy-start.3 = (bf16[1,512,384]{2,1,0:T(8,128)(2,1)S(1)}, bf16[1,512,384]{2,1,0:T(8,128)(2,1)}, u32[]{:S(2)}) copy-start(bf16[1,512,384]{2,1,0:T(8,128)(2,1)} %param.6) | copy-start | bytes 1179652
  11.3 85.7 %all-to-all-start.1 = ((bf16[8,520,384]{2,1,0:T(8,128)(2,1)}), bf16[8,520,384]{2,1,0:T(8,128)(2,1)}, u32[]{:S(2)}, u32[]{:S(2)}) async-start(bf16[8,520,384]{2,1,0:T(8,128)(2,1)} %pad_maximum_fusion), calls=%async_computation.1 | async-start | bytes 6389760 | tf_op jit(solution)/shard_map/parts/all_to_all | solution.py:96
  29.4 2.2 %copy-start.2 = (f32[384,3072]{1,0:T(8,128)}, f32[384,3072]{1,0:T(8,128)S(1)}, u32[]{:S(2)}) copy-start(f32[384,3072]{1,0:T(8,128)S(1)} %fusion.9) | copy-start | bytes 14155780
  31.6 10.9 %collective-permute-start = (bf16[32,3072]{1,0:T(8,128)(2,1)S(1)}, bf16[32,3072]{1,0:T(8,128)(2,1)S(1)}, u32[]{:S(2)}, u32[]{:S(2)}) collective-permute-start(bf16[32,3072]{1,0:T(8,128)(2,1)S(1)} %get-tuple-element.29), channel_id=1, source_target_pairs={{0,4},{4,8},{8,12},{12,16},{16,20},{20,24},{24,28},{28,32},{32,36}... | collective-permute-start | bytes 589832 | tf_op jit(solution)/shard_map/up6/ppermute | solution.py:16
  33.6 12.0 %collective-permute-start.2 = (bf16[32,3072]{1,0:T(8,128)(2,1)S(1)}, bf16[32,3072]{1,0:T(8,128)(2,1)S(1)}, u32[]{:S(2)}, u32[]{:S(2)}) collective-permute-start(bf16[32,3072]{1,0:T(8,128)(2,1)S(1)} %get-tuple-element.28), channel_id=1, source_target_pairs={{0,44},{4,0},{8,4},{12,8},{16,12},{20,16},{24,20},{28,24},{32,28},... | collective-permute-start | bytes 589832 | tf_op jit(solution)/shard_map/down5/ppermute | solution.py:16
  43.6 8.8 %collective-permute-start.1 = (bf16[32,3072]{1,0:T(8,128)(2,1)S(1)}, bf16[32,3072]{1,0:T(8,128)(2,1)S(1)}, u32[]{:S(2)}, u32[]{:S(2)}) collective-permute-start(bf16[32,3072]{1,0:T(8,128)(2,1)S(1)} %add_convert_fusion.11), channel_id=1, source_target_pairs={{0,4},{4,8},{8,12},{12,16},{16,20},{20,24},{24,28},{28,32},{32,36}... | collective-permute-start | bytes 589832 | tf_op jit(solution)/shard_map/up5/ppermute | solution.py:16
  53.5 8.8 %collective-permute-start.3 = (bf16[32,3072]{1,0:T(8,128)(2,1)S(1)}, bf16[32,3072]{1,0:T(8,128)(2,1)S(1)}, u32[]{:S(2)}, u32[]{:S(2)}) collective-permute-start(bf16[32,3072]{1,0:T(8,128)(2,1)S(1)} %get-tuple-element.27), channel_id=1, source_target_pairs={{0,4},{4,8},{8,12},{12,16},{16,20},{20,24},{24,28},{28,32},{32,36}... | collective-permute-start | bytes 589832 | tf_op jit(solution)/shard_map/up4/ppermute | solution.py:16
  55.4 8.3 %collective-permute-start.4 = (bf16[32,3072]{1,0:T(8,128)(2,1)S(1)}, bf16[32,3072]{1,0:T(8,128)(2,1)S(1)}, u32[]{:S(2)}, u32[]{:S(2)}) collective-permute-start(bf16[32,3072]{1,0:T(8,128)(2,1)S(1)} %get-tuple-element.26), channel_id=1, source_target_pairs={{0,44},{4,0},{8,4},{12,8},{16,12},{20,16},{24,20},{28,24},{32,28},... | collective-permute-start | bytes 589832 | tf_op jit(solution)/shard_map/down4/ppermute | solution.py:16
  64.9 9.2 %collective-permute-start.5 = (bf16[32,3072]{1,0:T(8,128)(2,1)S(1)}, bf16[32,3072]{1,0:T(8,128)(2,1)S(1)}, u32[]{:S(2)}, u32[]{:S(2)}) collective-permute-start(bf16[32,3072]{1,0:T(8,128)(2,1)S(1)} %get-tuple-element.25), channel_id=1, source_target_pairs={{0,4},{4,8},{8,12},{12,16},{16,20},{20,24},{24,28},{28,32},{32,36}... | collective-permute-start | bytes 589832 | tf_op jit(solution)/shard_map/up3/ppermute | solution.py:16
  66.9 8.8 %collective-permute-start.6 = (bf16[32,3072]{1,0:T(8,128)(2,1)S(1)}, bf16[32,3072]{1,0:T(8,128)(2,1)S(1)}, u32[]{:S(2)}, u32[]{:S(2)}) collective-permute-start(bf16[32,3072]{1,0:T(8,128)(2,1)S(1)} %get-tuple-element.24), channel_id=1, source_target_pairs={{0,44},{4,0},{8,4},{12,8},{16,12},{20,16},{24,20},{28,24},{32,28},... | collective-permute-start | bytes 589832 | tf_op jit(solution)/shard_map/down3/ppermute | solution.py:16
  76.8 9.2 %collective-permute-start.7 = (bf16[32,3072]{1,0:T(8,128)(2,1)S(1)}, bf16[32,3072]{1,0:T(8,128)(2,1)S(1)}, u32[]{:S(2)}, u32[]{:S(2)}) collective-permute-start(bf16[32,3072]{1,0:T(8,128)(2,1)S(1)} %get-tuple-element.23), channel_id=1, source_target_pairs={{0,4},{4,8},{8,12},{12,16},{16,20},{20,24},{24,28},{28,32},{32,36}... | collective-permute-start | bytes 589832 | tf_op jit(solution)/shard_map/up2/ppermute | solution.py:16
  78.8 8.8 %collective-permute-start.8 = (bf16[32,3072]{1,0:T(8,128)(2,1)S(1)}, bf16[32,3072]{1,0:T(8,128)(2,1)S(1)}, u32[]{:S(2)}, u32[]{:S(2)}) collective-permute-start(bf16[32,3072]{1,0:T(8,128)(2,1)S(1)} %get-tuple-element.22), channel_id=1, source_target_pairs={{0,44},{4,0},{8,4},{12,8},{16,12},{20,16},{24,20},{28,24},{32,28},... | collective-permute-start | bytes 589832 | tf_op jit(solution)/shard_map/down2/ppermute | solution.py:16
  89.5 13.6 %collective-permute-start.10 = (bf16[32,3072]{1,0:T(8,128)(2,1)}, bf16[32,3072]{1,0:T(8,128)(2,1)}, u32[]{:S(2)}, u32[]{:S(2)}) collective-permute-start(bf16[32,3072]{1,0:T(8,128)(2,1)} %get-tuple-element.21), channel_id=1, source_target_pairs={{0,44},{4,0},{8,4},{12,8},{16,12},{20,16},{24,20},{28,24},{32,28},... | collective-permute-start | bytes 589832 | tf_op jit(solution)/shard_map/down1/ppermute | solution.py:16
  95.1 9.1 %collective-permute-start.9 = (bf16[32,3072]{1,0:T(8,128)(2,1)}, bf16[32,3072]{1,0:T(8,128)(2,1)}, u32[]{:S(2)}, u32[]{:S(2)}) collective-permute-start(bf16[32,3072]{1,0:T(8,128)(2,1)} %get-tuple-element.20), channel_id=1, source_target_pairs={{0,4},{4,8},{8,12},{12,16},{16,20},{20,24},{24,28},{28,32},{32,36}... | collective-permute-start | bytes 589832 | tf_op jit(solution)/shard_map/up1/ppermute | solution.py:16
  101.8 23.4 %collective-permute-start.11 = (bf16[512,384]{1,0:T(8,128)(2,1)S(1)}, bf16[512,384]{1,0:T(8,128)(2,1)}, u32[]{:S(2)}, u32[]{:S(2)}) collective-permute-start(bf16[512,384]{1,0:T(8,128)(2,1)S(1)} %add_convert_fusion.1), channel_id=1, source_target_pairs={{384,0},{385,1},{386,2},{387,3},{388,4},{389,5},{390,6},{391,7},{3... | collective-permute-start | bytes 1179656 | tf_op jit(solution)/shard_map/ppermute | solution.py:109
  106.1 17.5 %all-to-all-start = ((bf16[4,8,3072]{2,1,0:T(8,128)(2,1)}), bf16[4,8,3072]{2,1,0:T(8,128)(2,1)}, u32[]{:S(2)}, u32[]{:S(2)}) async-start(bf16[4,8,3072]{2,1,0:T(8,128)(2,1)} %fusion.20), calls=%async_computation | async-start | bytes 393216 | tf_op jit(solution)/shard_map/all_to_all | solution.py:63

commit v3 on v2

v3 whole, which is shorter than its diff:
```python
import jax
import jax.numpy as jnp
from jax import lax
from jax.experimental import pallas as pl
from jax.experimental.pallas import tpu as pltpu
from jax.sharding import Mesh
from jax.sharding import PartitionSpec as P


TOK_MB = 256
DP = ("dz", "dy")
MP = ("my", "mx")
F32 = jnp.float32
BF16 = jnp.bfloat16
TOK = 512
BLOCK = 128
CHUNK = 16
WIDTH = 3072
SHARE = 384
RING = 12
ROWS = SHARE // RING
PARTS = 8
EXTRA = 8
COLS = 512


def in_hbm(*arrays):
    return [pltpu.with_memory_space_constraint(a, pltpu.HBM) for a in arrays]


def front_kernel(scal, stream, value_grad, gain, white, scale, average, own, *rest):
    blocks, (normed, masked, grad) = rest[:-3], rest[-3:]
    step = pl.program_id(0)
    base = step * BLOCK
    gains = gain[...]

    def chunk(i, carry):
        rows = pl.ds(pl.multiple_of(i * CHUNK, CHUNK), CHUNK)
        values = stream[rows, :].astype(F32)
        mean = jnp.sum(values, axis=1, keepdims=True) * (1.0 / WIDTH)
        centred = values - mean
        variance = jnp.sum(centred * centred, axis=1, keepdims=True) * (1.0 / WIDTH)
        inv = lax.rsqrt(variance + 1e-06)
        at = pl.ds(pl.multiple_of(base + i * CHUNK, CHUNK), CHUNK)
        normed[at, :] = (centred * inv * gains).astype(BF16)
        scale[rows, :] = inv
        average[rows, :] = mean
        return carry

    lax.fori_loop(0, BLOCK // CHUNK, chunk, 0, unroll=2)
    share = stream[:, pl.ds(pl.multiple_of(scal[2] * SHARE, 128), SHARE)].astype(F32)
    white[...] = (share - average[...]) * scale[...]
    live = jnp.where(base // TOK_MB < scal[3], 1.0, 0.0)
    masked[pl.ds(pl.multiple_of(base, BLOCK), BLOCK), :] = (value_grad[...].astype(F32) * live).astype(BF16)

    @pl.when(step == TOK // BLOCK - 1)
    def _():
        left = masked[...].T
        for n in range(WIDTH // COLS):
            cols = slice(n * COLS, (n + 1) * COLS)
            grad[...] = jnp.dot(left, normed[:, cols], preferred_element_type=F32)
            for r in range(RING):
                at = lax.rem(scal[0] + r * scal[1] + RING, RING) * ROWS
                piece = grad[pl.ds(pl.multiple_of(at, ROWS), ROWS), :]
                if r == 0:
                    own[:, cols] = piece
                else:
                    blocks[r - 1][:, cols] = piece.astype(BF16)


def front(scal, stream, value_grad, gain):
    token = lambda width: pl.BlockSpec((BLOCK, width), lambda i, s: (i, 0))
    whole = lambda shape: pl.BlockSpec(shape, lambda i, s: (0,) * len(shape))
    out = [((TOK, SHARE), F32), ((TOK, 1), F32), ((TOK, 1), F32), ((ROWS, WIDTH), F32)]
    out += [((ROWS, WIDTH), BF16)] * (RING - 1)
    return pl.pallas_call(
        front_kernel,
        grid_spec=pltpu.PrefetchScalarGridSpec(
            num_scalar_prefetch=1,
            grid=(TOK // BLOCK,),
            in_specs=[token(WIDTH), token(SHARE), whole((1, WIDTH))],
            out_specs=[token(SHARE), token(1), token(1)] + [whole((ROWS, WIDTH))] * RING,
            scratch_shapes=[
                pltpu.VMEM((TOK, WIDTH), BF16),
                pltpu.VMEM((TOK, SHARE), BF16),
                pltpu.VMEM((SHARE, COLS), F32),
            ],
        ),
        out_shape=[jax.ShapeDtypeStruct(*o) if i == 3 + RING // 2 else pltpu.HBM(*o) for i, o in enumerate(out)],
        compiler_params=pltpu.CompilerParams(
            dimension_semantics=("arbitrary",), vmem_limit_bytes=40 * 1024 * 1024
        ),
        cost_estimate=pl.CostEstimate(flops=2 * TOK * SHARE * WIDTH * 4, transcendentals=0, bytes_accessed=8_000_000),
    )(scal, *in_hbm(stream, value_grad, gain))


def parts_kernel(value_grad, weights, stream, gain, scale, average, out, held, extra, first, second, sems):
    m = pl.program_id(0)

    @pl.when(m == 0)
    def _():
        first[...] = jnp.zeros_like(first)
        second[...] = jnp.zeros_like(second)

    part = jnp.dot(value_grad[...], weights[...], preferred_element_type=F32).astype(BF16)
    held[m] = part
    copy = pltpu.make_async_copy(held.at[m], out.at[m, pl.ds(0, TOK), :], sems.at[m])
    copy.start()
    scaled = part.astype(F32) * gain[...]
    product = scaled * ((stream[...].astype(F32) - average[...]) * scale[...])
    first[...] += scaled[:, :128] + scaled[:, 128:256] + scaled[:, 256:]
    second[...] += product[:, :128] + product[:, 128:256] + product[:, 256:]

    @pl.when(m == PARTS - 1)
    def _():
        lines = []
        for total in (first, second):
            line = jnp.sum(total[...].T, axis=0, keepdims=True)
            high = line.astype(BF16).astype(F32)
            lines += [high, line - high]
        stacked = jnp.concatenate(lines, axis=0)
        tail = jnp.concatenate([stacked[:, SHARE:], jnp.zeros((4, SHARE - 128), F32)], axis=1)
        extra[...] = jnp.concatenate([stacked[:, :SHARE], tail], axis=0).astype(BF16)
        ends = []
        for j in range(PARTS):
            end = pltpu.make_async_copy(extra, out.at[j, pl.ds(TOK, EXTRA), :], sems.at[PARTS + j])
            end.start()
            ends.append(end)
        for j in range(PARTS):
            pltpu.make_async_copy(held.at[j], out.at[j, pl.ds(0, TOK), :], sems.at[j]).wait()
            ends[j].wait()


def parts(value_grad, weights, stream, gain, scale, average):
    whole = lambda shape: pl.BlockSpec(shape, lambda m: (0,) * len(shape))
    cols = lambda rows: pl.BlockSpec((rows, SHARE), lambda m: (0, m))
    return pl.pallas_call(
        parts_kernel,
        grid=(PARTS,),
        in_specs=[whole((TOK, SHARE)), cols(SHARE), cols(TOK), cols(1), whole((TOK, 1)), whole((TOK, 1))],
        out_specs=pl.BlockSpec(memory_space=pl.ANY),
        out_shape=pltpu.HBM((PARTS, TOK + EXTRA, SHARE), BF16),
        scratch_shapes=[
            pltpu.VMEM((PARTS, TOK, SHARE), BF16),
            pltpu.VMEM((EXTRA, SHARE), BF16),
            pltpu.VMEM((TOK, 128), F32),
            pltpu.VMEM((TOK, 128), F32),
            pltpu.SemaphoreType.DMA((2 * PARTS,)),
        ],
        compiler_params=pltpu.CompilerParams(
            dimension_semantics=("arbitrary",), vmem_limit_bytes=24 * 1024 * 1024
        ),
        cost_estimate=pl.CostEstimate(flops=2 * TOK * SHARE * WIDTH * 3, transcendentals=0, bytes_accessed=9_000_000),
    )(value_grad, weights, stream, gain, scale, average)


def back_kernel(scal, arrived, extra, white, scale, gain, top, back, above, columns):
    step = pl.program_id(0)

    @pl.when(step == 0)
    def _():
        sums = jnp.sum(extra[...].astype(F32), axis=0)
        lines = jnp.concatenate([sums[:4], sums[4:, :128]], axis=1)
        for j, line in enumerate((lines[0:1] + lines[1:2], lines[2:3] + lines[3:4])):
            for b in range(TOK // BLOCK):
                square = jnp.broadcast_to(line[:, b * BLOCK : (b + 1) * BLOCK], (BLOCK, BLOCK))
                columns[j, b * BLOCK : (b + 1) * BLOCK, :] = square.T * (1.0 / WIDTH)

    rows = pl.ds(pl.multiple_of(step * BLOCK, BLOCK), BLOCK)
    mean = columns[0, rows, :][:, :1]
    slope = columns[1, rows, :][:, :1]
    total = arrived[0].astype(F32)
    for j in range(1, PARTS):
        total = total + arrived[j].astype(F32)
    branch = scale[...] * (total * gain[...] - mean - white[...] * slope)
    back[...] = branch
    above[...] = (top[...].astype(F32) + branch).astype(BF16)


def backward(scal, arrived, white, scale, gain, top):
    token = lambda width: pl.BlockSpec((BLOCK, width), lambda i, s: (i, 0))
    return pl.pallas_call(
        back_kernel,
        grid_spec=pltpu.PrefetchScalarGridSpec(
            num_scalar_prefetch=1,
            grid=(TOK // BLOCK,),
            in_specs=[
                pl.BlockSpec((PARTS, BLOCK, SHARE), lambda i, s: (0, i, 0)),
                pl.BlockSpec((PARTS, EXTRA, SHARE), lambda i, s: (0, TOK // EXTRA, 0)),
                token(SHARE),
                token(1),
                pl.BlockSpec((1, SHARE), lambda i, s: (0, s[2])),
                pl.BlockSpec((BLOCK, SHARE), lambda i, s: (i, s[2])),
            ],
            out_specs=[token(SHARE), token(SHARE)],
            scratch_shapes=[pltpu.VMEM((2, TOK, BLOCK), F32)],
        ),
        out_shape=[jax.ShapeDtypeStruct((TOK, SHARE), F32), jax.ShapeDtypeStruct((TOK, SHARE), BF16)],
        compiler_params=pltpu.CompilerParams(
            dimension_semantics=("arbitrary",), vmem_limit_bytes=16 * 1024 * 1024
        ),
        cost_estimate=pl.CostEstimate(flops=500_000_000, transcendentals=0, bytes_accessed=6_000_000),
    )(scal, *in_hbm(arrived, arrived, white, scale, gain, top))


def swapped(value, axis, first):
    peers = lax.axis_size(axis)
    pairs = []
    for i in range(first, peers, 2):
        pairs += [(i, (i + 1) % peers), ((i + 1) % peers, i)]
    return lax.ppermute(value, axis, pairs)


def tied(value, *others):
    return lax.optimization_barrier((value, *others))[0]


def joined(own, got):
    return (own.astype(F32) + got.astype(F32)).astype(BF16)


def sum_over_z(own, blocks):
    def block(link, distance):
        return blocks[(distance if link == 0 else RING - distance) - 1]

    far = RING // 2
    long = swapped(block(0, far), "dz", 0)
    short = None
    link = 0
    for k in range(far - 1, 0, -1):
        link = 1 - link
        if short is None:
            mine_short = tied(block(1 - link, k), long)
        else:
            mine_short = joined(block(1 - link, k), tied(short, long))
        mine = joined(block(link, k), long)
        long = swapped(mine, "dz", link)
        short = swapped(mine_short, "dz", 1 - link)
    return own + long.astype(F32) + short.astype(F32)


def sum_over_y(rows_sum):
    peers = lax.axis_size("dy")
    tiles = rows_sum.astype(BF16).reshape(peers, rows_sum.shape[0] // peers, rows_sum.shape[1])
    arrived = lax.all_to_all(tiles, "dy", split_axis=0, concat_axis=0, tiled=True)
    return arrived.astype(F32).sum(axis=0)


def shards(value_grad, stream, weights, gain, top_grad, counts):
    section_index = lax.axis_index("section")
    model_index = lax.axis_index(MP)
    place = lax.axis_index("dz")
    scal = jnp.stack([place, 1 - 2 * (place % 2), model_index, counts[0]]).astype(jnp.int32)
    white, scale, average, own, *blocks = front(scal, stream[0], value_grad[0], gain)
    weight_grad = sum_over_y(sum_over_z(own, blocks)).astype(BF16)[None]
    tiles = parts(value_grad[0], weights[0], stream[0], gain, scale, average)
    arrived = lax.all_to_all(tiles, MP, split_axis=0, concat_axis=0, tiled=True)
    norm_back, above_grad = backward(scal, arrived, white, scale, gain, top_grad)
    below_grad = lax.ppermute(above_grad, "section", [(1, 0)])
    lower_grad = (below_grad.astype(F32) + norm_back).astype(BF16)
    result = jnp.where(section_index == 0, lower_grad, above_grad)
    return (weight_grad, result[None])


def solution(mesh):
    split = Mesh(
        mesh.devices.reshape(mesh.shape["section"], 2, 4, 12, 4),
        ("section", "my", "mx", "dz", "dy"),
    )
    placed = (
        P("section", DP, MP),
        P("section", DP, None),
        P("section", MP, None),
        P("section", None),
        P(DP, None),
        P(DP),
    )

    return jax.shard_map(
        shards,
        mesh=split,
        in_specs=placed,
        out_specs=(P("section", MP + DP, None), P("section", DP, MP)),
        check_vma=False,
    )
```

time: 129 us -> 117 us (0.907)
  the two profiles are of different devices: /device:TPU:6 before, /device:TPU:2 now
where the time goes in v3:
time: 117 us; the launch traced here: 116 us
  starting transfers between devices  57.3 us (49%)
  waiting for transfers between devices  31.6 us (27%)
  Pallas kernels  19.7 us (17%)
  other arithmetic  3.72 us (3%)
  local copies, waits for them, and re-layouts  1.95 us (2%)
  between operations  1.65 us (1%)
    ppermute x11, starting transfers between devices, swapped(): return lax.ppermute(value, axis, pairs)  44 us
    ppermute x11, waiting for transfers between devices, swapped(): return lax.ppermute(value, axis, pairs)  20.8 us
    all_to_all x1, waiting for transfers between devices, sum_over_y(): lax.all_to_all(tiles, 'dy', split_axis=0, concat_axis=0, tiled=True)  10.8 us
    pallas_call x1, Pallas kernels, front(): pl.pallas_call(front_kernel, grid_spec=pltpu.PrefetchScalarGridSpec(num_s...  10.1 us
    all_to_all x1, starting transfers between devices, shards(): arrived = lax.all_to_all(tiles, MP, split_axis=0, concat_axis=0, tiled=True)  6 us
    all_to_all x1, starting transfers between devices, sum_over_y(): lax.all_to_all(tiles, 'dy', split_axis=0, concat_axis=0, tiled=True)  6 us
    pallas_call x1, Pallas kernels, parts(): pl.pallas_call(parts_kernel, grid=(PARTS,), in_specs=[whole((TOK, SHARE))...  5.62 us
    pallas_call x1, Pallas kernels, backward(): pl.pallas_call(back_kernel, grid_spec=pltpu.PrefetchScalarGridSpec(num_sc...  3.98 us
  transfers between devices with their start and end apart: 14, of which 9 were waited for; matrix products, arithmetic and copies ran while one was open for 2% of the time, Pallas kernels for 8%

profile of v3, /device:TPU:2, one launch (start us, length us, event | category | flops | bytes accessed | tf_op | source)
XLA Modules:
  0.0 115.9 jit_solution(3703167288574105489)
XLA Ops:
  1.3 0.1 pad_add_fusion.scal
  1.4 10.1 %shard_map.77 = (f32[512,384]{1,0:T(8,128)}, f32[512,1]{1,0:T(8,128)}, f32[512,1]{1,0:T(8,128)}, f32[32,3072]{1,0:T(8,128)}, bf16[32,3072]{1,0:T(8,128)(2,1)}, /...) custom-call(s32[4]{0:T(128)S(1)} %pad_add_fusion.scal, ...), custom_call_target="tpu_custom_call" | custom-call | flops 4831838208 | bytes 8000000 | tf_op jit(solution)/shard_map/pallas_call | solution.py:76
  11.5 4.3 %collective-permute-start = (bf16[32,3072]{1,0:T(8,128)(2,1)S(1)}, bf16[32,3072]{1,0:T(8,128)(2,1)S(1)}, u32[]{:S(2)}, u32[]{:S(2)}) collective-permute-start(bf16[32,3072]{1,0:T(8,128)(2,1)S(1)} %get-tuple-element.30), channel_id=1, source_target_pairs={{0,4},{4,0},{8,12},{12,8},{16,20},{20,16},{24,28},{28,24},{32,36},... | collective-permute-start | bytes 589832 | tf_op jit(solution)/shard_map/ppermute | solution.py:211
  15.8 4.9 %collective-permute-done = bf16[32,3072]{1,0:T(8,128)(2,1)S(1)} collective-permute-done((bf16[32,3072]{1,0:T(8,128)(2,1)S(1)}, bf16[32,3072]{1,0:T(8,128)(2,1)S(1)}, u32[]{:S(2)}, u32[]{:S(2)}) %collective-permute-start) | collective-permute-done | bytes 196640 | tf_op jit(solution)/shard_map/ppermute | solution.py:211
  20.7 3.6 %collective-permute-start.6 = (bf16[32,3072]{1,0:T(8,128)(2,1)}, bf16[32,3072]{1,0:T(8,128)(2,1)S(1)}, u32[]{:S(2)}, u32[]{:S(2)}) collective-permute-start(bf16[32,3072]{1,0:T(8,128)(2,1)} %get-tuple-element.36), channel_id=1, source_target_pairs={{0,4},{4,0},{8,12},{12,8},{16,20},{20,16},{24,28},{28,24},{32,36},... | collective-permute-start | bytes 589832 | tf_op jit(solution)/shard_map/ppermute | solution.py:211
  24.3 1.0 add_convert_fusion.10
  25.3 12.8 %collective-permute-start.1 = (bf16[32,3072]{1,0:T(8,128)(2,1)S(1)}, bf16[32,3072]{1,0:T(8,128)(2,1)S(1)}, u32[]{:S(2)}, u32[]{:S(2)}) collective-permute-start(bf16[32,3072]{1,0:T(8,128)(2,1)S(1)} %add_convert_fusion.10), channel_id=1, source_target_pairs={{4,8},{8,4},{12,16},{16,12},{20,24},{24,20},{28,32},{32,28},{36,40... | collective-permute-start | bytes 589832 | tf_op jit(solution)/shard_map/ppermute | solution.py:211
  38.0 0.0 copy-done.1
  38.1 0.0 copy-done.2
  38.1 0.0 copy-done.3
  38.1 0.0 copy-done.4
  38.1 0.0 copy-start
  38.1 0.9 copy-done
  39.0 0.9 copy-done.5
  40.0 5.6 %shard_map.78 = bf16[8,520,384]{2,1,0:T(8,128)(2,1)} custom-call(bf16[512,384]{1,0:T(8,128)(2,1)S(1)} %bitcast.15, bf16[384,3072]{1,0:T(8,128)(2,1)S(1)} %bitcast.13, bf16[512,3072]{1,0:T(8,128)(2,1)S(1)} %bitcast.12, f32[1,3072]{1,0:T(1,128)S(1)} %copy-done.1, f32[512,1]{1,0:T(8,128)S(1)} %copy-done, f32[512,1]{1,0:T(8,128)S(1)} %copy-done.5), custom_call_target="tpu_custom_call" | custom-call | flops 3623878656 | bytes 9000000 | tf_op jit(solution)/shard_map/pallas_call | solution.py:137
  45.6 0.0 copy-start.14
  45.6 0.0 copy-start.13
  45.7 6.0 %all-to-all-start.1 = ((bf16[8,520,384]{2,1,0:T(8,128)(2,1)}), bf16[8,520,384]{2,1,0:T(8,128)(2,1)}, u32[]{:S(2)}, u32[]{:S(2)}) async-start(bf16[8,520,384]{2,1,0:T(8,128)(2,1)} %shard_map.78), calls=%async_computation.1 | async-start | bytes 6389760 | tf_op jit(solution)/shard_map/all_to_all | solution.py:257
  51.7 0.0 collective-permute-done.6
  51.7 0.0 collective-permute-done.1
  51.8 2.1 %collective-permute-start.7 = (bf16[32,3072]{1,0:T(8,128)(2,1)S(1)}, bf16[32,3072]{1,0:T(8,128)(2,1)S(1)}, u32[]{:S(2)}, u32[]{:S(2)}) collective-permute-start(bf16[32,3072]{1,0:T(8,128)(2,1)S(1)} %add_convert_fusion.5), channel_id=1, source_target_pairs={{4,8},{8,4},{12,16},{16,12},{20,24},{24,20},{28,32},{32,28},{36,40... | collective-permute-start | bytes 589832 | tf_op jit(solution)/shard_map/ppermute | solution.py:211
  53.9 1.9 %collective-permute-start.2 = (bf16[32,3072]{1,0:T(8,128)(2,1)S(1)}, bf16[32,3072]{1,0:T(8,128)(2,1)S(1)}, u32[]{:S(2)}, u32[]{:S(2)}) collective-permute-start(bf16[32,3072]{1,0:T(8,128)(2,1)S(1)} %add_convert_fusion.9), channel_id=1, source_target_pairs={{0,4},{4,0},{8,12},{12,8},{16,20},{20,16},{24,28},{28,24},{32,36},... | collective-permute-start | bytes 589832 | tf_op jit(solution)/shard_map/ppermute | solution.py:211
  55.8 4.8 %collective-permute-done.7 = bf16[32,3072]{1,0:T(8,128)(2,1)S(1)} collective-permute-done((bf16[32,3072]{1,0:T(8,128)(2,1)S(1)}, bf16[32,3072]{1,0:T(8,128)(2,1)S(1)}, u32[]{:S(2)}, u32[]{:S(2)}) %collective-permute-start.7) | collective-permute-done | bytes 196640 | tf_op jit(solution)/shard_map/ppermute | solution.py:211
  60.7 0.8 collective-permute-done.2
  61.5 1.9 %collective-permute-start.8 = (bf16[32,3072]{1,0:T(8,128)(2,1)S(1)}, bf16[32,3072]{1,0:T(8,128)(2,1)S(1)}, u32[]{:S(2)}, u32[]{:S(2)}) collective-permute-start(bf16[32,3072]{1,0:T(8,128)(2,1)S(1)} %add_convert_fusion.4), channel_id=1, source_target_pairs={{0,4},{4,0},{8,12},{12,8},{16,20},{20,16},{24,28},{28,24},{32,36},... | collective-permute-start | bytes 589832 | tf_op jit(solution)/shard_map/ppermute | solution.py:211
  63.5 5.4 %collective-permute-start.3 = (bf16[32,3072]{1,0:T(8,128)(2,1)S(1)}, bf16[32,3072]{1,0:T(8,128)(2,1)S(1)}, u32[]{:S(2)}, u32[]{:S(2)}) collective-permute-start(bf16[32,3072]{1,0:T(8,128)(2,1)S(1)} %add_convert_fusion.8), channel_id=1, source_target_pairs={{4,8},{8,4},{12,16},{16,12},{20,24},{24,20},{28,32},{32,28},{36,40... | collective-permute-start | bytes 589832 | tf_op jit(solution)/shard_map/ppermute | solution.py:211
  68.9 0.2 collective-permute-done.8
  69.1 3.4 %collective-permute-done.3 = bf16[32,3072]{1,0:T(8,128)(2,1)S(1)} collective-permute-done((bf16[32,3072]{1,0:T(8,128)(2,1)S(1)}, bf16[32,3072]{1,0:T(8,128)(2,1)S(1)}, u32[]{:S(2)}, u32[]{:S(2)}) %collective-permute-start.3) | collective-permute-done | bytes 196640 | tf_op jit(solution)/shard_map/ppermute | solution.py:211
  72.5 0.0 copy-done.10
  72.6 5.1 %collective-permute-start.9 = (bf16[32,3072]{1,0:T(8,128)(2,1)S(1)}, bf16[32,3072]{1,0:T(8,128)(2,1)S(1)}, u32[]{:S(2)}, u32[]{:S(2)}) collective-permute-start(bf16[32,3072]{1,0:T(8,128)(2,1)S(1)} %add_convert_fusion.3), channel_id=1, source_target_pairs={{4,8},{8,4},{12,16},{16,12},{20,24},{24,20},{28,32},{32,28},{36,40... | collective-permute-start | bytes 589832 | tf_op jit(solution)/shard_map/ppermute | solution.py:211
  77.7 0.0 copy-done.9
  77.8 1.9 %collective-permute-start.4 = (bf16[32,3072]{1,0:T(8,128)(2,1)S(1)}, bf16[32,3072]{1,0:T(8,128)(2,1)S(1)}, u32[]{:S(2)}, u32[]{:S(2)}) collective-permute-start(bf16[32,3072]{1,0:T(8,128)(2,1)S(1)} %add_convert_fusion.7), channel_id=1, source_target_pairs={{0,4},{4,0},{8,12},{12,8},{16,20},{20,16},{24,28},{28,24},{32,36},... | collective-permute-start | bytes 589832 | tf_op jit(solution)/shard_map/ppermute | solution.py:211
  79.7 1.6 %collective-permute-done.9 = bf16[32,3072]{1,0:T(8,128)(2,1)S(1)} collective-permute-done((bf16[32,3072]{1,0:T(8,128)(2,1)S(1)}, bf16[32,3072]{1,0:T(8,128)(2,1)S(1)}, u32[]{:S(2)}, u32[]{:S(2)}) %collective-permute-start.9) | collective-permute-done | bytes 196640 | tf_op jit(solution)/shard_map/ppermute | solution.py:211
  81.3 4.6 %collective-permute-done.4 = bf16[32,3072]{1,0:T(8,128)(2,1)S(1)} collective-permute-done((bf16[32,3072]{1,0:T(8,128)(2,1)S(1)}, bf16[32,3072]{1,0:T(8,128)(2,1)S(1)}, u32[]{:S(2)}, u32[]{:S(2)}) %collective-permute-start.4) | collective-permute-done | bytes 196640 | tf_op jit(solution)/shard_map/ppermute | solution.py:211
  86.1 1.9 %collective-permute-start.10 = (bf16[32,3072]{1,0:T(8,128)(2,1)S(1)}, bf16[32,3072]{1,0:T(8,128)(2,1)S(1)}, u32[]{:S(2)}, u32[]{:S(2)}) collective-permute-start(bf16[32,3072]{1,0:T(8,128)(2,1)S(1)} %add_convert_fusion.2), channel_id=1, source_target_pairs={{0,4},{4,0},{8,12},{12,8},{16,20},{20,16},{24,28},{28,24},{32,36},... | collective-permute-start | bytes 589832 | tf_op jit(solution)/shard_map/ppermute | solution.py:211
  88.0 3.1 %collective-permute-start.5 = (bf16[32,3072]{1,0:T(8,128)(2,1)S(1)}, bf16[32,3072]{1,0:T(8,128)(2,1)S(1)}, u32[]{:S(2)}, u32[]{:S(2)}) collective-permute-start(bf16[32,3072]{1,0:T(8,128)(2,1)S(1)} %add_convert_fusion.6), channel_id=1, source_target_pairs={{4,8},{8,4},{12,16},{16,12},{20,24},{24,20},{28,32},{32,28},{36,40... | collective-permute-start | bytes 589832 | tf_op jit(solution)/shard_map/ppermute | solution.py:211
  91.2 0.0 all-to-all-done.1.arrived.extra
  91.2 0.0 copy-start.6
  91.2 4.0 %shard_map.79 = (f32[512,384]{1,0:T(8,128)S(1)}, bf16[512,384]{1,0:T(8,128)(2,1)S(1)}) custom-call(s32[4]{0:T(128)S(1)} %pad_add_fusion.scal, bf16[8,520,384]{2,1,0:T(8,128)(2,1)} %all-to-all-done.1.arrived.extra, bf16[8,520,384]{2,1,0:T(8,128)(2,1)} %all-to-all-done.1.arrived.extra, f32[512,384]{1,0:T(8,128)} %get-tuple-element.43.white, ...), custom_call_target="tpu_custom_call" | custom-call | flops 500000000 | bytes 6000000 | tf_op jit(solution)/shard_map/pallas_call | solution.py:182
  95.2 1.3 %collective-permute-start.11 = (bf16[512,384]{1,0:T(8,128)(2,1)S(1)}, bf16[512,384]{1,0:T(8,128)(2,1)S(1)}, u32[]{:S(2)}, u32[]{:S(2)}) collective-permute-start(bf16[512,384]{1,0:T(8,128)(2,1)S(1)} %get-tuple-element.44), channel_id=1, source_target_pairs={{384,0},{385,1},{386,2},{387,3},{388,4},{389,5},{390,6},{391,7},{3... | collective-permute-start | bytes 1179656 | tf_op jit(solution)/shard_map/ppermute | solution.py:259
  96.5 0.0 collective-permute-done.10
  96.5 0.3 collective-permute-done.5
  96.8 0.7 fusion.2
  97.6 6.0 %all-to-all-start = ((bf16[4,8,3072]{2,1,0:T(8,128)(2,1)}), bf16[4,8,3072]{2,1,0:T(8,128)(2,1)S(1)}, u32[]{:S(2)}, u32[]{:S(2)}) async-start(bf16[4,8,3072]{2,1,0:T(8,128)(2,1)} %fusion.2), calls=%async_computation | async-start | bytes 393216 | tf_op jit(solution)/shard_map/all_to_all | solution.py:245
  103.6 10.8 %all-to-all-done = bf16[4,8,3072]{2,1,0:T(8,128)(2,1)S(1)} async-done(((bf16[4,8,3072]{2,1,0:T(8,128)(2,1)}), bf16[4,8,3072]{2,1,0:T(8,128)(2,1)S(1)}, u32[]{:S(2)}, u32[]{:S(2)}) %all-to-all-start) | async-done | bytes 196640 | tf_op jit(solution)/shard_map/all_to_all | solution.py:245
  114.4 0.7 reduce_sum.12
  115.0 0.0 collective-permute-done.11
  115.0 0.9 fusion.1
  (26 shorter events, 0.4 us)
Async XLA Ops:
  1.4 36.7 %copy-start.1 = (f32[1,3072]{1,0:T(1,128)S(1)}, f32[1,3072]{1,0:T(1,128)}, u32[]{:S(2)}) copy-start(f32[1,3072]{1,0:T(1,128)} %gain.5) | copy-start | bytes 36868
  1.4 36.7 %copy-start.2 = (bf16[1,512,3072]{2,1,0:T(8,128)(2,1)S(1)}, bf16[1,512,3072]{2,1,0:T(8,128)(2,1)}, u32[]{:S(2)}) copy-start(bf16[1,512,3072]{2,1,0:T(8,128)(2,1)} %param.7) | copy-start | bytes 9437188
  1.4 36.7 %copy-start.3 = (bf16[1,384,3072]{2,1,0:T(8,128)(2,1)S(1)}, bf16[1,384,3072]{2,1,0:T(8,128)(2,1)}, u32[]{:S(2)}) copy-start(bf16[1,384,3072]{2,1,0:T(8,128)(2,1)} %param.8) | copy-start | bytes 7077892
  1.4 36.7 %copy-start.4 = (bf16[1,512,384]{2,1,0:T(8,128)(2,1)S(1)}, bf16[1,512,384]{2,1,0:T(8,128)(2,1)}, u32[]{:S(2)}) copy-start(bf16[1,512,384]{2,1,0:T(8,128)(2,1)} %param.6) | copy-start | bytes 1179652
  11.5 9.2 %collective-permute-start = (bf16[32,3072]{1,0:T(8,128)(2,1)S(1)}, bf16[32,3072]{1,0:T(8,128)(2,1)S(1)}, u32[]{:S(2)}, u32[]{:S(2)}) collective-permute-start(bf16[32,3072]{1,0:T(8,128)(2,1)S(1)} %get-tuple-element.30), channel_id=1, source_target_pairs={{0,4},{4,0},{8,12},{12,8},{16,20},{20,16},{24,28},{28,24},{32,36},... | collective-permute-start | bytes 589832 | tf_op jit(solution)/shard_map/ppermute | solution.py:211
  20.7 31.0 %collective-permute-start.6 = (bf16[32,3072]{1,0:T(8,128)(2,1)}, bf16[32,3072]{1,0:T(8,128)(2,1)S(1)}, u32[]{:S(2)}, u32[]{:S(2)}) collective-permute-start(bf16[32,3072]{1,0:T(8,128)(2,1)} %get-tuple-element.36), channel_id=1, source_target_pairs={{0,4},{4,0},{8,12},{12,8},{16,20},{20,16},{24,28},{28,24},{32,36},... | collective-permute-start | bytes 589832 | tf_op jit(solution)/shard_map/ppermute | solution.py:211
  25.3 26.4 %collective-permute-start.1 = (bf16[32,3072]{1,0:T(8,128)(2,1)S(1)}, bf16[32,3072]{1,0:T(8,128)(2,1)S(1)}, u32[]{:S(2)}, u32[]{:S(2)}) collective-permute-start(bf16[32,3072]{1,0:T(8,128)(2,1)S(1)} %add_convert_fusion.10), channel_id=1, source_target_pairs={{4,8},{8,4},{12,16},{16,12},{20,24},{24,20},{28,32},{32,28},{36,40... | collective-permute-start | bytes 589832 | tf_op jit(solution)/shard_map/ppermute | solution.py:211
  38.1 1.0 copy-start
  39.0 0.9 copy-start.5
  45.6 6.1 %copy-start.14 = (bf16[32,3072]{1,0:T(8,128)(2,1)S(1)}, bf16[32,3072]{1,0:T(8,128)(2,1)}, u32[]{:S(2)}) copy-start(bf16[32,3072]{1,0:T(8,128)(2,1)} %get-tuple-element.34) | copy-start | bytes 589828
  45.6 8.2 %copy-start.13 = (bf16[32,3072]{1,0:T(8,128)(2,1)S(1)}, bf16[32,3072]{1,0:T(8,128)(2,1)}, u32[]{:S(2)}) copy-start(bf16[32,3072]{1,0:T(8,128)(2,1)} %get-tuple-element.28) | copy-start | bytes 589828
  45.6 15.8 %copy-start.12 = (bf16[32,3072]{1,0:T(8,128)(2,1)S(1)}, bf16[32,3072]{1,0:T(8,128)(2,1)}, u32[]{:S(2)}) copy-start(bf16[32,3072]{1,0:T(8,128)(2,1)} %get-tuple-element.33) | copy-start | bytes 589828
  45.6 17.8 %copy-start.11 = (bf16[32,3072]{1,0:T(8,128)(2,1)S(1)}, bf16[32,3072]{1,0:T(8,128)(2,1)}, u32[]{:S(2)}) copy-start(bf16[32,3072]{1,0:T(8,128)(2,1)} %get-tuple-element.27) | copy-start | bytes 589828
  45.7 26.9 %copy-start.10 = (bf16[32,3072]{1,0:T(8,128)(2,1)S(1)}, bf16[32,3072]{1,0:T(8,128)(2,1)}, u32[]{:S(2)}) copy-start(bf16[32,3072]{1,0:T(8,128)(2,1)} %get-tuple-element.32) | copy-start | bytes 589828
  45.7 32.0 %copy-start.9 = (bf16[32,3072]{1,0:T(8,128)(2,1)S(1)}, bf16[32,3072]{1,0:T(8,128)(2,1)}, u32[]{:S(2)}) copy-start(bf16[32,3072]{1,0:T(8,128)(2,1)} %get-tuple-element.26) | copy-start | bytes 589828
  45.7 45.5 %all-to-all-start.1 = ((bf16[8,520,384]{2,1,0:T(8,128)(2,1)}), bf16[8,520,384]{2,1,0:T(8,128)(2,1)}, u32[]{:S(2)}, u32[]{:S(2)}) async-start(bf16[8,520,384]{2,1,0:T(8,128)(2,1)} %shard_map.78), calls=%async_computation.1 | async-start | bytes 6389760 | tf_op jit(solution)/shard_map/all_to_all | solution.py:257
  51.7 34.3 %copy-start.8 = (bf16[32,3072]{1,0:T(8,128)(2,1)S(1)}, bf16[32,3072]{1,0:T(8,128)(2,1)}, u32[]{:S(2)}) copy-start(bf16[32,3072]{1,0:T(8,128)(2,1)} %get-tuple-element.31) | copy-start | bytes 589828
  51.7 36.3 %copy-start.7 = (bf16[32,3072]{1,0:T(8,128)(2,1)S(1)}, bf16[32,3072]{1,0:T(8,128)(2,1)}, u32[]{:S(2)}) copy-start(bf16[32,3072]{1,0:T(8,128)(2,1)} %get-tuple-element.25) | copy-start | bytes 589828
  51.8 8.9 %collective-permute-start.7 = (bf16[32,3072]{1,0:T(8,128)(2,1)S(1)}, bf16[32,3072]{1,0:T(8,128)(2,1)S(1)}, u32[]{:S(2)}, u32[]{:S(2)}) collective-permute-start(bf16[32,3072]{1,0:T(8,128)(2,1)S(1)} %add_convert_fusion.5), channel_id=1, source_target_pairs={{4,8},{8,4},{12,16},{16,12},{20,24},{24,20},{28,32},{32,28},{36,40... | collective-permute-start | bytes 589832 | tf_op jit(solution)/shard_map/ppermute | solution.py:211
  53.9 7.6 %collective-permute-start.2 = (bf16[32,3072]{1,0:T(8,128)(2,1)S(1)}, bf16[32,3072]{1,0:T(8,128)(2,1)S(1)}, u32[]{:S(2)}, u32[]{:S(2)}) collective-permute-start(bf16[32,3072]{1,0:T(8,128)(2,1)S(1)} %add_convert_fusion.9), channel_id=1, source_target_pairs={{0,4},{4,0},{8,12},{12,8},{16,20},{20,16},{24,28},{28,24},{32,36},... | collective-permute-start | bytes 589832 | tf_op jit(solution)/shard_map/ppermute | solution.py:211
  61.5 7.6 %collective-permute-start.8 = (bf16[32,3072]{1,0:T(8,128)(2,1)S(1)}, bf16[32,3072]{1,0:T(8,128)(2,1)S(1)}, u32[]{:S(2)}, u32[]{:S(2)}) collective-permute-start(bf16[32,3072]{1,0:T(8,128)(2,1)S(1)} %add_convert_fusion.4), channel_id=1, source_target_pairs={{0,4},{4,0},{8,12},{12,8},{16,20},{20,16},{24,28},{28,24},{32,36},... | collective-permute-start | bytes 589832 | tf_op jit(solution)/shard_map/ppermute | solution.py:211
  63.5 9.0 %collective-permute-start.3 = (bf16[32,3072]{1,0:T(8,128)(2,1)S(1)}, bf16[32,3072]{1,0:T(8,128)(2,1)S(1)}, u32[]{:S(2)}, u32[]{:S(2)}) collective-permute-start(bf16[32,3072]{1,0:T(8,128)(2,1)S(1)} %add_convert_fusion.8), channel_id=1, source_target_pairs={{4,8},{8,4},{12,16},{16,12},{20,24},{24,20},{28,32},{32,28},{36,40... | collective-permute-start | bytes 589832 | tf_op jit(solution)/shard_map/ppermute | solution.py:211
  72.6 8.8 %collective-permute-start.9 = (bf16[32,3072]{1,0:T(8,128)(2,1)S(1)}, bf16[32,3072]{1,0:T(8,128)(2,1)S(1)}, u32[]{:S(2)}, u32[]{:S(2)}) collective-permute-start(bf16[32,3072]{1,0:T(8,128)(2,1)S(1)} %add_convert_fusion.3), channel_id=1, source_target_pairs={{4,8},{8,4},{12,16},{16,12},{20,24},{24,20},{28,32},{32,28},{36,40... | collective-permute-start | bytes 589832 | tf_op jit(solution)/shard_map/ppermute | solution.py:211
  77.8 8.2 %collective-permute-start.4 = (bf16[32,3072]{1,0:T(8,128)(2,1)S(1)}, bf16[32,3072]{1,0:T(8,128)(2,1)S(1)}, u32[]{:S(2)}, u32[]{:S(2)}) collective-permute-start(bf16[32,3072]{1,0:T(8,128)(2,1)S(1)} %add_convert_fusion.7), channel_id=1, source_target_pairs={{0,4},{4,0},{8,12},{12,8},{16,20},{20,16},{24,28},{28,24},{32,36},... | collective-permute-start | bytes 589832 | tf_op jit(solution)/shard_map/ppermute | solution.py:211
  86.1 10.4 %collective-permute-start.10 = (bf16[32,3072]{1,0:T(8,128)(2,1)S(1)}, bf16[32,3072]{1,0:T(8,128)(2,1)S(1)}, u32[]{:S(2)}, u32[]{:S(2)}) collective-permute-start(bf16[32,3072]{1,0:T(8,128)(2,1)S(1)} %add_convert_fusion.2), channel_id=1, source_target_pairs={{0,4},{4,0},{8,12},{12,8},{16,20},{20,16},{24,28},{28,24},{32,36},... | collective-permute-start | bytes 589832 | tf_op jit(solution)/shard_map/ppermute | solution.py:211
  88.0 8.8 %collective-permute-start.5 = (bf16[32,3072]{1,0:T(8,128)(2,1)S(1)}, bf16[32,3072]{1,0:T(8,128)(2,1)S(1)}, u32[]{:S(2)}, u32[]{:S(2)}) collective-permute-start(bf16[32,3072]{1,0:T(8,128)(2,1)S(1)} %add_convert_fusion.6), channel_id=1, source_target_pairs={{4,8},{8,4},{12,16},{16,12},{20,24},{24,20},{28,32},{32,28},{36,40... | collective-permute-start | bytes 589832 | tf_op jit(solution)/shard_map/ppermute | solution.py:211
  91.2 5.7 %copy-start.6 = (f32[32,3072]{1,0:T(8,128)S(1)}, f32[32,3072]{1,0:T(8,128)}, u32[]{:S(2)}) copy-start(f32[32,3072]{1,0:T(8,128)} %get-tuple-element.24) | copy-start | bytes 1179652
  95.2 19.9 %collective-permute-start.11 = (bf16[512,384]{1,0:T(8,128)(2,1)S(1)}, bf16[512,384]{1,0:T(8,128)(2,1)S(1)}, u32[]{:S(2)}, u32[]{:S(2)}) collective-permute-start(bf16[512,384]{1,0:T(8,128)(2,1)S(1)} %get-tuple-element.44), channel_id=1, source_target_pairs={{384,0},{385,1},{386,2},{387,3},{388,4},{389,5},{390,6},{391,7},{3... | collective-permute-start | bytes 1179656 | tf_op jit(solution)/shard_map/ppermute | solution.py:259
  97.6 16.8 %all-to-all-start = ((bf16[4,8,3072]{2,1,0:T(8,128)(2,1)}), bf16[4,8,3072]{2,1,0:T(8,128)(2,1)S(1)}, u32[]{:S(2)}, u32[]{:S(2)}) async-start(bf16[4,8,3072]{2,1,0:T(8,128)(2,1)} %fusion.2), calls=%async_computation | async-start | bytes 393216 | tf_op jit(solution)/shard_map/all_to_all | solution.py:245

commit v4 on v3

--- a/solution.py
+++ b/solution.py
@@ -203,12 +203,14 @@
     )(scal, *in_hbm(arrived, arrived, white, scale, gain, top))
 
 
-def swapped(value, axis, first):
-    peers = lax.axis_size(axis)
+def swapped(value, link):
+    peers = lax.axis_size("dz")
     pairs = []
-    for i in range(first, peers, 2):
-        pairs += [(i, (i + 1) % peers), ((i + 1) % peers, i)]
-    return lax.ppermute(value, axis, pairs)
+    for section in range(2):
+        for i in range((link + section) % 2, peers, 2):
+            here, there = section * peers + i, section * peers + (i + 1) % peers
+            pairs += [(here, there), (there, here)]
+    return lax.ppermute(value, ("section", "dz"), pairs)
 
 
 def tied(value, *others):
@@ -224,7 +226,7 @@
         return blocks[(distance if link == 0 else RING - distance) - 1]
 
     far = RING // 2
-    long = swapped(block(0, far), "dz", 0)
+    long = swapped(block(0, far), 0)
     short = None
     link = 0
     for k in range(far - 1, 0, -1):
@@ -234,8 +236,8 @@
         else:
             mine_short = joined(block(1 - link, k), tied(short, long))
         mine = joined(block(link, k), long)
-        long = swapped(mine, "dz", link)
-        short = swapped(mine_short, "dz", 1 - link)
+        long = swapped(mine, link)
+        short = swapped(mine_short, 1 - link)
     return own + long.astype(F32) + short.astype(F32)
 
 
@@ -250,7 +252,7 @@
     section_index = lax.axis_index("section")
     model_index = lax.axis_index(MP)
     place = lax.axis_index("dz")
-    scal = jnp.stack([place, 1 - 2 * (place % 2), model_index, counts[0]]).astype(jnp.int32)
+    scal = jnp.stack([place, 1 - 2 * ((place + section_index) % 2), model_index, counts[0]]).astype(jnp.int32)
     white, scale, average, own, *blocks = front(scal, stream[0], value_grad[0], gain)
     weight_grad = sum_over_y(sum_over_z(own, blocks)).astype(BF16)[None]
     tiles = parts(value_grad[0], weights[0], stream[0], gain, scale, average)

time: 117 us -> 115 us (0.983)
  waiting for transfers between devices: 31.6 us -> 30.2 us
    ppermute x11, waiting for transfers between devices: 20.8 us -> 19.4 us  [swapped(): return lax.ppermute(value, ('section', 'dz'), pairs)]
  transfers between devices with their start and end apart: 14 -> 14, of which waited for: 9 -> 8; matrix products, arithmetic and copies ran while one was open for 2% -> 2% of each run, Pallas kernels for 8% -> 8%
where the time goes in v4:
time: 115 us; the launch traced here: 114 us
  starting transfers between devices  57.3 us (50%)
  waiting for transfers between devices  30.2 us (26%)
  Pallas kernels  19.7 us (17%)
  other arithmetic  3.72 us (3%)
  local copies, waits for them, and re-layouts  1.95 us (2%)
  between operations  1.65 us (1%)
    ppermute x11, starting transfers between devices, swapped(): return lax.ppermute(value, ('section', 'dz'), pairs)  43.8 us
    ppermute x11, waiting for transfers between devices, swapped(): return lax.ppermute(value, ('section', 'dz'), pairs)  19.4 us
    all_to_all x1, waiting for transfers between devices, sum_over_y(): lax.all_to_all(tiles, 'dy', split_axis=0, concat_axis=0, tiled=True)  10.8 us
    pallas_call x1, Pallas kernels, front(): pl.pallas_call(front_kernel, grid_spec=pltpu.PrefetchScalarGridSpec(num_s...  10.1 us
    all_to_all x1, starting transfers between devices, sum_over_y(): lax.all_to_all(tiles, 'dy', split_axis=0, concat_axis=0, tiled=True)  6.18 us
    all_to_all x1, starting transfers between devices, shards(): arrived = lax.all_to_all(tiles, MP, split_axis=0, concat_axis=0, tiled=True)  6 us
    pallas_call x1, Pallas kernels, parts(): pl.pallas_call(parts_kernel, grid=(PARTS,), in_specs=[whole((TOK, SHARE))...  5.62 us
    pallas_call x1, Pallas kernels, backward(): pl.pallas_call(back_kernel, grid_spec=pltpu.PrefetchScalarGridSpec(num_sc...  3.98 us
  transfers between devices with their start and end apart: 14, of which 8 were waited for; matrix products, arithmetic and copies ran while one was open for 2% of the time, Pallas kernels for 8%

profile of v4, /device:TPU:2, one launch (start us, length us, event | category | flops | bytes accessed | tf_op | source)
XLA Modules:
  0.0 114.5 jit_solution(9139800777838741152)
XLA Ops:
  1.3 0.1 pad_add_fusion.scal
  1.4 10.1 %shard_map.77 = (f32[512,384]{1,0:T(8,128)}, f32[512,1]{1,0:T(8,128)}, f32[512,1]{1,0:T(8,128)}, f32[32,3072]{1,0:T(8,128)}, bf16[32,3072]{1,0:T(8,128)(2,1)}, /...) custom-call(s32[4]{0:T(128)S(1)} %pad_add_fusion.scal, ...), custom_call_target="tpu_custom_call" | custom-call | flops 4831838208 | bytes 8000000 | tf_op jit(solution)/shard_map/pallas_call | solution.py:76
  11.5 4.3 %collective-permute-start = (bf16[32,3072]{1,0:T(8,128)(2,1)S(1)}, bf16[32,3072]{1,0:T(8,128)(2,1)S(1)}, u32[]{:S(2)}, u32[]{:S(2)}) collective-permute-start(bf16[32,3072]{1,0:T(8,128)(2,1)S(1)} %get-tuple-element.30), channel_id=1, source_target_pairs={{0,4},{4,0},{8,12},{12,8},{16,20},{20,16},{24,28},{28,24},{32,36},... | collective-permute-start | bytes 589832 | tf_op jit(solution)/shard_map/ppermute | solution.py:213
  15.8 3.6 %collective-permute-done = bf16[32,3072]{1,0:T(8,128)(2,1)S(1)} collective-permute-done((bf16[32,3072]{1,0:T(8,128)(2,1)S(1)}, bf16[32,3072]{1,0:T(8,128)(2,1)S(1)}, u32[]{:S(2)}, u32[]{:S(2)}) %collective-permute-start) | collective-permute-done | bytes 196640 | tf_op jit(solution)/shard_map/ppermute | solution.py:213
  19.4 3.9 %collective-permute-start.6 = (bf16[32,3072]{1,0:T(8,128)(2,1)}, bf16[32,3072]{1,0:T(8,128)(2,1)S(1)}, u32[]{:S(2)}, u32[]{:S(2)}) collective-permute-start(bf16[32,3072]{1,0:T(8,128)(2,1)} %get-tuple-element.36), channel_id=1, source_target_pairs={{0,4},{4,0},{8,12},{12,8},{16,20},{20,16},{24,28},{28,24},{32,36},... | collective-permute-start | bytes 589832 | tf_op jit(solution)/shard_map/ppermute | solution.py:213
  23.3 1.0 add_convert_fusion.10
  24.3 12.8 %collective-permute-start.1 = (bf16[32,3072]{1,0:T(8,128)(2,1)S(1)}, bf16[32,3072]{1,0:T(8,128)(2,1)S(1)}, u32[]{:S(2)}, u32[]{:S(2)}) collective-permute-start(bf16[32,3072]{1,0:T(8,128)(2,1)S(1)} %add_convert_fusion.10), channel_id=1, source_target_pairs={{4,8},{8,4},{12,16},{16,12},{20,24},{24,20},{28,32},{32,28},{36,40... | collective-permute-start | bytes 589832 | tf_op jit(solution)/shard_map/ppermute | solution.py:213
  37.1 0.0 copy-done.1
  37.1 0.0 copy-done.2
  37.1 0.0 copy-done.3
  37.1 0.0 copy-done.4
  37.1 0.0 copy-start
  37.1 0.9 copy-done
  38.1 0.9 copy-done.5
  39.0 5.6 %shard_map.78 = bf16[8,520,384]{2,1,0:T(8,128)(2,1)} custom-call(bf16[512,384]{1,0:T(8,128)(2,1)S(1)} %bitcast.15, bf16[384,3072]{1,0:T(8,128)(2,1)S(1)} %bitcast.13, bf16[512,3072]{1,0:T(8,128)(2,1)S(1)} %bitcast.12, f32[1,3072]{1,0:T(1,128)S(1)} %copy-done.1, f32[512,1]{1,0:T(8,128)S(1)} %copy-done, f32[512,1]{1,0:T(8,128)S(1)} %copy-done.5), custom_call_target="tpu_custom_call" | custom-call | flops 3623878656 | bytes 9000000 | tf_op jit(solution)/shard_map/pallas_call | solution.py:137
  44.7 6.0 %all-to-all-start.1 = ((bf16[8,520,384]{2,1,0:T(8,128)(2,1)}), bf16[8,520,384]{2,1,0:T(8,128)(2,1)}, u32[]{:S(2)}, u32[]{:S(2)}) async-start(bf16[8,520,384]{2,1,0:T(8,128)(2,1)} %shard_map.78), calls=%async_computation.1 | async-start | bytes 6389760 | tf_op jit(solution)/shard_map/all_to_all | solution.py:259
  50.7 0.0 collective-permute-done.6
  50.7 0.0 collective-permute-done.1
  50.7 0.0 copy-done.14
  50.8 2.1 %collective-permute-start.7 = (bf16[32,3072]{1,0:T(8,128)(2,1)S(1)}, bf16[32,3072]{1,0:T(8,128)(2,1)S(1)}, u32[]{:S(2)}, u32[]{:S(2)}) collective-permute-start(bf16[32,3072]{1,0:T(8,128)(2,1)S(1)} %add_convert_fusion.5), channel_id=1, source_target_pairs={{4,8},{8,4},{12,16},{16,12},{20,24},{24,20},{28,32},{32,28},{36,40... | collective-permute-start | bytes 589832 | tf_op jit(solution)/shard_map/ppermute | solution.py:213
  52.9 1.9 %collective-permute-start.2 = (bf16[32,3072]{1,0:T(8,128)(2,1)S(1)}, bf16[32,3072]{1,0:T(8,128)(2,1)S(1)}, u32[]{:S(2)}, u32[]{:S(2)}) collective-permute-start(bf16[32,3072]{1,0:T(8,128)(2,1)S(1)} %add_convert_fusion.9), channel_id=1, source_target_pairs={{0,4},{4,0},{8,12},{12,8},{16,20},{20,16},{24,28},{28,24},{32,36},... | collective-permute-start | bytes 589832 | tf_op jit(solution)/shard_map/ppermute | solution.py:213
  54.8 6.0 %collective-permute-done.7 = bf16[32,3072]{1,0:T(8,128)(2,1)S(1)} collective-permute-done((bf16[32,3072]{1,0:T(8,128)(2,1)S(1)}, bf16[32,3072]{1,0:T(8,128)(2,1)S(1)}, u32[]{:S(2)}, u32[]{:S(2)}) %collective-permute-start.7) | collective-permute-done | bytes 196640 | tf_op jit(solution)/shard_map/ppermute | solution.py:213
  60.8 0.0 collective-permute-done.2
  60.9 1.9 %collective-permute-start.8 = (bf16[32,3072]{1,0:T(8,128)(2,1)S(1)}, bf16[32,3072]{1,0:T(8,128)(2,1)S(1)}, u32[]{:S(2)}, u32[]{:S(2)}) collective-permute-start(bf16[32,3072]{1,0:T(8,128)(2,1)S(1)} %add_convert_fusion.4), channel_id=1, source_target_pairs={{0,4},{4,0},{8,12},{12,8},{16,20},{20,16},{24,28},{28,24},{32,36},... | collective-permute-start | bytes 589832 | tf_op jit(solution)/shard_map/ppermute | solution.py:213
  62.8 0.0 copy-done.11
  62.9 5.1 %collective-permute-start.3 = (bf16[32,3072]{1,0:T(8,128)(2,1)S(1)}, bf16[32,3072]{1,0:T(8,128)(2,1)S(1)}, u32[]{:S(2)}, u32[]{:S(2)}) collective-permute-start(bf16[32,3072]{1,0:T(8,128)(2,1)S(1)} %add_convert_fusion.8), channel_id=1, source_target_pairs={{4,8},{8,4},{12,16},{16,12},{20,24},{24,20},{28,32},{32,28},{36,40... | collective-permute-start | bytes 589832 | tf_op jit(solution)/shard_map/ppermute | solution.py:213
  67.9 0.5 collective-permute-done.8
  68.4 3.4 %collective-permute-done.3 = bf16[32,3072]{1,0:T(8,128)(2,1)S(1)} collective-permute-done((bf16[32,3072]{1,0:T(8,128)(2,1)S(1)}, bf16[32,3072]{1,0:T(8,128)(2,1)S(1)}, u32[]{:S(2)}, u32[]{:S(2)}) %collective-permute-start.3) | collective-permute-done | bytes 196640 | tf_op jit(solution)/shard_map/ppermute | solution.py:213
  71.8 0.0 copy-done.10
  71.9 4.9 %collective-permute-start.9 = (bf16[32,3072]{1,0:T(8,128)(2,1)S(1)}, bf16[32,3072]{1,0:T(8,128)(2,1)S(1)}, u32[]{:S(2)}, u32[]{:S(2)}) collective-permute-start(bf16[32,3072]{1,0:T(8,128)(2,1)S(1)} %add_convert_fusion.3), channel_id=1, source_target_pairs={{4,8},{8,4},{12,16},{16,12},{20,24},{24,20},{28,32},{32,28},{36,40... | collective-permute-start | bytes 589832 | tf_op jit(solution)/shard_map/ppermute | solution.py:213
  76.8 0.0 copy-done.9
  76.8 1.9 %collective-permute-start.4 = (bf16[32,3072]{1,0:T(8,128)(2,1)S(1)}, bf16[32,3072]{1,0:T(8,128)(2,1)S(1)}, u32[]{:S(2)}, u32[]{:S(2)}) collective-permute-start(bf16[32,3072]{1,0:T(8,128)(2,1)S(1)} %add_convert_fusion.7), channel_id=1, source_target_pairs={{0,4},{4,0},{8,12},{12,8},{16,20},{20,16},{24,28},{28,24},{32,36},... | collective-permute-start | bytes 589832 | tf_op jit(solution)/shard_map/ppermute | solution.py:213
  78.8 4.0 %collective-permute-done.9 = bf16[32,3072]{1,0:T(8,128)(2,1)S(1)} collective-permute-done((bf16[32,3072]{1,0:T(8,128)(2,1)S(1)}, bf16[32,3072]{1,0:T(8,128)(2,1)S(1)}, u32[]{:S(2)}, u32[]{:S(2)}) %collective-permute-start.9) | collective-permute-done | bytes 196640 | tf_op jit(solution)/shard_map/ppermute | solution.py:213
  82.7 1.7 %collective-permute-done.4 = bf16[32,3072]{1,0:T(8,128)(2,1)S(1)} collective-permute-done((bf16[32,3072]{1,0:T(8,128)(2,1)S(1)}, bf16[32,3072]{1,0:T(8,128)(2,1)S(1)}, u32[]{:S(2)}, u32[]{:S(2)}) %collective-permute-start.4) | collective-permute-done | bytes 196640 | tf_op jit(solution)/shard_map/ppermute | solution.py:213
  84.5 1.9 %collective-permute-start.10 = (bf16[32,3072]{1,0:T(8,128)(2,1)S(1)}, bf16[32,3072]{1,0:T(8,128)(2,1)S(1)}, u32[]{:S(2)}, u32[]{:S(2)}) collective-permute-start(bf16[32,3072]{1,0:T(8,128)(2,1)S(1)} %add_convert_fusion.2), channel_id=1, source_target_pairs={{0,4},{4,0},{8,12},{12,8},{16,20},{20,16},{24,28},{28,24},{32,36},... | collective-permute-start | bytes 589832 | tf_op jit(solution)/shard_map/ppermute | solution.py:213
  86.4 3.1 %collective-permute-start.5 = (bf16[32,3072]{1,0:T(8,128)(2,1)S(1)}, bf16[32,3072]{1,0:T(8,128)(2,1)S(1)}, u32[]{:S(2)}, u32[]{:S(2)}) collective-permute-start(bf16[32,3072]{1,0:T(8,128)(2,1)S(1)} %add_convert_fusion.6), channel_id=1, source_target_pairs={{4,8},{8,4},{12,16},{16,12},{20,24},{24,20},{28,32},{32,28},{36,40... | collective-permute-start | bytes 589832 | tf_op jit(solution)/shard_map/ppermute | solution.py:213
  89.6 0.0 all-to-all-done.1.arrived.extra
  89.6 0.0 copy-start.6
  89.6 4.0 %shard_map.79 = (f32[512,384]{1,0:T(8,128)S(1)}, bf16[512,384]{1,0:T(8,128)(2,1)S(1)}) custom-call(s32[4]{0:T(128)S(1)} %pad_add_fusion.scal, bf16[8,520,384]{2,1,0:T(8,128)(2,1)} %all-to-all-done.1.arrived.extra, bf16[8,520,384]{2,1,0:T(8,128)(2,1)} %all-to-all-done.1.arrived.extra, f32[512,384]{1,0:T(8,128)} %get-tuple-element.43.white, ...), custom_call_target="tpu_custom_call" | custom-call | flops 500000000 | bytes 6000000 | tf_op jit(solution)/shard_map/pallas_call | solution.py:182
  93.6 1.3 %collective-permute-start.11 = (bf16[512,384]{1,0:T(8,128)(2,1)S(1)}, bf16[512,384]{1,0:T(8,128)(2,1)S(1)}, u32[]{:S(2)}, u32[]{:S(2)}) collective-permute-start(bf16[512,384]{1,0:T(8,128)(2,1)S(1)} %get-tuple-element.44), channel_id=1, source_target_pairs={{384,0},{385,1},{386,2},{387,3},{388,4},{389,5},{390,6},{391,7},{3... | collective-permute-start | bytes 1179656 | tf_op jit(solution)/shard_map/ppermute | solution.py:261
  94.9 0.0 collective-permute-done.10
  94.9 0.3 collective-permute-done.5
  95.2 0.7 fusion.2
  96.0 6.2 %all-to-all-start = ((bf16[4,8,3072]{2,1,0:T(8,128)(2,1)}), bf16[4,8,3072]{2,1,0:T(8,128)(2,1)S(1)}, u32[]{:S(2)}, u32[]{:S(2)}) async-start(bf16[4,8,3072]{2,1,0:T(8,128)(2,1)} %fusion.2), calls=%async_computation | async-start | bytes 393216 | tf_op jit(solution)/shard_map/all_to_all | solution.py:247
  102.2 10.8 %all-to-all-done = bf16[4,8,3072]{2,1,0:T(8,128)(2,1)S(1)} async-done(((bf16[4,8,3072]{2,1,0:T(8,128)(2,1)}), bf16[4,8,3072]{2,1,0:T(8,128)(2,1)S(1)}, u32[]{:S(2)}, u32[]{:S(2)}) %all-to-all-start) | async-done | bytes 196640 | tf_op jit(solution)/shard_map/all_to_all | solution.py:247
  112.9 0.7 reduce_sum.12
  113.6 0.0 collective-permute-done.11
  113.6 0.9 fusion.1
  (26 shorter events, 0.4 us)
Async XLA Ops:
  1.4 35.7 %copy-start.1 = (f32[1,3072]{1,0:T(1,128)S(1)}, f32[1,3072]{1,0:T(1,128)}, u32[]{:S(2)}) copy-start(f32[1,3072]{1,0:T(1,128)} %gain.5) | copy-start | bytes 36868
  1.4 35.7 %copy-start.2 = (bf16[1,512,3072]{2,1,0:T(8,128)(2,1)S(1)}, bf16[1,512,3072]{2,1,0:T(8,128)(2,1)}, u32[]{:S(2)}) copy-start(bf16[1,512,3072]{2,1,0:T(8,128)(2,1)} %param.7) | copy-start | bytes 9437188
  1.4 35.7 %copy-start.3 = (bf16[1,384,3072]{2,1,0:T(8,128)(2,1)S(1)}, bf16[1,384,3072]{2,1,0:T(8,128)(2,1)}, u32[]{:S(2)}) copy-start(bf16[1,384,3072]{2,1,0:T(8,128)(2,1)} %param.8) | copy-start | bytes 7077892
  1.4 35.7 %copy-start.4 = (bf16[1,512,384]{2,1,0:T(8,128)(2,1)S(1)}, bf16[1,512,384]{2,1,0:T(8,128)(2,1)}, u32[]{:S(2)}) copy-start(bf16[1,512,384]{2,1,0:T(8,128)(2,1)} %param.6) | copy-start | bytes 1179652
  11.5 7.9 %collective-permute-start = (bf16[32,3072]{1,0:T(8,128)(2,1)S(1)}, bf16[32,3072]{1,0:T(8,128)(2,1)S(1)}, u32[]{:S(2)}, u32[]{:S(2)}) collective-permute-start(bf16[32,3072]{1,0:T(8,128)(2,1)S(1)} %get-tuple-element.30), channel_id=1, source_target_pairs={{0,4},{4,0},{8,12},{12,8},{16,20},{20,16},{24,28},{28,24},{32,36},... | collective-permute-start | bytes 589832 | tf_op jit(solution)/shard_map/ppermute | solution.py:213
  19.4 31.3 %collective-permute-start.6 = (bf16[32,3072]{1,0:T(8,128)(2,1)}, bf16[32,3072]{1,0:T(8,128)(2,1)S(1)}, u32[]{:S(2)}, u32[]{:S(2)}) collective-permute-start(bf16[32,3072]{1,0:T(8,128)(2,1)} %get-tuple-element.36), channel_id=1, source_target_pairs={{0,4},{4,0},{8,12},{12,8},{16,20},{20,16},{24,28},{28,24},{32,36},... | collective-permute-start | bytes 589832 | tf_op jit(solution)/shard_map/ppermute | solution.py:213
  24.3 26.4 %collective-permute-start.1 = (bf16[32,3072]{1,0:T(8,128)(2,1)S(1)}, bf16[32,3072]{1,0:T(8,128)(2,1)S(1)}, u32[]{:S(2)}, u32[]{:S(2)}) collective-permute-start(bf16[32,3072]{1,0:T(8,128)(2,1)S(1)} %add_convert_fusion.10), channel_id=1, source_target_pairs={{4,8},{8,4},{12,16},{16,12},{20,24},{24,20},{28,32},{32,28},{36,40... | collective-permute-start | bytes 589832 | tf_op jit(solution)/shard_map/ppermute | solution.py:213
  37.1 1.0 copy-start
  38.1 0.9 copy-start.5
  44.6 6.1 %copy-start.14 = (bf16[32,3072]{1,0:T(8,128)(2,1)S(1)}, bf16[32,3072]{1,0:T(8,128)(2,1)}, u32[]{:S(2)}) copy-start(bf16[32,3072]{1,0:T(8,128)(2,1)} %get-tuple-element.34) | copy-start | bytes 589828
  44.6 8.2 %copy-start.13 = (bf16[32,3072]{1,0:T(8,128)(2,1)S(1)}, bf16[32,3072]{1,0:T(8,128)(2,1)}, u32[]{:S(2)}) copy-start(bf16[32,3072]{1,0:T(8,128)(2,1)} %get-tuple-element.28) | copy-start | bytes 589828
  44.7 16.1 %copy-start.12 = (bf16[32,3072]{1,0:T(8,128)(2,1)S(1)}, bf16[32,3072]{1,0:T(8,128)(2,1)}, u32[]{:S(2)}) copy-start(bf16[32,3072]{1,0:T(8,128)(2,1)} %get-tuple-element.33) | copy-start | bytes 589828
  44.7 18.1 %copy-start.11 = (bf16[32,3072]{1,0:T(8,128)(2,1)S(1)}, bf16[32,3072]{1,0:T(8,128)(2,1)}, u32[]{:S(2)}) copy-start(bf16[32,3072]{1,0:T(8,128)(2,1)} %get-tuple-element.27) | copy-start | bytes 589828
  44.7 27.1 %copy-start.10 = (bf16[32,3072]{1,0:T(8,128)(2,1)S(1)}, bf16[32,3072]{1,0:T(8,128)(2,1)}, u32[]{:S(2)}) copy-start(bf16[32,3072]{1,0:T(8,128)(2,1)} %get-tuple-element.32) | copy-start | bytes 589828
  44.7 32.1 %copy-start.9 = (bf16[32,3072]{1,0:T(8,128)(2,1)S(1)}, bf16[32,3072]{1,0:T(8,128)(2,1)}, u32[]{:S(2)}) copy-start(bf16[32,3072]{1,0:T(8,128)(2,1)} %get-tuple-element.26) | copy-start | bytes 589828
  44.7 44.9 %all-to-all-start.1 = ((bf16[8,520,384]{2,1,0:T(8,128)(2,1)}), bf16[8,520,384]{2,1,0:T(8,128)(2,1)}, u32[]{:S(2)}, u32[]{:S(2)}) async-start(bf16[8,520,384]{2,1,0:T(8,128)(2,1)} %shard_map.78), calls=%async_computation.1 | async-start | bytes 6389760 | tf_op jit(solution)/shard_map/all_to_all | solution.py:259
  50.7 33.7 %copy-start.8 = (bf16[32,3072]{1,0:T(8,128)(2,1)S(1)}, bf16[32,3072]{1,0:T(8,128)(2,1)}, u32[]{:S(2)}) copy-start(bf16[32,3072]{1,0:T(8,128)(2,1)} %get-tuple-element.31) | copy-start | bytes 589828
  50.7 35.7 %copy-start.7 = (bf16[32,3072]{1,0:T(8,128)(2,1)S(1)}, bf16[32,3072]{1,0:T(8,128)(2,1)}, u32[]{:S(2)}) copy-start(bf16[32,3072]{1,0:T(8,128)(2,1)} %get-tuple-element.25) | copy-start | bytes 589828
  50.8 10.0 %collective-permute-start.7 = (bf16[32,3072]{1,0:T(8,128)(2,1)S(1)}, bf16[32,3072]{1,0:T(8,128)(2,1)S(1)}, u32[]{:S(2)}, u32[]{:S(2)}) collective-permute-start(bf16[32,3072]{1,0:T(8,128)(2,1)S(1)} %add_convert_fusion.5), channel_id=1, source_target_pairs={{4,8},{8,4},{12,16},{16,12},{20,24},{24,20},{28,32},{32,28},{36,40... | collective-permute-start | bytes 589832 | tf_op jit(solution)/shard_map/ppermute | solution.py:213
  52.9 7.9 %collective-permute-start.2 = (bf16[32,3072]{1,0:T(8,128)(2,1)S(1)}, bf16[32,3072]{1,0:T(8,128)(2,1)S(1)}, u32[]{:S(2)}, u32[]{:S(2)}) collective-permute-start(bf16[32,3072]{1,0:T(8,128)(2,1)S(1)} %add_convert_fusion.9), channel_id=1, source_target_pairs={{0,4},{4,0},{8,12},{12,8},{16,20},{20,16},{24,28},{28,24},{32,36},... | collective-permute-start | bytes 589832 | tf_op jit(solution)/shard_map/ppermute | solution.py:213
  60.9 7.6 %collective-permute-start.8 = (bf16[32,3072]{1,0:T(8,128)(2,1)S(1)}, bf16[32,3072]{1,0:T(8,128)(2,1)S(1)}, u32[]{:S(2)}, u32[]{:S(2)}) collective-permute-start(bf16[32,3072]{1,0:T(8,128)(2,1)S(1)} %add_convert_fusion.4), channel_id=1, source_target_pairs={{0,4},{4,0},{8,12},{12,8},{16,20},{20,16},{24,28},{28,24},{32,36},... | collective-permute-start | bytes 589832 | tf_op jit(solution)/shard_map/ppermute | solution.py:213
  62.9 9.0 %collective-permute-start.3 = (bf16[32,3072]{1,0:T(8,128)(2,1)S(1)}, bf16[32,3072]{1,0:T(8,128)(2,1)S(1)}, u32[]{:S(2)}, u32[]{:S(2)}) collective-permute-start(bf16[32,3072]{1,0:T(8,128)(2,1)S(1)} %add_convert_fusion.8), channel_id=1, source_target_pairs={{4,8},{8,4},{12,16},{16,12},{20,24},{24,20},{28,32},{32,28},{36,40... | collective-permute-start | bytes 589832 | tf_op jit(solution)/shard_map/ppermute | solution.py:213
  71.9 10.8 %collective-permute-start.9 = (bf16[32,3072]{1,0:T(8,128)(2,1)S(1)}, bf16[32,3072]{1,0:T(8,128)(2,1)S(1)}, u32[]{:S(2)}, u32[]{:S(2)}) collective-permute-start(bf16[32,3072]{1,0:T(8,128)(2,1)S(1)} %add_convert_fusion.3), channel_id=1, source_target_pairs={{4,8},{8,4},{12,16},{16,12},{20,24},{24,20},{28,32},{32,28},{36,40... | collective-permute-start | bytes 589832 | tf_op jit(solution)/shard_map/ppermute | solution.py:213
  76.8 7.6 %collective-permute-start.4 = (bf16[32,3072]{1,0:T(8,128)(2,1)S(1)}, bf16[32,3072]{1,0:T(8,128)(2,1)S(1)}, u32[]{:S(2)}, u32[]{:S(2)}) collective-permute-start(bf16[32,3072]{1,0:T(8,128)(2,1)S(1)} %add_convert_fusion.7), channel_id=1, source_target_pairs={{0,4},{4,0},{8,12},{12,8},{16,20},{20,16},{24,28},{28,24},{32,36},... | collective-permute-start | bytes 589832 | tf_op jit(solution)/shard_map/ppermute | solution.py:213
  84.5 10.5 %collective-permute-start.10 = (bf16[32,3072]{1,0:T(8,128)(2,1)S(1)}, bf16[32,3072]{1,0:T(8,128)(2,1)S(1)}, u32[]{:S(2)}, u32[]{:S(2)}) collective-permute-start(bf16[32,3072]{1,0:T(8,128)(2,1)S(1)} %add_convert_fusion.2), channel_id=1, source_target_pairs={{0,4},{4,0},{8,12},{12,8},{16,20},{20,16},{24,28},{28,24},{32,36},... | collective-permute-start | bytes 589832 | tf_op jit(solution)/shard_map/ppermute | solution.py:213
  86.4 8.8 %collective-permute-start.5 = (bf16[32,3072]{1,0:T(8,128)(2,1)S(1)}, bf16[32,3072]{1,0:T(8,128)(2,1)S(1)}, u32[]{:S(2)}, u32[]{:S(2)}) collective-permute-start(bf16[32,3072]{1,0:T(8,128)(2,1)S(1)} %add_convert_fusion.6), channel_id=1, source_target_pairs={{4,8},{8,4},{12,16},{16,12},{20,24},{24,20},{28,32},{32,28},{36,40... | collective-permute-start | bytes 589832 | tf_op jit(solution)/shard_map/ppermute | solution.py:213
  89.6 5.6 %copy-start.6 = (f32[32,3072]{1,0:T(8,128)S(1)}, f32[32,3072]{1,0:T(8,128)}, u32[]{:S(2)}) copy-start(f32[32,3072]{1,0:T(8,128)} %get-tuple-element.24) | copy-start | bytes 1179652
  93.6 20.0 %collective-permute-start.11 = (bf16[512,384]{1,0:T(8,128)(2,1)S(1)}, bf16[512,384]{1,0:T(8,128)(2,1)S(1)}, u32[]{:S(2)}, u32[]{:S(2)}) collective-permute-start(bf16[512,384]{1,0:T(8,128)(2,1)S(1)} %get-tuple-element.44), channel_id=1, source_target_pairs={{384,0},{385,1},{386,2},{387,3},{388,4},{389,5},{390,6},{391,7},{3... | collective-permute-start | bytes 1179656 | tf_op jit(solution)/shard_map/ppermute | solution.py:261
  96.0 17.0 %all-to-all-start = ((bf16[4,8,3072]{2,1,0:T(8,128)(2,1)}), bf16[4,8,3072]{2,1,0:T(8,128)(2,1)S(1)}, u32[]{:S(2)}, u32[]{:S(2)}) async-start(bf16[4,8,3072]{2,1,0:T(8,128)(2,1)} %fusion.2), calls=%async_computation | async-start | bytes 393216 | tf_op jit(solution)/shard_map/all_to_all | solution.py:247

commit v5 on v4

v5 whole, which is shorter than its diff:
```python
import jax
import jax.numpy as jnp
from jax import lax
from jax.experimental import pallas as pl
from jax.experimental.pallas import tpu as pltpu
from jax.sharding import Mesh
from jax.sharding import PartitionSpec as P


TOK_MB = 256
DP = ("dz", "dy")
MP = ("my", "mx")
F32 = jnp.float32
BF16 = jnp.bfloat16
TOK = 512
BLOCK = 128
CHUNK = 16
UNROLL = 8
WIDTH = 3072
SHARE = 384
RING = 12
ROWS = SHARE // RING
PARTS = 8
EXTRA = 8
COLS = 512


def in_hbm(*arrays):
    return [pltpu.with_memory_space_constraint(a, pltpu.HBM) for a in arrays]


def front_kernel(scal, stream, value_grad_from, gain_from, held, stats, own, *rest):
    blocks, (normed, grad, value_grad, gain, sems) = rest[:-5], rest[-5:]
    per = TOK // BLOCK
    gain_here = pltpu.make_async_copy(gain_from, gain, sems.at[per])
    gain_here.start()
    arrivals = []
    for b in range(TOK // BLOCK):
        rows = pl.ds(b * BLOCK, BLOCK)
        arrivals.append(pltpu.make_async_copy(stream.at[rows, :], held.at[rows, :], sems.at[b]))
        arrivals[-1].start()
    value_grad_here = pltpu.make_async_copy(value_grad_from, value_grad, sems.at[per + 1])
    value_grad_here.start()
    gain_here.wait()
    lanes = [slice(t * 128, (t + 1) * 128) for t in range(WIDTH // 128)]

    def chunk(i, carry):
        rows = pl.ds(pl.multiple_of(i * CHUNK, CHUNK), CHUNK)
        total = [jnp.zeros((CHUNK, 128), F32)] * 2
        for t, lane in enumerate(lanes):
            total[t % 2] += held[rows, lane].astype(F32)
        mean = jnp.sum(total[0] + total[1], axis=1, keepdims=True) * (1.0 / WIDTH)
        total = [jnp.zeros((CHUNK, 128), F32)] * 2
        for t, lane in enumerate(lanes):
            centred = held[rows, lane].astype(F32) - mean
            total[t % 2] += centred * centred
        variance = jnp.sum(total[0] + total[1], axis=1, keepdims=True) * (1.0 / WIDTH)
        inv = lax.rsqrt(variance + 1e-06)
        for lane in lanes:
            normed[rows, lane] = ((held[rows, lane].astype(F32) - mean) * inv * gain[:, lane]).astype(BF16)
        stats[0, rows, :] = jnp.broadcast_to(inv, (CHUNK, 128))
        stats[1, rows, :] = jnp.broadcast_to(mean, (CHUNK, 128))
        return carry

    per = BLOCK // CHUNK
    for b in range(TOK // BLOCK):
        arrivals[b].wait()
        lax.fori_loop(b * per, (b + 1) * per, chunk, 0, unroll=UNROLL)
    value_grad_here.wait()
    token = lax.broadcasted_iota(jnp.int32, (TOK, SHARE), 0)
    live = token < scal[3] * TOK_MB
    left = jnp.where(live, value_grad[...].astype(F32), 0.0).astype(BF16).T
    for n in range(WIDTH // COLS):
        cols = slice(n * COLS, (n + 1) * COLS)
        grad[...] = jnp.dot(left, normed[:, cols], preferred_element_type=F32)
        for r in range(RING):
            at = lax.rem(scal[0] + r * scal[1] + RING, RING) * ROWS
            piece = grad[pl.ds(pl.multiple_of(at, ROWS), ROWS), :]
            if r == 0:
                own[:, cols] = piece
            else:
                blocks[r - 1][:, cols] = piece.astype(BF16)


def front(scal, stream, value_grad, gain):
    vmem = pl.BlockSpec(memory_space=pltpu.VMEM)
    out = [((TOK, WIDTH), BF16), ((2, TOK, 128), F32), ((ROWS, WIDTH), F32)]
    out += [((ROWS, WIDTH), BF16)] * (RING - 1)
    return pl.pallas_call(
        front_kernel,
        in_specs=[
            pl.BlockSpec(memory_space=pltpu.SMEM),
            *[pl.BlockSpec(memory_space=pl.ANY)] * 3,
        ],
        out_specs=[vmem] * len(out),
        scratch_shapes=[
            pltpu.VMEM((TOK, WIDTH), BF16),
            pltpu.VMEM((SHARE, COLS), F32),
            pltpu.VMEM((TOK, SHARE), BF16),
            pltpu.VMEM((1, WIDTH), F32),
            pltpu.SemaphoreType.DMA((TOK // BLOCK + 2,)),
        ],
        out_shape=[jax.ShapeDtypeStruct(*o) for o in out],
        compiler_params=pltpu.CompilerParams(vmem_limit_bytes=24 * 1024 * 1024),
        cost_estimate=pl.CostEstimate(flops=2 * TOK * SHARE * WIDTH * 4, transcendentals=0, bytes_accessed=8_000_000),
    )(scal, *in_hbm(stream, value_grad, gain))


def parts_kernel(value_grad, weights, held, gain, stats, out, packed, extra, sums, sems):
    copies = []
    for m in range(PARTS):
        cols = slice(m * SHARE, (m + 1) * SHARE)
        part = jnp.dot(value_grad[...], weights[:, cols], preferred_element_type=F32).astype(BF16)
        packed[m] = part
        copies.append(pltpu.make_async_copy(packed.at[m], out.at[m, pl.ds(0, TOK), :], sems.at[m]))
        copies[-1].start()
        scaled = part.astype(F32) * gain[:, cols]
        tiles = [scaled[:, t * 128 : (t + 1) * 128] for t in range(SHARE // 128)]
        first = tiles[0] + tiles[1] + tiles[2]
        second = None
        for t, tile in enumerate(tiles):
            low = m * SHARE + t * 128
            term = tile * (held[:, low : low + 128].astype(F32) - stats[1])
            second = term if second is None else second + term
        if m == 0:
            sums[0] = first
            sums[1] = second
        else:
            sums[0] += first
            sums[1] += second
    lines = []
    for total in (sums[0], sums[1] * stats[0]):
        line = jnp.sum(total.T, axis=0, keepdims=True)
        high = line.astype(BF16).astype(F32)
        lines += [high, line - high]
    stacked = jnp.concatenate(lines, axis=0)
    tail = jnp.concatenate([stacked[:, SHARE:], jnp.zeros((4, SHARE - 128), F32)], axis=1)
    extra[...] = jnp.concatenate([stacked[:, :SHARE], tail], axis=0).astype(BF16)
    for m in range(PARTS):
        copies.append(pltpu.make_async_copy(extra, out.at[m, pl.ds(TOK, EXTRA), :], sems.at[PARTS + m]))
        copies[-1].start()
    for copy in copies:
        copy.wait()


def parts(value_grad, weights, held, gain, stats):
    vmem = pl.BlockSpec(memory_space=pltpu.VMEM)
    return pl.pallas_call(
        parts_kernel,
        in_specs=[vmem] * 5,
        out_specs=pl.BlockSpec(memory_space=pl.ANY),
        out_shape=pltpu.HBM((PARTS, TOK + EXTRA, SHARE), BF16),
        scratch_shapes=[
            pltpu.VMEM((PARTS, TOK, SHARE), BF16),
            pltpu.VMEM((EXTRA, SHARE), BF16),
            pltpu.VMEM((2, TOK, 128), F32),
            pltpu.SemaphoreType.DMA((2 * PARTS,)),
        ],
        compiler_params=pltpu.CompilerParams(vmem_limit_bytes=16 * 1024 * 1024),
        cost_estimate=pl.CostEstimate(flops=2 * TOK * SHARE * WIDTH * 3, transcendentals=0, bytes_accessed=9_000_000),
    )(value_grad, weights, held, gain, stats)


def back_kernel(scal, arrived, extra, stream, stats, gain, top, back, above, columns):
    step = pl.program_id(0)

    @pl.when(step == 0)
    def _():
        sums = jnp.sum(extra[...].astype(F32), axis=0)
        lines = jnp.concatenate([sums[:4], sums[4:, :128]], axis=1)
        for j, line in enumerate((lines[0:1] + lines[1:2], lines[2:3] + lines[3:4])):
            for b in range(TOK // BLOCK):
                square = jnp.broadcast_to(line[:, b * BLOCK : (b + 1) * BLOCK], (BLOCK, BLOCK))
                columns[j, b * BLOCK : (b + 1) * BLOCK, :] = square.T * (1.0 / WIDTH)

    rows = pl.ds(pl.multiple_of(step * BLOCK, BLOCK), BLOCK)
    mean = columns[0, rows, :][:, :1]
    slope = columns[1, rows, :][:, :1]
    total = arrived[0].astype(F32)
    for j in range(1, PARTS):
        total = total + arrived[j].astype(F32)
    scale = stats[0][:, 0:1]
    white = (stream[...].astype(F32) - stats[1][:, 0:1]) * scale
    branch = scale * (total * gain[...] - mean - white * slope)
    back[...] = branch
    above[...] = (top[...].astype(F32) + branch).astype(BF16)


def backward(scal, arrived, stream, stats, gain, top):
    token = lambda width: pl.BlockSpec((BLOCK, width), lambda i, s: (i, 0))
    return pl.pallas_call(
        back_kernel,
        grid_spec=pltpu.PrefetchScalarGridSpec(
            num_scalar_prefetch=1,
            grid=(TOK // BLOCK,),
            in_specs=[
                pl.BlockSpec((PARTS, BLOCK, SHARE), lambda i, s: (0, i, 0)),
                pl.BlockSpec((PARTS, EXTRA, SHARE), lambda i, s: (0, TOK // EXTRA, 0)),
                pl.BlockSpec((BLOCK, SHARE), lambda i, s: (i, s[2])),
                pl.BlockSpec((2, BLOCK, 128), lambda i, s: (0, i, 0)),
                pl.BlockSpec((1, SHARE), lambda i, s: (0, s[2])),
                pl.BlockSpec((BLOCK, SHARE), lambda i, s: (i, s[2])),
            ],
            out_specs=[token(SHARE), token(SHARE)],
            scratch_shapes=[pltpu.VMEM((2, TOK, BLOCK), F32)],
        ),
        out_shape=[jax.ShapeDtypeStruct((TOK, SHARE), F32), jax.ShapeDtypeStruct((TOK, SHARE), BF16)],
        compiler_params=pltpu.CompilerParams(
            dimension_semantics=("arbitrary",), vmem_limit_bytes=16 * 1024 * 1024
        ),
        cost_estimate=pl.CostEstimate(flops=500_000_000, transcendentals=0, bytes_accessed=6_000_000),
    )(scal, *in_hbm(arrived, arrived, stream, stats, gain, top))


def swapped(value, link):
    peers = lax.axis_size("dz")
    pairs = []
    for i in range(link, peers, 2):
        pairs += [(i, (i + 1) % peers), ((i + 1) % peers, i)]
    return lax.ppermute(value, "dz", pairs)


def tied(value, *others):
    return lax.optimization_barrier((value, *others))[0]


def joined_kernel(own, got, out):
    out[...] = (own[...].astype(F32) + got[...].astype(F32)).astype(BF16)


def joined(own, got):
    vmem = pl.BlockSpec(memory_space=pltpu.VMEM)
    return pl.pallas_call(
        joined_kernel,
        in_specs=[vmem, vmem],
        out_specs=vmem,
        out_shape=jax.ShapeDtypeStruct(own.shape, BF16),
        compiler_params=pltpu.CompilerParams(vmem_limit_bytes=4 * 1024 * 1024),
    )(own, got)


def sum_over_z(own, blocks):
    def block(link, distance):
        return blocks[(distance if link == 0 else RING - distance) - 1]

    far = RING // 2
    long = swapped(block(0, far), 0)
    short = None
    link = 0
    for k in range(far - 1, 0, -1):
        link = 1 - link
        if short is None:
            mine_short = tied(block(1 - link, k), long)
        else:
            mine_short = joined(block(1 - link, k), tied(short, long))
        mine = joined(block(link, k), long)
        long = swapped(mine, link)
        short = swapped(mine_short, 1 - link)
    return own + long.astype(F32) + short.astype(F32)


def sum_over_y(rows_sum):
    peers = lax.axis_size("dy")
    tiles = rows_sum.astype(BF16).reshape(peers, rows_sum.shape[0] // peers, rows_sum.shape[1])
    arrived = lax.all_to_all(tiles, "dy", split_axis=0, concat_axis=0, tiled=True)
    return arrived.astype(F32).sum(axis=0)


def shards(value_grad, stream, weights, gain, top_grad, counts):
    section_index = lax.axis_index("section")
    model_index = lax.axis_index(MP)
    place = lax.axis_index("dz")
    scal = jnp.stack([place, 1 - 2 * (place % 2), model_index, counts[0]]).astype(jnp.int32)
    held, stats, own, *blocks = front(scal, stream[0], value_grad[0], gain)
    weight_grad = sum_over_y(sum_over_z(own, blocks)).astype(BF16)[None]
    tiles = parts(value_grad[0], weights[0], held, gain, stats)
    arrived = lax.all_to_all(tiles, MP, split_axis=0, concat_axis=0, tiled=True)
    norm_back, above_grad = backward(scal, arrived, stream[0], stats, gain, top_grad)
    below_grad = lax.ppermute(above_grad, "section", [(1, 0)])
    lower_grad = (below_grad.astype(F32) + norm_back).astype(BF16)
    result = jnp.where(section_index == 0, lower_grad, above_grad)
    return (weight_grad, result[None])


def solution(mesh):
    split = Mesh(
        mesh.devices.reshape(mesh.shape["section"], 2, 4, 12, 4),
        ("section", "my", "mx", "dz", "dy"),
    )
    placed = (
        P("section", DP, MP),
        P("section", DP, None),
        P("section", MP, None),
        P("section", None),
        P(DP, None),
        P(DP),
    )

    return jax.shard_map(
        shards,
        mesh=split,
        in_specs=placed,
        out_specs=(P("section", MP + DP, None), P("section", DP, MP)),
        check_vma=False,
    )
```

time: 115 us -> 113 us (0.983)
  the two profiles are of different devices: /device:TPU:2 before, /device:TPU:1 now
where the time goes in v5:
time: 113 us; the launch traced here: 112 us
  starting transfers between devices  63.4 us (56%)
  waiting for transfers between devices  31 us (27%)
  Pallas kernels  14.2 us (13%)
  other arithmetic  2.35 us (2%)
  between operations  1.54 us (1%)
    ppermute x11, starting transfers between devices, swapped(): return lax.ppermute(value, 'dz', pairs)  42.3 us
    ppermute x11, waiting for transfers between devices, swapped(): return lax.ppermute(value, 'dz', pairs)  21.2 us
    all_to_all x1, waiting for transfers between devices, sum_over_y(): lax.all_to_all(tiles, 'dy', split_axis=0, concat_axis=0, tiled=True)  9.83 us
    ppermute x1, starting transfers between devices, shards(): below_grad = lax.ppermute(above_grad, 'section', [(1, 0)])  9.24 us
    all_to_all x1, starting transfers between devices, sum_over_y(): lax.all_to_all(tiles, 'dy', split_axis=0, concat_axis=0, tiled=True)  5.97 us
    pallas_call x1, Pallas kernels, front(): pl.pallas_call(front_kernel, in_specs=[pl.BlockSpec(memory_space=pltpu.SM...  5.94 us
    all_to_all x1, starting transfers between devices, shards(): arrived = lax.all_to_all(tiles, MP, split_axis=0, concat_axis=0, tiled=True)  5.87 us
    pallas_call x1, Pallas kernels, backward(): pl.pallas_call(back_kernel, grid_spec=pltpu.PrefetchScalarGridSpec(num_sc...  4.05 us
  transfers between devices with their start and end apart: 14, of which 9 were waited for; matrix products, arithmetic and copies ran while one was open for 1% of the time, Pallas kernels for 4%

profile of v5, /device:TPU:1, one launch (start us, length us, event | category | flops | bytes accessed | tf_op | source)
XLA Modules:
  0.0 112.5 jit_solution(11262641275995062806)
XLA Ops:
  1.3 0.1 pad_add_fusion.scal
  1.4 0.0 copy-start.1
  1.4 0.0 copy-start.2
  1.4 0.0 copy-start.3
  1.4 5.9 %shard_map.77 = (bf16[512,3072]{1,0:T(8,128)(2,1)S(1)}, f32[2,512,128]{2,1,0:T(8,128)S(1)}, f32[32,3072]{1,0:T(8,128)S(1)}, bf16[32,3072]{1,0:T(8,128)(2,1)S(1)}...) custom-call(s32[4]{0:T(128)S(1)} %pad_add_fusion.scal, ...), custom_call_target="tpu_custom_call" | custom-call | flops 4831838208 | bytes 8000000 | tf_op jit(solution)/shard_map/pallas_call | solution.py:89
  7.3 0.0 copy-start
  7.3 0.0 copy-done.1
  7.3 0.0 copy-done.2
  7.4 0.0 copy-done.3
  7.4 3.8 %shard_map.87 = bf16[8,520,384]{2,1,0:T(8,128)(2,1)} custom-call(bf16[512,384]{1,0:T(8,128)(2,1)S(1)} %bitcast.13, bf16[384,3072]{1,0:T(8,128)(2,1)S(1)} %bitcast.11, bf16[512,3072]{1,0:T(8,128)(2,1)S(1)} %get-tuple-element.40.held, f32[1,3072]{1,0:T(1,128)S(1)} %copy-done.1, f32[2,512,128]{2,1,0:T(8,128)S(1)} %get-tuple-element.41.stats), custom_call_target="tpu_custom_call" | custom-call | flops 3623878656 | bytes 9000000 | tf_op jit(solution)/shard_map/pallas_call | solution.py:148
  11.1 0.0 copy-done
  11.1 5.9 %all-to-all-start.1 = ((bf16[8,520,384]{2,1,0:T(8,128)(2,1)}), bf16[8,520,384]{2,1,0:T(8,128)(2,1)}, u32[]{:S(2)}, u32[]{:S(2)}) async-start(bf16[8,520,384]{2,1,0:T(8,128)(2,1)} %shard_map.87), calls=%async_computation.1 | async-start | bytes 6389760 | tf_op jit(solution)/shard_map/all_to_all | solution.py:277
  17.0 4.0 %collective-permute-start = (bf16[32,3072]{1,0:T(8,128)(2,1)S(1)}, bf16[32,3072]{1,0:T(8,128)(2,1)S(1)}, u32[]{:S(2)}, u32[]{:S(2)}) collective-permute-start(bf16[32,3072]{1,0:T(8,128)(2,1)S(1)} %get-tuple-element.29), channel_id=1, source_target_pairs={{0,4},{4,0},{8,12},{12,8},{16,20},{20,16},{24,28},{28,24},{32,36},... | collective-permute-start | bytes 589832 | tf_op jit(solution)/shard_map/ppermute | solution.py:220
  21.0 3.0 %collective-permute-done.got = bf16[32,3072]{1,0:T(8,128)(2,1)S(1)} collective-permute-done((bf16[32,3072]{1,0:T(8,128)(2,1)S(1)}, bf16[32,3072]{1,0:T(8,128)(2,1)S(1)}, u32[]{:S(2)}, u32[]{:S(2)}) %collective-permute-start) | collective-permute-done | bytes 196640 | tf_op jit(solution)/shard_map/ppermute | solution.py:220
  24.1 3.8 %collective-permute-start.6 = (bf16[32,3072]{1,0:T(8,128)(2,1)S(1)}, bf16[32,3072]{1,0:T(8,128)(2,1)S(1)}, u32[]{:S(2)}, u32[]{:S(2)}) collective-permute-start(bf16[32,3072]{1,0:T(8,128)(2,1)S(1)} %get-tuple-element.35), channel_id=1, source_target_pairs={{0,4},{4,0},{8,12},{12,8},{16,20},{20,16},{24,28},{28,24},{32,36},... | collective-permute-start | bytes 589832 | tf_op jit(solution)/shard_map/ppermute | solution.py:220
  27.9 13.2 %collective-permute-start.1 = (bf16[32,3072]{1,0:T(8,128)(2,1)S(1)}, bf16[32,3072]{1,0:T(8,128)(2,1)S(1)}, u32[]{:S(2)}, u32[]{:S(2)}) collective-permute-start(bf16[32,3072]{1,0:T(8,128)(2,1)S(1)} %shard_map.78), channel_id=1, source_target_pairs={{4,8},{8,4},{12,16},{16,12},{20,24},{24,20},{28,32},{32,28},{36,40... | collective-permute-start | bytes 589832 | tf_op jit(solution)/shard_map/ppermute | solution.py:220
  41.1 0.0 collective-permute-done.6.got
  41.1 3.4 %collective-permute-done.1.got = bf16[32,3072]{1,0:T(8,128)(2,1)S(1)} collective-permute-done((bf16[32,3072]{1,0:T(8,128)(2,1)S(1)}, bf16[32,3072]{1,0:T(8,128)(2,1)S(1)}, u32[]{:S(2)}, u32[]{:S(2)}) %collective-permute-start.1) | collective-permute-done | bytes 196640 | tf_op jit(solution)/shard_map/ppermute | solution.py:220
  44.6 4.6 %collective-permute-start.7 = (bf16[32,3072]{1,0:T(8,128)(2,1)S(1)}, bf16[32,3072]{1,0:T(8,128)(2,1)S(1)}, u32[]{:S(2)}, u32[]{:S(2)}) collective-permute-start(bf16[32,3072]{1,0:T(8,128)(2,1)S(1)} %shard_map.83), channel_id=1, source_target_pairs={{4,8},{8,4},{12,16},{16,12},{20,24},{24,20},{28,32},{32,28},{36,40... | collective-permute-start | bytes 589832 | tf_op jit(solution)/shard_map/ppermute | solution.py:220
  49.2 1.9 %collective-permute-start.2 = (bf16[32,3072]{1,0:T(8,128)(2,1)S(1)}, bf16[32,3072]{1,0:T(8,128)(2,1)S(1)}, u32[]{:S(2)}, u32[]{:S(2)}) collective-permute-start(bf16[32,3072]{1,0:T(8,128)(2,1)S(1)} %shard_map.79), channel_id=1, source_target_pairs={{0,4},{4,0},{8,12},{12,8},{16,20},{20,16},{24,28},{28,24},{32,36},... | collective-permute-start | bytes 589832 | tf_op jit(solution)/shard_map/ppermute | solution.py:220
  51.1 1.5 %collective-permute-done.7.got = bf16[32,3072]{1,0:T(8,128)(2,1)S(1)} collective-permute-done((bf16[32,3072]{1,0:T(8,128)(2,1)S(1)}, bf16[32,3072]{1,0:T(8,128)(2,1)S(1)}, u32[]{:S(2)}, u32[]{:S(2)}) %collective-permute-start.7) | collective-permute-done | bytes 196640 | tf_op jit(solution)/shard_map/ppermute | solution.py:220
  52.6 3.0 %collective-permute-done.2.got = bf16[32,3072]{1,0:T(8,128)(2,1)S(1)} collective-permute-done((bf16[32,3072]{1,0:T(8,128)(2,1)S(1)}, bf16[32,3072]{1,0:T(8,128)(2,1)S(1)}, u32[]{:S(2)}, u32[]{:S(2)}) %collective-permute-start.2) | collective-permute-done | bytes 196640 | tf_op jit(solution)/shard_map/ppermute | solution.py:220
  55.7 2.3 %collective-permute-start.8 = (bf16[32,3072]{1,0:T(8,128)(2,1)S(1)}, bf16[32,3072]{1,0:T(8,128)(2,1)S(1)}, u32[]{:S(2)}, u32[]{:S(2)}) collective-permute-start(bf16[32,3072]{1,0:T(8,128)(2,1)S(1)} %shard_map.84), channel_id=1, source_target_pairs={{0,4},{4,0},{8,12},{12,8},{16,20},{20,16},{24,28},{28,24},{32,36},... | collective-permute-start | bytes 589832 | tf_op jit(solution)/shard_map/ppermute | solution.py:220
  58.1 1.9 %collective-permute-start.3 = (bf16[32,3072]{1,0:T(8,128)(2,1)S(1)}, bf16[32,3072]{1,0:T(8,128)(2,1)S(1)}, u32[]{:S(2)}, u32[]{:S(2)}) collective-permute-start(bf16[32,3072]{1,0:T(8,128)(2,1)S(1)} %shard_map.80), channel_id=1, source_target_pairs={{4,8},{8,4},{12,16},{16,12},{20,24},{24,20},{28,32},{32,28},{36,40... | collective-permute-start | bytes 589832 | tf_op jit(solution)/shard_map/ppermute | solution.py:220
  60.0 2.1 %collective-permute-done.8.got = bf16[32,3072]{1,0:T(8,128)(2,1)S(1)} collective-permute-done((bf16[32,3072]{1,0:T(8,128)(2,1)S(1)}, bf16[32,3072]{1,0:T(8,128)(2,1)S(1)}, u32[]{:S(2)}, u32[]{:S(2)}) %collective-permute-start.8) | collective-permute-done | bytes 196640 | tf_op jit(solution)/shard_map/ppermute | solution.py:220
  62.1 3.6 %collective-permute-done.3.got = bf16[32,3072]{1,0:T(8,128)(2,1)S(1)} collective-permute-done((bf16[32,3072]{1,0:T(8,128)(2,1)S(1)}, bf16[32,3072]{1,0:T(8,128)(2,1)S(1)}, u32[]{:S(2)}, u32[]{:S(2)}) %collective-permute-start.3) | collective-permute-done | bytes 196640 | tf_op jit(solution)/shard_map/ppermute | solution.py:220
  65.7 2.3 %collective-permute-start.9 = (bf16[32,3072]{1,0:T(8,128)(2,1)S(1)}, bf16[32,3072]{1,0:T(8,128)(2,1)S(1)}, u32[]{:S(2)}, u32[]{:S(2)}) collective-permute-start(bf16[32,3072]{1,0:T(8,128)(2,1)S(1)} %shard_map.85), channel_id=1, source_target_pairs={{4,8},{8,4},{12,16},{16,12},{20,24},{24,20},{28,32},{32,28},{36,40... | collective-permute-start | bytes 589832 | tf_op jit(solution)/shard_map/ppermute | solution.py:220
  68.1 1.9 %collective-permute-start.4 = (bf16[32,3072]{1,0:T(8,128)(2,1)S(1)}, bf16[32,3072]{1,0:T(8,128)(2,1)S(1)}, u32[]{:S(2)}, u32[]{:S(2)}) collective-permute-start(bf16[32,3072]{1,0:T(8,128)(2,1)S(1)} %shard_map.81), channel_id=1, source_target_pairs={{0,4},{4,0},{8,12},{12,8},{16,20},{20,16},{24,28},{28,24},{32,36},... | collective-permute-start | bytes 589832 | tf_op jit(solution)/shard_map/ppermute | solution.py:220
  70.0 3.3 %collective-permute-done.9.got = bf16[32,3072]{1,0:T(8,128)(2,1)S(1)} collective-permute-done((bf16[32,3072]{1,0:T(8,128)(2,1)S(1)}, bf16[32,3072]{1,0:T(8,128)(2,1)S(1)}, u32[]{:S(2)}, u32[]{:S(2)}) %collective-permute-start.9) | collective-permute-done | bytes 196640 | tf_op jit(solution)/shard_map/ppermute | solution.py:220
  73.4 1.2 %collective-permute-done.4.got = bf16[32,3072]{1,0:T(8,128)(2,1)S(1)} collective-permute-done((bf16[32,3072]{1,0:T(8,128)(2,1)S(1)}, bf16[32,3072]{1,0:T(8,128)(2,1)S(1)}, u32[]{:S(2)}, u32[]{:S(2)}) %collective-permute-start.4) | collective-permute-done | bytes 196640 | tf_op jit(solution)/shard_map/ppermute | solution.py:220
  74.6 1.9 %collective-permute-start.10 = (bf16[32,3072]{1,0:T(8,128)(2,1)S(1)}, bf16[32,3072]{1,0:T(8,128)(2,1)S(1)}, u32[]{:S(2)}, u32[]{:S(2)}) collective-permute-start(bf16[32,3072]{1,0:T(8,128)(2,1)S(1)} %shard_map.86), channel_id=1, source_target_pairs={{0,4},{4,0},{8,12},{12,8},{16,20},{20,16},{24,28},{28,24},{32,36},... | collective-permute-start | bytes 589832 | tf_op jit(solution)/shard_map/ppermute | solution.py:220
  76.6 4.5 %collective-permute-start.5 = (bf16[32,3072]{1,0:T(8,128)(2,1)S(1)}, bf16[32,3072]{1,0:T(8,128)(2,1)S(1)}, u32[]{:S(2)}, u32[]{:S(2)}) collective-permute-start(bf16[32,3072]{1,0:T(8,128)(2,1)S(1)} %shard_map.82), channel_id=1, source_target_pairs={{4,8},{8,4},{12,16},{16,12},{20,24},{24,20},{28,32},{32,28},{36,40... | collective-permute-start | bytes 589832 | tf_op jit(solution)/shard_map/ppermute | solution.py:220
  81.0 0.0 all-to-all-done.1.arrived.extra
  81.0 4.1 %shard_map.88 = (f32[512,384]{1,0:T(8,128)S(1)}, bf16[512,384]{1,0:T(8,128)(2,1)S(1)}) custom-call(s32[4]{0:T(128)S(1)} %pad_add_fusion.scal, bf16[8,520,384]{2,1,0:T(8,128)(2,1)} %all-to-all-done.1.arrived.extra, bf16[8,520,384]{2,1,0:T(8,128)(2,1)} %all-to-all-done.1.arrived.extra, bf16[512,3072]{1,0:T(8,128)(2,1)} %bitcast.15, f32[2,512,128]{2,1,0:T(8,128)} %copy-done, ...), custom_call_target="tpu_custom_call" | custom-call | flops 500000000 | bytes 6000000 | tf_op jit(solution)/shard_map/pallas_call | solution.py:191
  85.1 9.2 %collective-permute-start.11 = (bf16[512,384]{1,0:T(8,128)(2,1)S(1)}, bf16[512,384]{1,0:T(8,128)(2,1)S(1)}, u32[]{:S(2)}, u32[]{:S(2)}) collective-permute-start(bf16[512,384]{1,0:T(8,128)(2,1)S(1)} %get-tuple-element.42), channel_id=1, source_target_pairs={{384,0},{385,1},{386,2},{387,3},{388,4},{389,5},{390,6},{391,7},{3... | collective-permute-start | bytes 1179656 | tf_op jit(solution)/shard_map/ppermute | solution.py:279
  94.4 0.0 collective-permute-done.10
  94.4 0.0 collective-permute-done.5
  94.4 0.7 fusion.2
  95.1 6.0 %all-to-all-start = ((bf16[4,8,3072]{2,1,0:T(8,128)(2,1)}), bf16[4,8,3072]{2,1,0:T(8,128)(2,1)S(1)}, u32[]{:S(2)}, u32[]{:S(2)}) async-start(bf16[4,8,3072]{2,1,0:T(8,128)(2,1)} %fusion.2), calls=%async_computation | async-start | bytes 393216 | tf_op jit(solution)/shard_map/all_to_all | solution.py:265
  101.1 9.8 %all-to-all-done = bf16[4,8,3072]{2,1,0:T(8,128)(2,1)S(1)} async-done(((bf16[4,8,3072]{2,1,0:T(8,128)(2,1)}), bf16[4,8,3072]{2,1,0:T(8,128)(2,1)S(1)}, u32[]{:S(2)}, u32[]{:S(2)}) %all-to-all-start) | async-done | bytes 196640 | tf_op jit(solution)/shard_map/all_to_all | solution.py:265
  110.9 0.7 reduce_sum.12
  111.6 0.0 collective-permute-done.11
  111.6 0.9 fusion.1
  (9 shorter events, 0.4 us)
Async XLA Ops:
  1.4 6.0 %copy-start.1 = (f32[1,3072]{1,0:T(1,128)S(1)}, f32[1,3072]{1,0:T(1,128)}, u32[]{:S(2)}) copy-start(f32[1,3072]{1,0:T(1,128)} %gain.3) | copy-start | bytes 36868
  1.4 6.0 %copy-start.2 = (bf16[1,384,3072]{2,1,0:T(8,128)(2,1)S(1)}, bf16[1,384,3072]{2,1,0:T(8,128)(2,1)}, u32[]{:S(2)}) copy-start(bf16[1,384,3072]{2,1,0:T(8,128)(2,1)} %param.8) | copy-start | bytes 7077892
  1.4 6.0 %copy-start.3 = (bf16[1,512,384]{2,1,0:T(8,128)(2,1)S(1)}, bf16[1,512,384]{2,1,0:T(8,128)(2,1)}, u32[]{:S(2)}) copy-start(bf16[1,512,384]{2,1,0:T(8,128)(2,1)} %param.6) | copy-start | bytes 1179652
  7.3 3.8 %copy-start = (f32[2,512,128]{2,1,0:T(8,128)}, f32[2,512,128]{2,1,0:T(8,128)S(1)}, u32[]{:S(2)}) copy-start(f32[2,512,128]{2,1,0:T(8,128)S(1)} %get-tuple-element.41.stats) | copy-start | bytes 1572868
  11.1 69.9 %all-to-all-start.1 = ((bf16[8,520,384]{2,1,0:T(8,128)(2,1)}), bf16[8,520,384]{2,1,0:T(8,128)(2,1)}, u32[]{:S(2)}, u32[]{:S(2)}) async-start(bf16[8,520,384]{2,1,0:T(8,128)(2,1)} %shard_map.87), calls=%async_computation.1 | async-start | bytes 6389760 | tf_op jit(solution)/shard_map/all_to_all | solution.py:277
  17.0 7.0 %collective-permute-start = (bf16[32,3072]{1,0:T(8,128)(2,1)S(1)}, bf16[32,3072]{1,0:T(8,128)(2,1)S(1)}, u32[]{:S(2)}, u32[]{:S(2)}) collective-permute-start(bf16[32,3072]{1,0:T(8,128)(2,1)S(1)} %get-tuple-element.29), channel_id=1, source_target_pairs={{0,4},{4,0},{8,12},{12,8},{16,20},{20,16},{24,28},{28,24},{32,36},... | collective-permute-start | bytes 589832 | tf_op jit(solution)/shard_map/ppermute | solution.py:220
  24.1 17.0 %collective-permute-start.6 = (bf16[32,3072]{1,0:T(8,128)(2,1)S(1)}, bf16[32,3072]{1,0:T(8,128)(2,1)S(1)}, u32[]{:S(2)}, u32[]{:S(2)}) collective-permute-start(bf16[32,3072]{1,0:T(8,128)(2,1)S(1)} %get-tuple-element.35), channel_id=1, source_target_pairs={{0,4},{4,0},{8,12},{12,8},{16,20},{20,16},{24,28},{28,24},{32,36},... | collective-permute-start | bytes 589832 | tf_op jit(solution)/shard_map/ppermute | solution.py:220
  27.9 16.6 %collective-permute-start.1 = (bf16[32,3072]{1,0:T(8,128)(2,1)S(1)}, bf16[32,3072]{1,0:T(8,128)(2,1)S(1)}, u32[]{:S(2)}, u32[]{:S(2)}) collective-permute-start(bf16[32,3072]{1,0:T(8,128)(2,1)S(1)} %shard_map.78), channel_id=1, source_target_pairs={{4,8},{8,4},{12,16},{16,12},{20,24},{24,20},{28,32},{32,28},{36,40... | collective-permute-start | bytes 589832 | tf_op jit(solution)/shard_map/ppermute | solution.py:220
  44.6 8.0 %collective-permute-start.7 = (bf16[32,3072]{1,0:T(8,128)(2,1)S(1)}, bf16[32,3072]{1,0:T(8,128)(2,1)S(1)}, u32[]{:S(2)}, u32[]{:S(2)}) collective-permute-start(bf16[32,3072]{1,0:T(8,128)(2,1)S(1)} %shard_map.83), channel_id=1, source_target_pairs={{4,8},{8,4},{12,16},{16,12},{20,24},{24,20},{28,32},{32,28},{36,40... | collective-permute-start | bytes 589832 | tf_op jit(solution)/shard_map/ppermute | solution.py:220
  49.2 6.4 %collective-permute-start.2 = (bf16[32,3072]{1,0:T(8,128)(2,1)S(1)}, bf16[32,3072]{1,0:T(8,128)(2,1)S(1)}, u32[]{:S(2)}, u32[]{:S(2)}) collective-permute-start(bf16[32,3072]{1,0:T(8,128)(2,1)S(1)} %shard_map.79), channel_id=1, source_target_pairs={{0,4},{4,0},{8,12},{12,8},{16,20},{20,16},{24,28},{28,24},{32,36},... | collective-permute-start | bytes 589832 | tf_op jit(solution)/shard_map/ppermute | solution.py:220
  55.7 6.4 %collective-permute-start.8 = (bf16[32,3072]{1,0:T(8,128)(2,1)S(1)}, bf16[32,3072]{1,0:T(8,128)(2,1)S(1)}, u32[]{:S(2)}, u32[]{:S(2)}) collective-permute-start(bf16[32,3072]{1,0:T(8,128)(2,1)S(1)} %shard_map.84), channel_id=1, source_target_pairs={{0,4},{4,0},{8,12},{12,8},{16,20},{20,16},{24,28},{28,24},{32,36},... | collective-permute-start | bytes 589832 | tf_op jit(solution)/shard_map/ppermute | solution.py:220
  58.1 7.6 %collective-permute-start.3 = (bf16[32,3072]{1,0:T(8,128)(2,1)S(1)}, bf16[32,3072]{1,0:T(8,128)(2,1)S(1)}, u32[]{:S(2)}, u32[]{:S(2)}) collective-permute-start(bf16[32,3072]{1,0:T(8,128)(2,1)S(1)} %shard_map.80), channel_id=1, source_target_pairs={{4,8},{8,4},{12,16},{16,12},{20,24},{24,20},{28,32},{32,28},{36,40... | collective-permute-start | bytes 589832 | tf_op jit(solution)/shard_map/ppermute | solution.py:220
  65.7 7.6 %collective-permute-start.9 = (bf16[32,3072]{1,0:T(8,128)(2,1)S(1)}, bf16[32,3072]{1,0:T(8,128)(2,1)S(1)}, u32[]{:S(2)}, u32[]{:S(2)}) collective-permute-start(bf16[32,3072]{1,0:T(8,128)(2,1)S(1)} %shard_map.85), channel_id=1, source_target_pairs={{4,8},{8,4},{12,16},{16,12},{20,24},{24,20},{28,32},{32,28},{36,40... | collective-permute-start | bytes 589832 | tf_op jit(solution)/shard_map/ppermute | solution.py:220
  68.1 6.4 %collective-permute-start.4 = (bf16[32,3072]{1,0:T(8,128)(2,1)S(1)}, bf16[32,3072]{1,0:T(8,128)(2,1)S(1)}, u32[]{:S(2)}, u32[]{:S(2)}) collective-permute-start(bf16[32,3072]{1,0:T(8,128)(2,1)S(1)} %shard_map.81), channel_id=1, source_target_pairs={{0,4},{4,0},{8,12},{12,8},{16,20},{20,16},{24,28},{28,24},{32,36},... | collective-permute-start | bytes 589832 | tf_op jit(solution)/shard_map/ppermute | solution.py:220
  74.6 19.8 %collective-permute-start.10 = (bf16[32,3072]{1,0:T(8,128)(2,1)S(1)}, bf16[32,3072]{1,0:T(8,128)(2,1)S(1)}, u32[]{:S(2)}, u32[]{:S(2)}) collective-permute-start(bf16[32,3072]{1,0:T(8,128)(2,1)S(1)} %shard_map.86), channel_id=1, source_target_pairs={{0,4},{4,0},{8,12},{12,8},{16,20},{20,16},{24,28},{28,24},{32,36},... | collective-permute-start | bytes 589832 | tf_op jit(solution)/shard_map/ppermute | solution.py:220
  76.6 17.8 %collective-permute-start.5 = (bf16[32,3072]{1,0:T(8,128)(2,1)S(1)}, bf16[32,3072]{1,0:T(8,128)(2,1)S(1)}, u32[]{:S(2)}, u32[]{:S(2)}) collective-permute-start(bf16[32,3072]{1,0:T(8,128)(2,1)S(1)} %shard_map.82), channel_id=1, source_target_pairs={{4,8},{8,4},{12,16},{16,12},{20,24},{24,20},{28,32},{32,28},{36,40... | collective-permute-start | bytes 589832 | tf_op jit(solution)/shard_map/ppermute | solution.py:220
  85.1 26.5 %collective-permute-start.11 = (bf16[512,384]{1,0:T(8,128)(2,1)S(1)}, bf16[512,384]{1,0:T(8,128)(2,1)S(1)}, u32[]{:S(2)}, u32[]{:S(2)}) collective-permute-start(bf16[512,384]{1,0:T(8,128)(2,1)S(1)} %get-tuple-element.42), channel_id=1, source_target_pairs={{384,0},{385,1},{386,2},{387,3},{388,4},{389,5},{390,6},{391,7},{3... | collective-permute-start | bytes 1179656 | tf_op jit(solution)/shard_map/ppermute | solution.py:279
  95.1 15.8 %all-to-all-start = ((bf16[4,8,3072]{2,1,0:T(8,128)(2,1)}), bf16[4,8,3072]{2,1,0:T(8,128)(2,1)S(1)}, u32[]{:S(2)}, u32[]{:S(2)}) async-start(bf16[4,8,3072]{2,1,0:T(8,128)(2,1)} %fusion.2), calls=%async_computation | async-start | bytes 393216 | tf_op jit(solution)/shard_map/all_to_all | solution.py:265

commit v6 on v5

--- a/solution.py
+++ b/solution.py
@@ -1,3 +1,5 @@
+import functools
+
 import jax
 import jax.numpy as jnp
 from jax import lax
@@ -23,6 +25,9 @@
 PARTS = 8
 EXTRA = 8
 COLS = 512
+HALF = WIDTH // 2
+KEEP = (7, 4, 9, 2, 11)
+GIVE = (5, 8, 3, 10, 1)
 
 
 def in_hbm(*arrays):
@@ -30,7 +35,7 @@
 
 
 def front_kernel(scal, stream, value_grad_from, gain_from, held, stats, own, *rest):
-    blocks, (normed, grad, value_grad, gain, sems) = rest[:-5], rest[-5:]
+    keep_half, give_half, keep, give, normed, grad, value_grad, gain, sems = rest
     per = TOK // BLOCK
     gain_here = pltpu.make_async_copy(gain_from, gain, sems.at[per])
     gain_here.start()
@@ -73,19 +78,32 @@
     for n in range(WIDTH // COLS):
         cols = slice(n * COLS, (n + 1) * COLS)
         grad[...] = jnp.dot(left, normed[:, cols], preferred_element_type=F32)
-        for r in range(RING):
+
+        def piece(r):
             at = lax.rem(scal[0] + r * scal[1] + RING, RING) * ROWS
-            piece = grad[pl.ds(pl.multiple_of(at, ROWS), ROWS), :]
-            if r == 0:
-                own[:, cols] = piece
-            else:
-                blocks[r - 1][:, cols] = piece.astype(BF16)
+            return grad[pl.ds(pl.multiple_of(at, ROWS), ROWS), :]
+
+        own[:, cols] = piece(0)
+        for j, (mine, other) in enumerate(zip(KEEP, GIVE)):
+            keep[j, :, cols] = piece(mine).astype(BF16)
+            give[j, :, cols] = piece(other).astype(BF16)
+        within = slice(n * COLS % HALF, n * COLS % HALF + COLS)
+        far = piece(RING // 2).astype(BF16)
+        kept = scal[4] == n * COLS // HALF
+
+        @pl.when(kept)
+        def _():
+            keep_half[:, within] = far
+
+        @pl.when(jnp.logical_not(kept))
+        def _():
+            give_half[:, within] = far
 
 
 def front(scal, stream, value_grad, gain):
     vmem = pl.BlockSpec(memory_space=pltpu.VMEM)
     out = [((TOK, WIDTH), BF16), ((2, TOK, 128), F32), ((ROWS, WIDTH), F32)]
-    out += [((ROWS, WIDTH), BF16)] * (RING - 1)
+    out += [((ROWS, HALF), BF16)] * 2 + [((len(KEEP), ROWS, WIDTH), BF16)] * 2
     return pl.pallas_call(
         front_kernel,
         in_specs=[
@@ -215,48 +233,50 @@
 def swapped(value, link):
     peers = lax.axis_size("dz")
     pairs = []
-    for i in range(link, peers, 2):
-        pairs += [(i, (i + 1) % peers), ((i + 1) % peers, i)]
-    return lax.ppermute(value, "dz", pairs)
-
-
-def tied(value, *others):
-    return lax.optimization_barrier((value, *others))[0]
-
-
-def joined_kernel(own, got, out):
-    out[...] = (own[...].astype(F32) + got[...].astype(F32)).astype(BF16)
-
-
-def joined(own, got):
+    for section in range(2):
+        for i in range((link + section) % 2, peers, 2):
+            here, there = section * peers + i, section * peers + (i + 1) % peers
+            pairs += [(here, there), (there, here)]
+    return lax.ppermute(value, ("section", "dz"), pairs)
+
+
+def traded(value):
+    return lax.ppermute(value, "section", [(0, 1), (1, 0)])
+
+
+def half_kernel(scal, keep, taken, got, out):
+    out[0] = keep[0]
+    out[1] = taken[0]
+    cols = pl.ds(pl.multiple_of(scal[4] * HALF, 128), HALF)
+    out[0, :, cols] = (keep[0, :, cols].astype(F32) + got[0].astype(F32)).astype(BF16)
+    out[1, :, cols] = (taken[0, :, cols].astype(F32) + got[1].astype(F32)).astype(BF16)
+
+
+def whole_kernel(j, scal, keep, taken, got, out):
+    out[0] = (keep[j].astype(F32) + got[0].astype(F32)).astype(BF16)
+    out[1] = (taken[j].astype(F32) + got[1].astype(F32)).astype(BF16)
+
+
+def joined(j, scal, keep, taken, got):
     vmem = pl.BlockSpec(memory_space=pltpu.VMEM)
     return pl.pallas_call(
-        joined_kernel,
-        in_specs=[vmem, vmem],
+        functools.partial(whole_kernel, j) if j else half_kernel,
+        in_specs=[pl.BlockSpec(memory_space=pltpu.SMEM), vmem, vmem, vmem],
         out_specs=vmem,
-        out_shape=jax.ShapeDtypeStruct(own.shape, BF16),
+        out_shape=jax.ShapeDtypeStruct((2, ROWS, WIDTH), BF16),
         compiler_params=pltpu.CompilerParams(vmem_limit_bytes=4 * 1024 * 1024),
-    )(own, got)
-
-
-def sum_over_z(own, blocks):
-    def block(link, distance):
-        return blocks[(distance if link == 0 else RING - distance) - 1]
-
-    far = RING // 2
-    long = swapped(block(0, far), 0)
-    short = None
-    link = 0
-    for k in range(far - 1, 0, -1):
-        link = 1 - link
-        if short is None:
-            mine_short = tied(block(1 - link, k), long)
-        else:
-            mine_short = joined(block(1 - link, k), tied(short, long))
-        mine = joined(block(link, k), long)
-        long = swapped(mine, link)
-        short = swapped(mine_short, 1 - link)
-    return own + long.astype(F32) + short.astype(F32)
+    )(scal, keep, taken, got)
+
+
+def sum_over_z(scal, own, keep_half, give_half, keep, give):
+    taken_half = traded(give_half)
+    got = swapped(jnp.stack([keep_half, taken_half]), 0)
+    taken = traded(give)
+    for j in range(len(KEEP)):
+        message = joined(j, scal, keep, taken, got)
+        got = swapped(message, (j + 1) % 2)
+    other = traded(got[1])
+    return own + got[0].astype(F32) + other.astype(F32)
 
 
 def sum_over_y(rows_sum):
@@ -270,9 +290,10 @@
     section_index = lax.axis_index("section")
     model_index = lax.axis_index(MP)
     place = lax.axis_index("dz")
-    scal = jnp.stack([place, 1 - 2 * (place % 2), model_index, counts[0]]).astype(jnp.int32)
-    held, stats, own, *blocks = front(scal, stream[0], value_grad[0], gain)
-    weight_grad = sum_over_y(sum_over_z(own, blocks)).astype(BF16)[None]
+    ahead = 1 - 2 * ((place + section_index) % 2)
+    scal = jnp.stack([place, ahead, model_index, counts[0], section_index]).astype(jnp.int32)
+    held, stats, *blocks = front(scal, stream[0], value_grad[0], gain)
+    weight_grad = sum_over_y(sum_over_z(scal, *blocks)).astype(BF16)[None]
     tiles = parts(value_grad[0], weights[0], held, gain, stats)
     arrived = lax.all_to_all(tiles, MP, split_axis=0, concat_axis=0, tiled=True)
     norm_back, above_grad = backward(scal, arrived, stream[0], stats, gain, top_grad)

time: 113 us -> 123 us (1.088)
  waiting for transfers between devices: 31 us -> 45.3 us
  starting transfers between devices: 63.4 us -> 55.4 us
  Pallas kernels: 14.2 us -> 17.9 us
    ppermute x11 -> x9, waiting for transfers between devices: 21.2 us -> 35.5 us  [the longest x6 34.2 us: swapped(): return lax.ppermute(value, ('section', 'dz'), pairs)]
    ppermute x1, starting transfers between devices: 9.24 us -> 1.94 us  [shards(): below_grad = lax.ppermute(above_grad, 'section', [(1, 0)])]
    pallas_call x9 -> x5, Pallas kernels: 0.44 us -> 3.15 us  [joined(): pl.pallas_call(functools.partial(whole_kernel, j) if j else half_kernel,...]
    ppermute x11 -> x9, starting transfers between devices: 42.3 us -> 41.6 us  [the longest x6 21.5 us: swapped(): return lax.ppermute(value, ('section', 'dz'), pairs)]
  transfers between devices with their start and end apart: 14 -> 12, of which waited for: 9 -> 8; matrix products, arithmetic and copies ran while one was open for 1% -> 1% of each run, Pallas kernels for 4% -> 6%
where the time goes in v6:
time: 123 us; the launch traced here: 122 us
  starting transfers between devices  55.4 us (45%)
  waiting for transfers between devices  45.3 us (37%)
  Pallas kernels  17.9 us (15%)
  other arithmetic  2.29 us (2%)
  between operations  1.51 us (1%)
    ppermute x6, waiting for transfers between devices, swapped(): return lax.ppermute(value, ('section', 'dz'), pairs)  34.2 us
    ppermute x6, starting transfers between devices, swapped(): return lax.ppermute(value, ('section', 'dz'), pairs)  21.5 us
    ppermute x3, starting transfers between devices, traded(): return lax.ppermute(value, 'section', [(0, 1), (1, 0)])  20.1 us
    all_to_all x1, waiting for transfers between devices, sum_over_y(): lax.all_to_all(tiles, 'dy', split_axis=0, concat_axis=0, tiled=True)  9.83 us
    pallas_call x1, Pallas kernels, front(): pl.pallas_call(front_kernel, in_specs=[pl.BlockSpec(memory_space=pltpu.SM...  6.91 us
    all_to_all x1, starting transfers between devices, sum_over_y(): lax.all_to_all(tiles, 'dy', split_axis=0, concat_axis=0, tiled=True)  5.98 us
    all_to_all x1, starting transfers between devices, shards(): arrived = lax.all_to_all(tiles, MP, split_axis=0, concat_axis=0, tiled=True)  5.87 us
    pallas_call x1, Pallas kernels, backward(): pl.pallas_call(back_kernel, grid_spec=pltpu.PrefetchScalarGridSpec(num_sc...  4.05 us
  transfers between devices with their start and end apart: 12, of which 8 were waited for; matrix products, arithmetic and copies ran while one was open for 1% of the time, Pallas kernels for 6%

profile of v6, /device:TPU:1, one launch (start us, length us, event | category | flops | bytes accessed | tf_op | source)
XLA Modules:
  0.0 122.5 jit_solution(316843879933885312)
XLA Ops:
  1.3 0.1 stack.28.scal
  1.4 0.0 copy-start.1
  1.4 0.0 copy-start.2
  1.4 0.0 copy-start.3
  1.4 6.9 %shard_map.77 = (bf16[512,3072]{1,0:T(8,128)(2,1)S(1)}, f32[2,512,128]{2,1,0:T(8,128)S(1)}, f32[32,3072]{1,0:T(8,128)S(1)}, bf16[32,1536]{1,0:T(8,128)(2,1)S(1)}...) custom-call(s32[5]{0:T(128)S(1)} %stack.28.scal, ...), custom_call_target="tpu_custom_call" | custom-call | flops 4831838208 | bytes 8000000 | tf_op jit(solution)/shard_map/pallas_call | solution.py:107
  8.3 0.0 copy-start
  8.3 0.0 copy-done.1
  8.3 0.0 copy-done.2
  8.3 0.0 copy-done.3
  8.3 3.8 %shard_map.83 = bf16[8,520,384]{2,1,0:T(8,128)(2,1)} custom-call(bf16[512,384]{1,0:T(8,128)(2,1)S(1)} %bitcast.24, bf16[384,3072]{1,0:T(8,128)(2,1)S(1)} %bitcast.22, bf16[512,3072]{1,0:T(8,128)(2,1)S(1)} %get-tuple-element.16.held, f32[1,3072]{1,0:T(1,128)S(1)} %copy-done.1, f32[2,512,128]{2,1,0:T(8,128)S(1)} %get-tuple-element.17.stats), custom_call_target="tpu_custom_call" | custom-call | flops 3623878656 | bytes 9000000 | tf_op jit(solution)/shard_map/pallas_call | solution.py:166
  12.1 0.0 copy-done
  12.1 5.9 %all-to-all-start.1 = ((bf16[8,520,384]{2,1,0:T(8,128)(2,1)}), bf16[8,520,384]{2,1,0:T(8,128)(2,1)}, u32[]{:S(2)}, u32[]{:S(2)}) async-start(bf16[8,520,384]{2,1,0:T(8,128)(2,1)} %shard_map.83), calls=%async_computation.1 | async-start | bytes 6389760 | tf_op jit(solution)/shard_map/all_to_all | solution.py:298
  18.0 11.0 %collective-permute-start = (bf16[5,32,3072]{2,1,0:T(8,128)(2,1)S(1)}, bf16[5,32,3072]{2,1,0:T(8,128)(2,1)S(1)}, u32[]{:S(2)}, u32[]{:S(2)}) collective-permute-start(bf16[5,32,3072]{2,1,0:T(8,128)(2,1)S(1)} %get-tuple-element.13), channel_id=1, source_target_pairs={{0,384},{384,0},{1,385},{385,1},{2,386},{386,2},{3,387},{387,3},{4... | collective-permute-start | bytes 2949128 | tf_op jit(solution)/shard_map/ppermute | solution.py:244
  29.0 1.9 %collective-permute-start.1 = (bf16[32,1536]{1,0:T(8,128)(2,1)S(1)}, bf16[32,1536]{1,0:T(8,128)(2,1)S(1)}, u32[]{:S(2)}, u32[]{:S(2)}) collective-permute-start(bf16[32,1536]{1,0:T(8,128)(2,1)S(1)} %get-tuple-element.15), channel_id=1, source_target_pairs={{0,384},{384,0},{1,385},{385,1},{2,386},{386,2},{3,387},{387,3},{4... | collective-permute-start | bytes 294920 | tf_op jit(solution)/shard_map/ppermute | solution.py:244
  30.9 1.3 %collective-permute-done.1 = bf16[32,1536]{1,0:T(8,128)(2,1)S(1)} collective-permute-done((bf16[32,1536]{1,0:T(8,128)(2,1)S(1)}, bf16[32,1536]{1,0:T(8,128)(2,1)S(1)}, u32[]{:S(2)}, u32[]{:S(2)}) %collective-permute-start.1) | collective-permute-done | bytes 98336 | tf_op jit(solution)/shard_map/ppermute | solution.py:244
  32.2 6.2 %collective-permute-start.2 = (bf16[2,32,1536]{2,1,0:T(8,128)(2,1)S(1)}, bf16[2,32,1536]{2,1,0:T(8,128)(2,1)S(1)}, u32[]{:S(2)}, u32[]{:S(2)}) collective-permute-start(bf16[2,32,1536]{2,1,0:T(8,128)(2,1)S(1)} %pad_maximum_fusion), channel_id=1, source_target_pairs={{0,4},{4,0},{8,12},{12,8},{16,20},{20,16},{24,28},{28,24},{32,36},... | collective-permute-start | bytes 589832 | tf_op jit(solution)/shard_map/ppermute | solution.py:240
  38.4 3.4 %collective-permute-done.2.got = bf16[2,32,1536]{2,1,0:T(8,128)(2,1)S(1)} collective-permute-done((bf16[2,32,1536]{2,1,0:T(8,128)(2,1)S(1)}, bf16[2,32,1536]{2,1,0:T(8,128)(2,1)S(1)}, u32[]{:S(2)}, u32[]{:S(2)}) %collective-permute-start.2) | collective-permute-done | bytes 196640 | tf_op jit(solution)/shard_map/ppermute | solution.py:240
  41.8 0.0 collective-permute-done.taken
  41.8 0.6 shard_map.78
  42.5 1.9 %collective-permute-start.3 = (bf16[2,32,3072]{2,1,0:T(8,128)(2,1)S(1)}, bf16[2,32,3072]{2,1,0:T(8,128)(2,1)S(1)}, u32[]{:S(2)}, u32[]{:S(2)}) collective-permute-start(bf16[2,32,3072]{2,1,0:T(8,128)(2,1)S(1)} %shard_map.78), channel_id=1, source_target_pairs={{4,8},{8,4},{12,16},{16,12},{20,24},{24,20},{28,32},{32,28},{36,40... | collective-permute-start | bytes 1179656 | tf_op jit(solution)/shard_map/ppermute | solution.py:240
  44.4 7.0 %collective-permute-done.3.got = bf16[2,32,3072]{2,1,0:T(8,128)(2,1)S(1)} collective-permute-done((bf16[2,32,3072]{2,1,0:T(8,128)(2,1)S(1)}, bf16[2,32,3072]{2,1,0:T(8,128)(2,1)S(1)}, u32[]{:S(2)}, u32[]{:S(2)}) %collective-permute-start.3) | collective-permute-done | bytes 393248 | tf_op jit(solution)/shard_map/ppermute | solution.py:240
  51.4 0.6 shard_map.79
  52.0 4.6 %collective-permute-start.4 = (bf16[2,32,3072]{2,1,0:T(8,128)(2,1)S(1)}, bf16[2,32,3072]{2,1,0:T(8,128)(2,1)S(1)}, u32[]{:S(2)}, u32[]{:S(2)}) collective-permute-start(bf16[2,32,3072]{2,1,0:T(8,128)(2,1)S(1)} %shard_map.79), channel_id=1, source_target_pairs={{0,4},{4,0},{8,12},{12,8},{16,20},{20,16},{24,28},{28,24},{32,36},... | collective-permute-start | bytes 1179656 | tf_op jit(solution)/shard_map/ppermute | solution.py:240
  56.6 5.2 %collective-permute-done.4.got = bf16[2,32,3072]{2,1,0:T(8,128)(2,1)S(1)} collective-permute-done((bf16[2,32,3072]{2,1,0:T(8,128)(2,1)S(1)}, bf16[2,32,3072]{2,1,0:T(8,128)(2,1)S(1)}, u32[]{:S(2)}, u32[]{:S(2)}) %collective-permute-start.4) | collective-permute-done | bytes 393248 | tf_op jit(solution)/shard_map/ppermute | solution.py:240
  61.8 0.6 shard_map.80
  62.4 1.9 %collective-permute-start.5 = (bf16[2,32,3072]{2,1,0:T(8,128)(2,1)S(1)}, bf16[2,32,3072]{2,1,0:T(8,128)(2,1)S(1)}, u32[]{:S(2)}, u32[]{:S(2)}) collective-permute-start(bf16[2,32,3072]{2,1,0:T(8,128)(2,1)S(1)} %shard_map.80), channel_id=1, source_target_pairs={{4,8},{8,4},{12,16},{16,12},{20,24},{24,20},{28,32},{32,28},{36,40... | collective-permute-start | bytes 1179656 | tf_op jit(solution)/shard_map/ppermute | solution.py:240
  64.3 6.9 %collective-permute-done.5.got = bf16[2,32,3072]{2,1,0:T(8,128)(2,1)S(1)} collective-permute-done((bf16[2,32,3072]{2,1,0:T(8,128)(2,1)S(1)}, bf16[2,32,3072]{2,1,0:T(8,128)(2,1)S(1)}, u32[]{:S(2)}, u32[]{:S(2)}) %collective-permute-start.5) | collective-permute-done | bytes 393248 | tf_op jit(solution)/shard_map/ppermute | solution.py:240
  71.2 0.6 shard_map.81
  71.9 5.0 %collective-permute-start.6 = (bf16[2,32,3072]{2,1,0:T(8,128)(2,1)S(1)}, bf16[2,32,3072]{2,1,0:T(8,128)(2,1)S(1)}, u32[]{:S(2)}, u32[]{:S(2)}) collective-permute-start(bf16[2,32,3072]{2,1,0:T(8,128)(2,1)S(1)} %shard_map.81), channel_id=1, source_target_pairs={{0,4},{4,0},{8,12},{12,8},{16,20},{20,16},{24,28},{28,24},{32,36},... | collective-permute-start | bytes 1179656 | tf_op jit(solution)/shard_map/ppermute | solution.py:240
  76.8 5.2 %collective-permute-done.6.got = bf16[2,32,3072]{2,1,0:T(8,128)(2,1)S(1)} collective-permute-done((bf16[2,32,3072]{2,1,0:T(8,128)(2,1)S(1)}, bf16[2,32,3072]{2,1,0:T(8,128)(2,1)S(1)}, u32[]{:S(2)}, u32[]{:S(2)}) %collective-permute-start.6) | collective-permute-done | bytes 393248 | tf_op jit(solution)/shard_map/ppermute | solution.py:240
  82.0 0.6 shard_map.82
  82.6 1.9 %collective-permute-start.7 = (bf16[2,32,3072]{2,1,0:T(8,128)(2,1)S(1)}, bf16[2,32,3072]{2,1,0:T(8,128)(2,1)S(1)}, u32[]{:S(2)}, u32[]{:S(2)}) collective-permute-start(bf16[2,32,3072]{2,1,0:T(8,128)(2,1)S(1)} %shard_map.82), channel_id=1, source_target_pairs={{4,8},{8,4},{12,16},{16,12},{20,24},{24,20},{28,32},{32,28},{36,40... | collective-permute-start | bytes 1179656 | tf_op jit(solution)/shard_map/ppermute | solution.py:240
  84.6 6.6 %collective-permute-done.7 = bf16[2,32,3072]{2,1,0:T(8,128)(2,1)S(1)} collective-permute-done((bf16[2,32,3072]{2,1,0:T(8,128)(2,1)S(1)}, bf16[2,32,3072]{2,1,0:T(8,128)(2,1)S(1)}, u32[]{:S(2)}, u32[]{:S(2)}) %collective-permute-start.7) | collective-permute-done | bytes 393248 | tf_op jit(solution)/shard_map/ppermute | solution.py:240
  91.2 7.2 %collective-permute-start.8 = (bf16[32,3072]{1,0:T(8,128)(2,1)S(1)}, bf16[32,3072]{1,0:T(8,128)(2,1)S(1)}, u32[]{:S(2)}, u32[]{:S(2)}) collective-permute-start(bf16[32,3072]{1,0:T(8,128)(2,1)S(1)} %slice_bitcast_fusion), channel_id=1, source_target_pairs={{0,384},{384,0},{1,385},{385,1},{2,386},{386,2},{3,387},{387,3},{4... | collective-permute-start | bytes 589832 | tf_op jit(solution)/shard_map/ppermute | solution.py:244
  98.4 0.0 all-to-all-done.1.arrived.extra
  98.4 4.1 %shard_map.84 = (f32[512,384]{1,0:T(8,128)S(1)}, bf16[512,384]{1,0:T(8,128)(2,1)S(1)}) custom-call(s32[5]{0:T(128)S(1)} %stack.28.scal, bf16[8,520,384]{2,1,0:T(8,128)(2,1)} %all-to-all-done.1.arrived.extra, bf16[8,520,384]{2,1,0:T(8,128)(2,1)} %all-to-all-done.1.arrived.extra, bf16[512,3072]{1,0:T(8,128)(2,1)} %bitcast.26, f32[2,512,128]{2,1,0:T(8,128)} %copy-done, ...), custom_call_target="tpu_custom_call" | custom-call | flops 500000000 | bytes 6000000 | tf_op jit(solution)/shard_map/pallas_call | solution.py:209
  102.4 1.9 %collective-permute-start.9 = (bf16[512,384]{1,0:T(8,128)(2,1)S(1)}, bf16[512,384]{1,0:T(8,128)(2,1)S(1)}, u32[]{:S(2)}, u32[]{:S(2)}) collective-permute-start(bf16[512,384]{1,0:T(8,128)(2,1)S(1)} %get-tuple-element.18), channel_id=1, source_target_pairs={{384,0},{385,1},{386,2},{387,3},{388,4},{389,5},{390,6},{391,7},{3... | collective-permute-start | bytes 1179656 | tf_op jit(solution)/shard_map/ppermute | solution.py:300
  104.4 0.0 collective-permute-done.8
  104.4 0.7 fusion.4
  105.1 6.0 %all-to-all-start = ((bf16[4,8,3072]{2,1,0:T(8,128)(2,1)}), bf16[4,8,3072]{2,1,0:T(8,128)(2,1)S(1)}, u32[]{:S(2)}, u32[]{:S(2)}) async-start(bf16[4,8,3072]{2,1,0:T(8,128)(2,1)} %fusion.4), calls=%async_computation | async-start | bytes 393216 | tf_op jit(solution)/shard_map/all_to_all | solution.py:285
  111.1 9.8 %all-to-all-done = bf16[4,8,3072]{2,1,0:T(8,128)(2,1)S(1)} async-done(((bf16[4,8,3072]{2,1,0:T(8,128)(2,1)}), bf16[4,8,3072]{2,1,0:T(8,128)(2,1)S(1)}, u32[]{:S(2)}, u32[]{:S(2)}) %all-to-all-start) | async-done | bytes 196640 | tf_op jit(solution)/shard_map/all_to_all | solution.py:285
  121.0 0.7 reduce_sum.12
  121.6 0.0 collective-permute-done.9
  121.6 0.9 fusion.1
  (2 shorter events, 0.0 us)
Async XLA Ops:
  1.4 6.9 %copy-start.1 = (f32[1,3072]{1,0:T(1,128)S(1)}, f32[1,3072]{1,0:T(1,128)}, u32[]{:S(2)}) copy-start(f32[1,3072]{1,0:T(1,128)} %gain.3) | copy-start | bytes 36868
  1.4 6.9 %copy-start.2 = (bf16[1,384,3072]{2,1,0:T(8,128)(2,1)S(1)}, bf16[1,384,3072]{2,1,0:T(8,128)(2,1)}, u32[]{:S(2)}) copy-start(bf16[1,384,3072]{2,1,0:T(8,128)(2,1)} %param.8) | copy-start | bytes 7077892
  1.4 7.0 %copy-start.3 = (bf16[1,512,384]{2,1,0:T(8,128)(2,1)S(1)}, bf16[1,512,384]{2,1,0:T(8,128)(2,1)}, u32[]{:S(2)}) copy-start(bf16[1,512,384]{2,1,0:T(8,128)(2,1)} %param.6) | copy-start | bytes 1179652
  8.3 3.8 %copy-start = (f32[2,512,128]{2,1,0:T(8,128)}, f32[2,512,128]{2,1,0:T(8,128)S(1)}, u32[]{:S(2)}) copy-start(f32[2,512,128]{2,1,0:T(8,128)S(1)} %get-tuple-element.17.stats) | copy-start | bytes 1572868
  12.1 86.2 %all-to-all-start.1 = ((bf16[8,520,384]{2,1,0:T(8,128)(2,1)}), bf16[8,520,384]{2,1,0:T(8,128)(2,1)}, u32[]{:S(2)}, u32[]{:S(2)}) async-start(bf16[8,520,384]{2,1,0:T(8,128)(2,1)} %shard_map.83), calls=%async_computation.1 | async-start | bytes 6389760 | tf_op jit(solution)/shard_map/all_to_all | solution.py:298
  18.0 23.8 %collective-permute-start = (bf16[5,32,3072]{2,1,0:T(8,128)(2,1)S(1)}, bf16[5,32,3072]{2,1,0:T(8,128)(2,1)S(1)}, u32[]{:S(2)}, u32[]{:S(2)}) collective-permute-start(bf16[5,32,3072]{2,1,0:T(8,128)(2,1)S(1)} %get-tuple-element.13), channel_id=1, source_target_pairs={{0,384},{384,0},{1,385},{385,1},{2,386},{386,2},{3,387},{387,3},{4... | collective-permute-start | bytes 2949128 | tf_op jit(solution)/shard_map/ppermute | solution.py:244
  29.0 3.2 %collective-permute-start.1 = (bf16[32,1536]{1,0:T(8,128)(2,1)S(1)}, bf16[32,1536]{1,0:T(8,128)(2,1)S(1)}, u32[]{:S(2)}, u32[]{:S(2)}) collective-permute-start(bf16[32,1536]{1,0:T(8,128)(2,1)S(1)} %get-tuple-element.15), channel_id=1, source_target_pairs={{0,384},{384,0},{1,385},{385,1},{2,386},{386,2},{3,387},{387,3},{4... | collective-permute-start | bytes 294920 | tf_op jit(solution)/shard_map/ppermute | solution.py:244
  32.2 9.6 %collective-permute-start.2 = (bf16[2,32,1536]{2,1,0:T(8,128)(2,1)S(1)}, bf16[2,32,1536]{2,1,0:T(8,128)(2,1)S(1)}, u32[]{:S(2)}, u32[]{:S(2)}) collective-permute-start(bf16[2,32,1536]{2,1,0:T(8,128)(2,1)S(1)} %pad_maximum_fusion), channel_id=1, source_target_pairs={{0,4},{4,0},{8,12},{12,8},{16,20},{20,16},{24,28},{28,24},{32,36},... | collective-permute-start | bytes 589832 | tf_op jit(solution)/shard_map/ppermute | solution.py:240
  42.5 8.9 %collective-permute-start.3 = (bf16[2,32,3072]{2,1,0:T(8,128)(2,1)S(1)}, bf16[2,32,3072]{2,1,0:T(8,128)(2,1)S(1)}, u32[]{:S(2)}, u32[]{:S(2)}) collective-permute-start(bf16[2,32,3072]{2,1,0:T(8,128)(2,1)S(1)} %shard_map.78), channel_id=1, source_target_pairs={{4,8},{8,4},{12,16},{16,12},{20,24},{24,20},{28,32},{32,28},{36,40... | collective-permute-start | bytes 1179656 | tf_op jit(solution)/shard_map/ppermute | solution.py:240
  52.0 9.7 %collective-permute-start.4 = (bf16[2,32,3072]{2,1,0:T(8,128)(2,1)S(1)}, bf16[2,32,3072]{2,1,0:T(8,128)(2,1)S(1)}, u32[]{:S(2)}, u32[]{:S(2)}) collective-permute-start(bf16[2,32,3072]{2,1,0:T(8,128)(2,1)S(1)} %shard_map.79), channel_id=1, source_target_pairs={{0,4},{4,0},{8,12},{12,8},{16,20},{20,16},{24,28},{28,24},{32,36},... | collective-permute-start | bytes 1179656 | tf_op jit(solution)/shard_map/ppermute | solution.py:240
  62.4 8.8 %collective-permute-start.5 = (bf16[2,32,3072]{2,1,0:T(8,128)(2,1)S(1)}, bf16[2,32,3072]{2,1,0:T(8,128)(2,1)S(1)}, u32[]{:S(2)}, u32[]{:S(2)}) collective-permute-start(bf16[2,32,3072]{2,1,0:T(8,128)(2,1)S(1)} %shard_map.80), channel_id=1, source_target_pairs={{4,8},{8,4},{12,16},{16,12},{20,24},{24,20},{28,32},{32,28},{36,40... | collective-permute-start | bytes 1179656 | tf_op jit(solution)/shard_map/ppermute | solution.py:240
  71.9 10.1 %collective-permute-start.6 = (bf16[2,32,3072]{2,1,0:T(8,128)(2,1)S(1)}, bf16[2,32,3072]{2,1,0:T(8,128)(2,1)S(1)}, u32[]{:S(2)}, u32[]{:S(2)}) collective-permute-start(bf16[2,32,3072]{2,1,0:T(8,128)(2,1)S(1)} %shard_map.81), channel_id=1, source_target_pairs={{0,4},{4,0},{8,12},{12,8},{16,20},{20,16},{24,28},{28,24},{32,36},... | collective-permute-start | bytes 1179656 | tf_op jit(solution)/shard_map/ppermute | solution.py:240
  82.6 8.5 %collective-permute-start.7 = (bf16[2,32,3072]{2,1,0:T(8,128)(2,1)S(1)}, bf16[2,32,3072]{2,1,0:T(8,128)(2,1)S(1)}, u32[]{:S(2)}, u32[]{:S(2)}) collective-permute-start(bf16[2,32,3072]{2,1,0:T(8,128)(2,1)S(1)} %shard_map.82), channel_id=1, source_target_pairs={{4,8},{8,4},{12,16},{16,12},{20,24},{24,20},{28,32},{32,28},{36,40... | collective-permute-start | bytes 1179656 | tf_op jit(solution)/shard_map/ppermute | solution.py:240
  91.2 13.2 %collective-permute-start.8 = (bf16[32,3072]{1,0:T(8,128)(2,1)S(1)}, bf16[32,3072]{1,0:T(8,128)(2,1)S(1)}, u32[]{:S(2)}, u32[]{:S(2)}) collective-permute-start(bf16[32,3072]{1,0:T(8,128)(2,1)S(1)} %slice_bitcast_fusion), channel_id=1, source_target_pairs={{0,384},{384,0},{1,385},{385,1},{2,386},{386,2},{3,387},{387,3},{4... | collective-permute-start | bytes 589832 | tf_op jit(solution)/shard_map/ppermute | solution.py:244
  102.4 19.2 %collective-permute-start.9 = (bf16[512,384]{1,0:T(8,128)(2,1)S(1)}, bf16[512,384]{1,0:T(8,128)(2,1)S(1)}, u32[]{:S(2)}, u32[]{:S(2)}) collective-permute-start(bf16[512,384]{1,0:T(8,128)(2,1)S(1)} %get-tuple-element.18), channel_id=1, source_target_pairs={{384,0},{385,1},{386,2},{387,3},{388,4},{389,5},{390,6},{391,7},{3... | collective-permute-start | bytes 1179656 | tf_op jit(solution)/shard_map/ppermute | solution.py:300
  105.1 15.8 %all-to-all-start = ((bf16[4,8,3072]{2,1,0:T(8,128)(2,1)}), bf16[4,8,3072]{2,1,0:T(8,128)(2,1)S(1)}, u32[]{:S(2)}, u32[]{:S(2)}) async-start(bf16[4,8,3072]{2,1,0:T(8,128)(2,1)} %fusion.4), calls=%async_computation | async-start | bytes 393216 | tf_op jit(solution)/shard_map/all_to_all | solution.py:285

commit v7 on v5

--- a/solution.py
+++ b/solution.py
@@ -239,7 +239,7 @@
     )(own, got)
 
 
-def sum_over_z(own, blocks):
+def sum_over_z(own, blocks, after):
     def block(link, distance):
         return blocks[(distance if link == 0 else RING - distance) - 1]
 
@@ -250,12 +250,13 @@
     for k in range(far - 1, 0, -1):
         link = 1 - link
         if short is None:
-            mine_short = tied(block(1 - link, k), long)
+            mine_short = tied(block(1 - link, k), after)
         else:
-            mine_short = joined(block(1 - link, k), tied(short, long))
+            mine_short = joined(block(1 - link, k), short)
+            long = tied(long, short)
+        short = swapped(mine_short, 1 - link)
         mine = joined(block(link, k), long)
         long = swapped(mine, link)
-        short = swapped(mine_short, 1 - link)
     return own + long.astype(F32) + short.astype(F32)
 
 
@@ -272,8 +273,8 @@
     place = lax.axis_index("dz")
     scal = jnp.stack([place, 1 - 2 * (place % 2), model_index, counts[0]]).astype(jnp.int32)
     held, stats, own, *blocks = front(scal, stream[0], value_grad[0], gain)
-    weight_grad = sum_over_y(sum_over_z(own, blocks)).astype(BF16)[None]
     tiles = parts(value_grad[0], weights[0], held, gain, stats)
+    weight_grad = sum_over_y(sum_over_z(own, blocks, tiles)).astype(BF16)[None]
     arrived = lax.all_to_all(tiles, MP, split_axis=0, concat_axis=0, tiled=True)
     norm_back, above_grad = backward(scal, arrived, stream[0], stats, gain, top_grad)
     below_grad = lax.ppermute(above_grad, "section", [(1, 0)])

time: 113 us -> 106 us (0.938)
  the two profiles are of different devices: /device:TPU:1 before, /device:TPU:7 now
where the time goes in v7:
time: 106 us; the launch traced here: 105 us
  starting transfers between devices  68.6 us (65%)
  waiting for transfers between devices  18.4 us (17%)
  Pallas kernels  14.2 us (13%)
  other arithmetic  2.35 us (2%)
  between operations  1.56 us (1%)
    ppermute x11, starting transfers between devices, swapped(): return lax.ppermute(value, 'dz', pairs)  46 us
    all_to_all x1, waiting for transfers between devices, sum_over_y(): lax.all_to_all(tiles, 'dy', split_axis=0, concat_axis=0, tiled=True)  9.83 us
    ppermute x1, starting transfers between devices, shards(): below_grad = lax.ppermute(above_grad, 'section', [(1, 0)])  9.57 us
    ppermute x11, waiting for transfers between devices, swapped(): return lax.ppermute(value, 'dz', pairs)  8.51 us
    all_to_all x1, starting transfers between devices, sum_over_y(): lax.all_to_all(tiles, 'dy', split_axis=0, concat_axis=0, tiled=True)  7.86 us
    pallas_call x1, Pallas kernels, front(): pl.pallas_call(front_kernel, in_specs=[pl.BlockSpec(memory_space=pltpu.SM...  5.94 us
    all_to_all x1, starting transfers between devices, shards(): arrived = lax.all_to_all(tiles, MP, split_axis=0, concat_axis=0, tiled=True)  5.25 us
    pallas_call x1, Pallas kernels, backward(): pl.pallas_call(back_kernel, grid_spec=pltpu.PrefetchScalarGridSpec(num_sc...  4.05 us
  transfers between devices with their start and end apart: 14, of which 6 were waited for; matrix products, arithmetic and copies ran while one was open for 1% of the time, Pallas kernels for 4%

profile of v7, /device:TPU:7, one launch (start us, length us, event | category | flops | bytes accessed | tf_op | source)
XLA Modules:
  0.0 105.1 jit_solution(8965872981505484288)
XLA Ops:
  1.3 0.1 pad_add_fusion.scal
  1.4 0.0 copy-start.1
  1.4 0.0 copy-start.2
  1.4 0.0 copy-start.3
  1.4 5.9 %shard_map.77 = (bf16[512,3072]{1,0:T(8,128)(2,1)S(1)}, f32[2,512,128]{2,1,0:T(8,128)S(1)}, f32[32,3072]{1,0:T(8,128)S(1)}, bf16[32,3072]{1,0:T(8,128)(2,1)S(1)}...) custom-call(s32[4]{0:T(128)S(1)} %pad_add_fusion.scal, ...), custom_call_target="tpu_custom_call" | custom-call | flops 4831838208 | bytes 8000000 | tf_op jit(solution)/shard_map/pallas_call | solution.py:89
  7.3 0.0 copy-start
  7.3 0.0 copy-done.1
  7.3 0.0 copy-done.2
  7.4 0.0 copy-done.3
  7.4 3.8 %shard_map.79 = bf16[8,520,384]{2,1,0:T(8,128)(2,1)} custom-call(bf16[512,384]{1,0:T(8,128)(2,1)S(1)} %bitcast.13, bf16[384,3072]{1,0:T(8,128)(2,1)S(1)} %bitcast.11, bf16[512,3072]{1,0:T(8,128)(2,1)S(1)} %get-tuple-element.31.held, f32[1,3072]{1,0:T(1,128)S(1)} %copy-done.1, f32[2,512,128]{2,1,0:T(8,128)S(1)} %get-tuple-element.32.stats), custom_call_target="tpu_custom_call" | custom-call | flops 3623878656 | bytes 9000000 | tf_op jit(solution)/shard_map/pallas_call | solution.py:148
  11.1 0.0 copy-done
  11.1 5.2 %all-to-all-start.1 = ((bf16[8,520,384]{2,1,0:T(8,128)(2,1)}), bf16[8,520,384]{2,1,0:T(8,128)(2,1)}, u32[]{:S(2)}, u32[]{:S(2)}) async-start(bf16[8,520,384]{2,1,0:T(8,128)(2,1)} %shard_map.79), calls=%async_computation.1 | async-start | bytes 6389760 | tf_op jit(solution)/shard_map/all_to_all | solution.py:278
  16.4 4.0 %collective-permute-start = (bf16[32,3072]{1,0:T(8,128)(2,1)S(1)}, bf16[32,3072]{1,0:T(8,128)(2,1)S(1)}, u32[]{:S(2)}, u32[]{:S(2)}) collective-permute-start(bf16[32,3072]{1,0:T(8,128)(2,1)S(1)} %get-tuple-element.29), channel_id=1, source_target_pairs={{0,4},{4,0},{8,12},{12,8},{16,20},{20,16},{24,28},{28,24},{32,36},... | collective-permute-start | bytes 589832 | tf_op jit(solution)/shard_map/ppermute | solution.py:220
  20.4 1.9 %collective-permute-start.2 = (bf16[32,3072]{1,0:T(8,128)(2,1)S(1)}, bf16[32,3072]{1,0:T(8,128)(2,1)S(1)}, u32[]{:S(2)}, u32[]{:S(2)}) collective-permute-start(bf16[32,3072]{1,0:T(8,128)(2,1)S(1)} %get-tuple-element.33), channel_id=1, source_target_pairs={{0,4},{4,0},{8,12},{12,8},{16,20},{20,16},{24,28},{28,24},{32,36},... | collective-permute-start | bytes 589832 | tf_op jit(solution)/shard_map/ppermute | solution.py:220
  22.3 1.1 %collective-permute-done.got = bf16[32,3072]{1,0:T(8,128)(2,1)S(1)} collective-permute-done((bf16[32,3072]{1,0:T(8,128)(2,1)S(1)}, bf16[32,3072]{1,0:T(8,128)(2,1)S(1)}, u32[]{:S(2)}, u32[]{:S(2)}) %collective-permute-start) | collective-permute-done | bytes 196640 | tf_op jit(solution)/shard_map/ppermute | solution.py:220
  23.5 14.5 %collective-permute-start.1 = (bf16[32,3072]{1,0:T(8,128)(2,1)S(1)}, bf16[32,3072]{1,0:T(8,128)(2,1)S(1)}, u32[]{:S(2)}, u32[]{:S(2)}) collective-permute-start(bf16[32,3072]{1,0:T(8,128)(2,1)S(1)} %shard_map.78), channel_id=1, source_target_pairs={{4,8},{8,4},{12,16},{16,12},{20,24},{24,20},{28,32},{32,28},{36,40... | collective-permute-start | bytes 589832 | tf_op jit(solution)/shard_map/ppermute | solution.py:220
  38.0 0.0 collective-permute-done.2.got
  38.0 4.1 %collective-permute-start.4 = (bf16[32,3072]{1,0:T(8,128)(2,1)S(1)}, bf16[32,3072]{1,0:T(8,128)(2,1)S(1)}, u32[]{:S(2)}, u32[]{:S(2)}) collective-permute-start(bf16[32,3072]{1,0:T(8,128)(2,1)S(1)} %shard_map.81), channel_id=1, source_target_pairs={{4,8},{8,4},{12,16},{16,12},{20,24},{24,20},{28,32},{32,28},{36,40... | collective-permute-start | bytes 589832 | tf_op jit(solution)/shard_map/ppermute | solution.py:220
  42.2 0.0 collective-permute-done.1.got
  42.3 1.9 %collective-permute-start.3 = (bf16[32,3072]{1,0:T(8,128)(2,1)S(1)}, bf16[32,3072]{1,0:T(8,128)(2,1)S(1)}, u32[]{:S(2)}, u32[]{:S(2)}) collective-permute-start(bf16[32,3072]{1,0:T(8,128)(2,1)S(1)} %shard_map.80), channel_id=1, source_target_pairs={{0,4},{4,0},{8,12},{12,8},{16,20},{20,16},{24,28},{28,24},{32,36},... | collective-permute-start | bytes 589832 | tf_op jit(solution)/shard_map/ppermute | solution.py:220
  44.2 3.2 %collective-permute-done.4.got = bf16[32,3072]{1,0:T(8,128)(2,1)S(1)} collective-permute-done((bf16[32,3072]{1,0:T(8,128)(2,1)S(1)}, bf16[32,3072]{1,0:T(8,128)(2,1)S(1)}, u32[]{:S(2)}, u32[]{:S(2)}) %collective-permute-start.4) | collective-permute-done | bytes 196640 | tf_op jit(solution)/shard_map/ppermute | solution.py:220
  47.4 1.9 %collective-permute-start.6 = (bf16[32,3072]{1,0:T(8,128)(2,1)S(1)}, bf16[32,3072]{1,0:T(8,128)(2,1)S(1)}, u32[]{:S(2)}, u32[]{:S(2)}) collective-permute-start(bf16[32,3072]{1,0:T(8,128)(2,1)S(1)} %shard_map.83), channel_id=1, source_target_pairs={{0,4},{4,0},{8,12},{12,8},{16,20},{20,16},{24,28},{28,24},{32,36},... | collective-permute-start | bytes 589832 | tf_op jit(solution)/shard_map/ppermute | solution.py:220
  49.4 0.0 collective-permute-done.3.got
  49.4 4.9 %collective-permute-start.5 = (bf16[32,3072]{1,0:T(8,128)(2,1)S(1)}, bf16[32,3072]{1,0:T(8,128)(2,1)S(1)}, u32[]{:S(2)}, u32[]{:S(2)}) collective-permute-start(bf16[32,3072]{1,0:T(8,128)(2,1)S(1)} %shard_map.82), channel_id=1, source_target_pairs={{4,8},{8,4},{12,16},{16,12},{20,24},{24,20},{28,32},{32,28},{36,40... | collective-permute-start | bytes 589832 | tf_op jit(solution)/shard_map/ppermute | solution.py:220
  54.4 1.7 %collective-permute-done.6.got = bf16[32,3072]{1,0:T(8,128)(2,1)S(1)} collective-permute-done((bf16[32,3072]{1,0:T(8,128)(2,1)S(1)}, bf16[32,3072]{1,0:T(8,128)(2,1)S(1)}, u32[]{:S(2)}, u32[]{:S(2)}) %collective-permute-start.6) | collective-permute-done | bytes 196640 | tf_op jit(solution)/shard_map/ppermute | solution.py:220
  56.1 4.6 %collective-permute-start.8 = (bf16[32,3072]{1,0:T(8,128)(2,1)S(1)}, bf16[32,3072]{1,0:T(8,128)(2,1)S(1)}, u32[]{:S(2)}, u32[]{:S(2)}) collective-permute-start(bf16[32,3072]{1,0:T(8,128)(2,1)S(1)} %shard_map.85), channel_id=1, source_target_pairs={{4,8},{8,4},{12,16},{16,12},{20,24},{24,20},{28,32},{32,28},{36,40... | collective-permute-start | bytes 589832 | tf_op jit(solution)/shard_map/ppermute | solution.py:220
  60.7 0.0 collective-permute-done.5.got
  60.8 1.9 %collective-permute-start.7 = (bf16[32,3072]{1,0:T(8,128)(2,1)S(1)}, bf16[32,3072]{1,0:T(8,128)(2,1)S(1)}, u32[]{:S(2)}, u32[]{:S(2)}) collective-permute-start(bf16[32,3072]{1,0:T(8,128)(2,1)S(1)} %shard_map.84), channel_id=1, source_target_pairs={{0,4},{4,0},{8,12},{12,8},{16,20},{20,16},{24,28},{28,24},{32,36},... | collective-permute-start | bytes 589832 | tf_op jit(solution)/shard_map/ppermute | solution.py:220
  62.7 2.4 %collective-permute-done.8.got = bf16[32,3072]{1,0:T(8,128)(2,1)S(1)} collective-permute-done((bf16[32,3072]{1,0:T(8,128)(2,1)S(1)}, bf16[32,3072]{1,0:T(8,128)(2,1)S(1)}, u32[]{:S(2)}, u32[]{:S(2)}) %collective-permute-start.8) | collective-permute-done | bytes 196640 | tf_op jit(solution)/shard_map/ppermute | solution.py:220
  65.2 1.9 %collective-permute-start.10 = (bf16[32,3072]{1,0:T(8,128)(2,1)S(1)}, bf16[32,3072]{1,0:T(8,128)(2,1)S(1)}, u32[]{:S(2)}, u32[]{:S(2)}) collective-permute-start(bf16[32,3072]{1,0:T(8,128)(2,1)S(1)} %shard_map.87), channel_id=1, source_target_pairs={{0,4},{4,0},{8,12},{12,8},{16,20},{20,16},{24,28},{28,24},{32,36},... | collective-permute-start | bytes 589832 | tf_op jit(solution)/shard_map/ppermute | solution.py:220
  67.1 0.1 collective-permute-done.7.got
  67.3 4.2 %collective-permute-start.9 = (bf16[32,3072]{1,0:T(8,128)(2,1)S(1)}, bf16[32,3072]{1,0:T(8,128)(2,1)S(1)}, u32[]{:S(2)}, u32[]{:S(2)}) collective-permute-start(bf16[32,3072]{1,0:T(8,128)(2,1)S(1)} %shard_map.86), channel_id=1, source_target_pairs={{4,8},{8,4},{12,16},{16,12},{20,24},{24,20},{28,32},{32,28},{36,40... | collective-permute-start | bytes 589832 | tf_op jit(solution)/shard_map/ppermute | solution.py:220
  71.5 0.0 all-to-all-done.1.arrived.extra
  71.5 4.1 %shard_map.88 = (f32[512,384]{1,0:T(8,128)S(1)}, bf16[512,384]{1,0:T(8,128)(2,1)S(1)}) custom-call(s32[4]{0:T(128)S(1)} %pad_add_fusion.scal, bf16[8,520,384]{2,1,0:T(8,128)(2,1)} %all-to-all-done.1.arrived.extra, bf16[8,520,384]{2,1,0:T(8,128)(2,1)} %all-to-all-done.1.arrived.extra, bf16[512,3072]{1,0:T(8,128)(2,1)} %bitcast.15, f32[2,512,128]{2,1,0:T(8,128)} %copy-done, ...), custom_call_target="tpu_custom_call" | custom-call | flops 500000000 | bytes 6000000 | tf_op jit(solution)/shard_map/pallas_call | solution.py:191
  75.5 9.6 %collective-permute-start.11 = (bf16[512,384]{1,0:T(8,128)(2,1)S(1)}, bf16[512,384]{1,0:T(8,128)(2,1)S(1)}, u32[]{:S(2)}, u32[]{:S(2)}) collective-permute-start(bf16[512,384]{1,0:T(8,128)(2,1)S(1)} %get-tuple-element.42), channel_id=1, source_target_pairs={{384,0},{385,1},{386,2},{387,3},{388,4},{389,5},{390,6},{391,7},{3... | collective-permute-start | bytes 1179656 | tf_op jit(solution)/shard_map/ppermute | solution.py:280
  85.1 0.0 collective-permute-done.10
  85.1 0.0 collective-permute-done.9
  85.1 0.7 fusion.2
  85.9 7.9 %all-to-all-start = ((bf16[4,8,3072]{2,1,0:T(8,128)(2,1)}), bf16[4,8,3072]{2,1,0:T(8,128)(2,1)S(1)}, u32[]{:S(2)}, u32[]{:S(2)}) async-start(bf16[4,8,3072]{2,1,0:T(8,128)(2,1)} %fusion.2), calls=%async_computation | async-start | bytes 393216 | tf_op jit(solution)/shard_map/all_to_all | solution.py:266
  93.7 9.8 %all-to-all-done = bf16[4,8,3072]{2,1,0:T(8,128)(2,1)S(1)} async-done(((bf16[4,8,3072]{2,1,0:T(8,128)(2,1)}), bf16[4,8,3072]{2,1,0:T(8,128)(2,1)S(1)}, u32[]{:S(2)}, u32[]{:S(2)}) %all-to-all-start) | async-done | bytes 196640 | tf_op jit(solution)/shard_map/all_to_all | solution.py:266
  103.6 0.7 reduce_sum.12
  104.2 0.0 collective-permute-done.11
  104.2 0.9 fusion.1
  (9 shorter events, 0.4 us)
Async XLA Ops:
  1.4 6.0 %copy-start.1 = (f32[1,3072]{1,0:T(1,128)S(1)}, f32[1,3072]{1,0:T(1,128)}, u32[]{:S(2)}) copy-start(f32[1,3072]{1,0:T(1,128)} %gain.3) | copy-start | bytes 36868
  1.4 6.0 %copy-start.2 = (bf16[1,384,3072]{2,1,0:T(8,128)(2,1)S(1)}, bf16[1,384,3072]{2,1,0:T(8,128)(2,1)}, u32[]{:S(2)}) copy-start(bf16[1,384,3072]{2,1,0:T(8,128)(2,1)} %param.8) | copy-start | bytes 7077892
  1.4 6.0 %copy-start.3 = (bf16[1,512,384]{2,1,0:T(8,128)(2,1)S(1)}, bf16[1,512,384]{2,1,0:T(8,128)(2,1)}, u32[]{:S(2)}) copy-start(bf16[1,512,384]{2,1,0:T(8,128)(2,1)} %param.6) | copy-start | bytes 1179652
  7.3 3.8 %copy-start = (f32[2,512,128]{2,1,0:T(8,128)}, f32[2,512,128]{2,1,0:T(8,128)S(1)}, u32[]{:S(2)}) copy-start(f32[2,512,128]{2,1,0:T(8,128)S(1)} %get-tuple-element.32.stats) | copy-start | bytes 1572868
  11.1 60.3 %all-to-all-start.1 = ((bf16[8,520,384]{2,1,0:T(8,128)(2,1)}), bf16[8,520,384]{2,1,0:T(8,128)(2,1)}, u32[]{:S(2)}, u32[]{:S(2)}) async-start(bf16[8,520,384]{2,1,0:T(8,128)(2,1)} %shard_map.79), calls=%async_computation.1 | async-start | bytes 6389760 | tf_op jit(solution)/shard_map/all_to_all | solution.py:278
  16.4 7.0 %collective-permute-start = (bf16[32,3072]{1,0:T(8,128)(2,1)S(1)}, bf16[32,3072]{1,0:T(8,128)(2,1)S(1)}, u32[]{:S(2)}, u32[]{:S(2)}) collective-permute-start(bf16[32,3072]{1,0:T(8,128)(2,1)S(1)} %get-tuple-element.29), channel_id=1, source_target_pairs={{0,4},{4,0},{8,12},{12,8},{16,20},{20,16},{24,28},{28,24},{32,36},... | collective-permute-start | bytes 589832 | tf_op jit(solution)/shard_map/ppermute | solution.py:220
  20.4 17.6 %collective-permute-start.2 = (bf16[32,3072]{1,0:T(8,128)(2,1)S(1)}, bf16[32,3072]{1,0:T(8,128)(2,1)S(1)}, u32[]{:S(2)}, u32[]{:S(2)}) collective-permute-start(bf16[32,3072]{1,0:T(8,128)(2,1)S(1)} %get-tuple-element.33), channel_id=1, source_target_pairs={{0,4},{4,0},{8,12},{12,8},{16,20},{20,16},{24,28},{28,24},{32,36},... | collective-permute-start | bytes 589832 | tf_op jit(solution)/shard_map/ppermute | solution.py:220
  23.5 18.7 %collective-permute-start.1 = (bf16[32,3072]{1,0:T(8,128)(2,1)S(1)}, bf16[32,3072]{1,0:T(8,128)(2,1)S(1)}, u32[]{:S(2)}, u32[]{:S(2)}) collective-permute-start(bf16[32,3072]{1,0:T(8,128)(2,1)S(1)} %shard_map.78), channel_id=1, source_target_pairs={{4,8},{8,4},{12,16},{16,12},{20,24},{24,20},{28,32},{32,28},{36,40... | collective-permute-start | bytes 589832 | tf_op jit(solution)/shard_map/ppermute | solution.py:220
  38.0 9.3 %collective-permute-start.4 = (bf16[32,3072]{1,0:T(8,128)(2,1)S(1)}, bf16[32,3072]{1,0:T(8,128)(2,1)S(1)}, u32[]{:S(2)}, u32[]{:S(2)}) collective-permute-start(bf16[32,3072]{1,0:T(8,128)(2,1)S(1)} %shard_map.81), channel_id=1, source_target_pairs={{4,8},{8,4},{12,16},{16,12},{20,24},{24,20},{28,32},{32,28},{36,40... | collective-permute-start | bytes 589832 | tf_op jit(solution)/shard_map/ppermute | solution.py:220
  42.3 7.1 %collective-permute-start.3 = (bf16[32,3072]{1,0:T(8,128)(2,1)S(1)}, bf16[32,3072]{1,0:T(8,128)(2,1)S(1)}, u32[]{:S(2)}, u32[]{:S(2)}) collective-permute-start(bf16[32,3072]{1,0:T(8,128)(2,1)S(1)} %shard_map.80), channel_id=1, source_target_pairs={{0,4},{4,0},{8,12},{12,8},{16,20},{20,16},{24,28},{28,24},{32,36},... | collective-permute-start | bytes 589832 | tf_op jit(solution)/shard_map/ppermute | solution.py:220
  47.4 8.6 %collective-permute-start.6 = (bf16[32,3072]{1,0:T(8,128)(2,1)S(1)}, bf16[32,3072]{1,0:T(8,128)(2,1)S(1)}, u32[]{:S(2)}, u32[]{:S(2)}) collective-permute-start(bf16[32,3072]{1,0:T(8,128)(2,1)S(1)} %shard_map.83), channel_id=1, source_target_pairs={{0,4},{4,0},{8,12},{12,8},{16,20},{20,16},{24,28},{28,24},{32,36},... | collective-permute-start | bytes 589832 | tf_op jit(solution)/shard_map/ppermute | solution.py:220
  49.4 11.3 %collective-permute-start.5 = (bf16[32,3072]{1,0:T(8,128)(2,1)S(1)}, bf16[32,3072]{1,0:T(8,128)(2,1)S(1)}, u32[]{:S(2)}, u32[]{:S(2)}) collective-permute-start(bf16[32,3072]{1,0:T(8,128)(2,1)S(1)} %shard_map.82), channel_id=1, source_target_pairs={{4,8},{8,4},{12,16},{16,12},{20,24},{24,20},{28,32},{32,28},{36,40... | collective-permute-start | bytes 589832 | tf_op jit(solution)/shard_map/ppermute | solution.py:220
  56.1 9.0 %collective-permute-start.8 = (bf16[32,3072]{1,0:T(8,128)(2,1)S(1)}, bf16[32,3072]{1,0:T(8,128)(2,1)S(1)}, u32[]{:S(2)}, u32[]{:S(2)}) collective-permute-start(bf16[32,3072]{1,0:T(8,128)(2,1)S(1)} %shard_map.85), channel_id=1, source_target_pairs={{4,8},{8,4},{12,16},{16,12},{20,24},{24,20},{28,32},{32,28},{36,40... | collective-permute-start | bytes 589832 | tf_op jit(solution)/shard_map/ppermute | solution.py:220
  60.8 6.4 %collective-permute-start.7 = (bf16[32,3072]{1,0:T(8,128)(2,1)S(1)}, bf16[32,3072]{1,0:T(8,128)(2,1)S(1)}, u32[]{:S(2)}, u32[]{:S(2)}) collective-permute-start(bf16[32,3072]{1,0:T(8,128)(2,1)S(1)} %shard_map.84), channel_id=1, source_target_pairs={{0,4},{4,0},{8,12},{12,8},{16,20},{20,16},{24,28},{28,24},{32,36},... | collective-permute-start | bytes 589832 | tf_op jit(solution)/shard_map/ppermute | solution.py:220
  65.2 19.9 %collective-permute-start.10 = (bf16[32,3072]{1,0:T(8,128)(2,1)S(1)}, bf16[32,3072]{1,0:T(8,128)(2,1)S(1)}, u32[]{:S(2)}, u32[]{:S(2)}) collective-permute-start(bf16[32,3072]{1,0:T(8,128)(2,1)S(1)} %shard_map.87), channel_id=1, source_target_pairs={{0,4},{4,0},{8,12},{12,8},{16,20},{20,16},{24,28},{28,24},{32,36},... | collective-permute-start | bytes 589832 | tf_op jit(solution)/shard_map/ppermute | solution.py:220
  67.3 17.9 %collective-permute-start.9 = (bf16[32,3072]{1,0:T(8,128)(2,1)S(1)}, bf16[32,3072]{1,0:T(8,128)(2,1)S(1)}, u32[]{:S(2)}, u32[]{:S(2)}) collective-permute-start(bf16[32,3072]{1,0:T(8,128)(2,1)S(1)} %shard_map.86), channel_id=1, source_target_pairs={{4,8},{8,4},{12,16},{16,12},{20,24},{24,20},{28,32},{32,28},{36,40... | collective-permute-start | bytes 589832 | tf_op jit(solution)/shard_map/ppermute | solution.py:220
  75.5 28.7 %collective-permute-start.11 = (bf16[512,384]{1,0:T(8,128)(2,1)S(1)}, bf16[512,384]{1,0:T(8,128)(2,1)S(1)}, u32[]{:S(2)}, u32[]{:S(2)}) collective-permute-start(bf16[512,384]{1,0:T(8,128)(2,1)S(1)} %get-tuple-element.42), channel_id=1, source_target_pairs={{384,0},{385,1},{386,2},{387,3},{388,4},{389,5},{390,6},{391,7},{3... | collective-permute-start | bytes 1179656 | tf_op jit(solution)/shard_map/ppermute | solution.py:280
  85.9 17.7 %all-to-all-start = ((bf16[4,8,3072]{2,1,0:T(8,128)(2,1)}), bf16[4,8,3072]{2,1,0:T(8,128)(2,1)S(1)}, u32[]{:S(2)}, u32[]{:S(2)}) async-start(bf16[4,8,3072]{2,1,0:T(8,128)(2,1)} %fusion.2), calls=%async_computation | async-start | bytes 393216 | tf_op jit(solution)/shard_map/all_to_all | solution.py:266

commit v8 on v7

--- a/solution.py
+++ b/solution.py
@@ -161,55 +161,65 @@
     )(value_grad, weights, held, gain, stats)
 
 
-def back_kernel(scal, arrived, extra, stream, stats, gain, top, back, above, columns):
-    step = pl.program_id(0)
-
-    @pl.when(step == 0)
-    def _():
-        sums = jnp.sum(extra[...].astype(F32), axis=0)
-        lines = jnp.concatenate([sums[:4], sums[4:, :128]], axis=1)
-        for j, line in enumerate((lines[0:1] + lines[1:2], lines[2:3] + lines[3:4])):
-            for b in range(TOK // BLOCK):
-                square = jnp.broadcast_to(line[:, b * BLOCK : (b + 1) * BLOCK], (BLOCK, BLOCK))
-                columns[j, b * BLOCK : (b + 1) * BLOCK, :] = square.T * (1.0 / WIDTH)
-
-    rows = pl.ds(pl.multiple_of(step * BLOCK, BLOCK), BLOCK)
-    mean = columns[0, rows, :][:, :1]
-    slope = columns[1, rows, :][:, :1]
-    total = arrived[0].astype(F32)
-    for j in range(1, PARTS):
-        total = total + arrived[j].astype(F32)
-    scale = stats[0][:, 0:1]
-    white = (stream[...].astype(F32) - stats[1][:, 0:1]) * scale
-    branch = scale * (total * gain[...] - mean - white * slope)
-    back[...] = branch
-    above[...] = (top[...].astype(F32) + branch).astype(BF16)
-
-
-def backward(scal, arrived, stream, stats, gain, top):
-    token = lambda width: pl.BlockSpec((BLOCK, width), lambda i, s: (i, 0))
+def back_kernel(scal, sent, stats, gain, top, stream, back, above, arrived, top_here, stream_here, columns, sems):
+    share = pl.ds(pl.multiple_of(scal[2] * SHARE, 128), SHARE)
+    fetches = [
+        pltpu.make_async_copy(stream.at[:, share], stream_here, sems.at[0]),
+        pltpu.make_async_copy(top.at[:, share], top_here, sems.at[1]),
+    ]
+    rows_of = [pl.ds(TOK, EXTRA)] + [pl.ds(b * BLOCK, BLOCK) for b in range(TOK // BLOCK)]
+    for i, rows in enumerate(rows_of):
+        fetches.append(pltpu.make_async_copy(sent.at[:, rows, :], arrived.at[:, rows, :], sems.at[2 + i]))
+    for i in (2, 0, 1, 3, 4, 5, 6):
+        fetches[i].start()
+    fetches[2].wait()
+    sums = jnp.sum(arrived[:, TOK:, :].astype(F32), axis=0)
+    lines = jnp.concatenate([sums[:4], sums[4:, :128]], axis=1)
+    for j, line in enumerate((lines[0:1] + lines[1:2], lines[2:3] + lines[3:4])):
+        for b in range(TOK // BLOCK):
+            square = jnp.broadcast_to(line[:, b * BLOCK : (b + 1) * BLOCK], (BLOCK, BLOCK))
+            columns[j, b * BLOCK : (b + 1) * BLOCK, :] = square.T * (1.0 / WIDTH)
+    gains = gain[:, share]
+    fetches[0].wait()
+    fetches[1].wait()
+
+    def chunk(i, carry):
+        rows = pl.ds(pl.multiple_of(i * CHUNK, CHUNK), CHUNK)
+        total = arrived[0, rows, :].astype(F32)
+        for j in range(1, PARTS):
+            total = total + arrived[j, rows, :].astype(F32)
+        spread = lambda a: jnp.concatenate([a] * (SHARE // 128), axis=1)
+        scale = spread(stats[0, rows, :])
+        white = (stream_here[rows, :].astype(F32) - spread(stats[1, rows, :])) * scale
+        branch = scale * (total * gains - spread(columns[0, rows, :]) - white * spread(columns[1, rows, :]))
+        back[rows, :] = branch
+        above[rows, :] = (top_here[rows, :].astype(F32) + branch).astype(BF16)
+        return carry
+
+    per = BLOCK // CHUNK
+    for b in range(TOK // BLOCK):
+        fetches[3 + b].wait()
+        lax.fori_loop(b * per, (b + 1) * per, chunk, 0, unroll=4)
+
+
+def backward(scal, arrived, stats, gain, top, stream):
+    vmem = pl.BlockSpec(memory_space=pltpu.VMEM)
+    hbm = pl.BlockSpec(memory_space=pl.ANY)
     return pl.pallas_call(
         back_kernel,
-        grid_spec=pltpu.PrefetchScalarGridSpec(
-            num_scalar_prefetch=1,
-            grid=(TOK // BLOCK,),
-            in_specs=[
-                pl.BlockSpec((PARTS, BLOCK, SHARE), lambda i, s: (0, i, 0)),
-                pl.BlockSpec((PARTS, EXTRA, SHARE), lambda i, s: (0, TOK // EXTRA, 0)),
-                pl.BlockSpec((BLOCK, SHARE), lambda i, s: (i, s[2])),
-                pl.BlockSpec((2, BLOCK, 128), lambda i, s: (0, i, 0)),
-                pl.BlockSpec((1, SHARE), lambda i, s: (0, s[2])),
-                pl.BlockSpec((BLOCK, SHARE), lambda i, s: (i, s[2])),
-            ],
-            out_specs=[token(SHARE), token(SHARE)],
-            scratch_shapes=[pltpu.VMEM((2, TOK, BLOCK), F32)],
-        ),
+        in_specs=[pl.BlockSpec(memory_space=pltpu.SMEM), hbm, vmem, vmem, hbm, hbm],
+        out_specs=[vmem, vmem],
+        scratch_shapes=[
+            pltpu.VMEM((PARTS, TOK + EXTRA, SHARE), BF16),
+            pltpu.VMEM((TOK, SHARE), BF16),
+            pltpu.VMEM((TOK, SHARE), BF16),
+            pltpu.VMEM((2, TOK, BLOCK), F32),
+            pltpu.SemaphoreType.DMA((2 + 1 + TOK // BLOCK,)),
+        ],
         out_shape=[jax.ShapeDtypeStruct((TOK, SHARE), F32), jax.ShapeDtypeStruct((TOK, SHARE), BF16)],
-        compiler_params=pltpu.CompilerParams(
-            dimension_semantics=("arbitrary",), vmem_limit_bytes=16 * 1024 * 1024
-        ),
+        compiler_params=pltpu.CompilerParams(vmem_limit_bytes=12 * 1024 * 1024),
         cost_estimate=pl.CostEstimate(flops=500_000_000, transcendentals=0, bytes_accessed=6_000_000),
-    )(scal, *in_hbm(arrived, arrived, stream, stats, gain, top))
+    )(scal, *in_hbm(arrived), stats, gain, *in_hbm(top, stream))
 
 
 def swapped(value, link):
@@ -276,7 +286,7 @@
     tiles = parts(value_grad[0], weights[0], held, gain, stats)
     weight_grad = sum_over_y(sum_over_z(own, blocks, tiles)).astype(BF16)[None]
     arrived = lax.all_to_all(tiles, MP, split_axis=0, concat_axis=0, tiled=True)
-    norm_back, above_grad = backward(scal, arrived, stream[0], stats, gain, top_grad)
+    norm_back, above_grad = backward(scal, arrived, stats, gain, top_grad, stream[0])
     below_grad = lax.ppermute(above_grad, "section", [(1, 0)])
     lower_grad = (below_grad.astype(F32) + norm_back).astype(BF16)
     result = jnp.where(section_index == 0, lower_grad, above_grad)

time: 106 us -> 105 us (level)
  Pallas kernels: 14.2 us -> 13.1 us
    pallas_call x1, Pallas kernels: 4.05 us -> 2.91 us  [backward(): pl.pallas_call(back_kernel, in_specs=[pl.BlockSpec(memory_space=pltpu.SME...]
  transfers between devices with their start and end apart: 14 -> 14, of which waited for: 6 -> 6; matrix products, arithmetic and copies ran while one was open for 1% -> 1% of each run, Pallas kernels for 4% -> 3%
where the time goes in v8:
time: 105 us; the launch traced here: 104 us
  starting transfers between devices  68.8 us (66%)
  waiting for transfers between devices  18.3 us (17%)
  Pallas kernels  13.1 us (12%)
  other arithmetic  2.34 us (2%)
  between operations  1.54 us (1%)
    ppermute x11, starting transfers between devices, swapped(): return lax.ppermute(value, 'dz', pairs)  46.1 us
    all_to_all x1, waiting for transfers between devices, sum_over_y(): lax.all_to_all(tiles, 'dy', split_axis=0, concat_axis=0, tiled=True)  9.83 us
    ppermute x1, starting transfers between devices, shards(): below_grad = lax.ppermute(above_grad, 'section', [(1, 0)])  9.52 us
    ppermute x11, waiting for transfers between devices, swapped(): return lax.ppermute(value, 'dz', pairs)  8.49 us
    all_to_all x1, starting transfers between devices, sum_over_y(): lax.all_to_all(tiles, 'dy', split_axis=0, concat_axis=0, tiled=True)  7.96 us
    pallas_call x1, Pallas kernels, front(): pl.pallas_call(front_kernel, in_specs=[pl.BlockSpec(memory_space=pltpu.SM...  5.94 us
    all_to_all x1, starting transfers between devices, shards(): arrived = lax.all_to_all(tiles, MP, split_axis=0, concat_axis=0, tiled=True)  5.25 us
    pallas_call x1, Pallas kernels, parts(): pl.pallas_call(parts_kernel, in_specs=[vmem] * 5, out_specs=pl.BlockSpec(...  3.77 us
  transfers between devices with their start and end apart: 14, of which 6 were waited for; matrix products, arithmetic and copies ran while one was open for 1% of the time, Pallas kernels for 3%

profile of v8, /device:TPU:7, one launch (start us, length us, event | category | flops | bytes accessed | tf_op | source)
XLA Modules:
  0.0 104.1 jit_solution(14483130670486389147)
XLA Ops:
  1.3 0.1 pad_add_fusion.scal
  1.4 0.0 copy-start
  1.4 0.0 copy-start.1
  1.4 0.0 copy-start.2
  1.4 5.9 %shard_map.77 = (bf16[512,3072]{1,0:T(8,128)(2,1)S(1)}, f32[2,512,128]{2,1,0:T(8,128)S(1)}, f32[32,3072]{1,0:T(8,128)S(1)}, bf16[32,3072]{1,0:T(8,128)(2,1)S(1)}...) custom-call(s32[4]{0:T(128)S(1)} %pad_add_fusion.scal, ...), custom_call_target="tpu_custom_call" | custom-call | flops 4831838208 | bytes 8000000 | tf_op jit(solution)/shard_map/pallas_call | solution.py:89
  7.3 0.0 copy-done
  7.3 0.0 copy-done.1
  7.3 0.0 copy-done.2
  7.4 3.8 %shard_map.79 = bf16[8,520,384]{2,1,0:T(8,128)(2,1)} custom-call(bf16[512,384]{1,0:T(8,128)(2,1)S(1)} %bitcast.13, bf16[384,3072]{1,0:T(8,128)(2,1)S(1)} %bitcast.11, bf16[512,3072]{1,0:T(8,128)(2,1)S(1)} %get-tuple-element.31.held, f32[1,3072]{1,0:T(1,128)S(1)} %copy-done, f32[2,512,128]{2,1,0:T(8,128)S(1)} %get-tuple-element.32.stats), custom_call_target="tpu_custom_call" | custom-call | flops 3623878656 | bytes 9000000 | tf_op jit(solution)/shard_map/pallas_call | solution.py:148
  11.1 5.2 %all-to-all-start.1 = ((bf16[8,520,384]{2,1,0:T(8,128)(2,1)}), bf16[8,520,384]{2,1,0:T(8,128)(2,1)}, u32[]{:S(2)}, u32[]{:S(2)}) async-start(bf16[8,520,384]{2,1,0:T(8,128)(2,1)} %shard_map.79), calls=%async_computation.1 | async-start | bytes 6389760 | tf_op jit(solution)/shard_map/all_to_all | solution.py:288
  16.4 4.0 %collective-permute-start = (bf16[32,3072]{1,0:T(8,128)(2,1)S(1)}, bf16[32,3072]{1,0:T(8,128)(2,1)S(1)}, u32[]{:S(2)}, u32[]{:S(2)}) collective-permute-start(bf16[32,3072]{1,0:T(8,128)(2,1)S(1)} %get-tuple-element.29), channel_id=1, source_target_pairs={{0,4},{4,0},{8,12},{12,8},{16,20},{20,16},{24,28},{28,24},{32,36},... | collective-permute-start | bytes 589832 | tf_op jit(solution)/shard_map/ppermute | solution.py:230
  20.4 1.9 %collective-permute-start.2 = (bf16[32,3072]{1,0:T(8,128)(2,1)S(1)}, bf16[32,3072]{1,0:T(8,128)(2,1)S(1)}, u32[]{:S(2)}, u32[]{:S(2)}) collective-permute-start(bf16[32,3072]{1,0:T(8,128)(2,1)S(1)} %get-tuple-element.33), channel_id=1, source_target_pairs={{0,4},{4,0},{8,12},{12,8},{16,20},{20,16},{24,28},{28,24},{32,36},... | collective-permute-start | bytes 589832 | tf_op jit(solution)/shard_map/ppermute | solution.py:230
  22.3 1.1 %collective-permute-done.got = bf16[32,3072]{1,0:T(8,128)(2,1)S(1)} collective-permute-done((bf16[32,3072]{1,0:T(8,128)(2,1)S(1)}, bf16[32,3072]{1,0:T(8,128)(2,1)S(1)}, u32[]{:S(2)}, u32[]{:S(2)}) %collective-permute-start) | collective-permute-done | bytes 196640 | tf_op jit(solution)/shard_map/ppermute | solution.py:230
  23.5 14.5 %collective-permute-start.1 = (bf16[32,3072]{1,0:T(8,128)(2,1)S(1)}, bf16[32,3072]{1,0:T(8,128)(2,1)S(1)}, u32[]{:S(2)}, u32[]{:S(2)}) collective-permute-start(bf16[32,3072]{1,0:T(8,128)(2,1)S(1)} %shard_map.78), channel_id=1, source_target_pairs={{4,8},{8,4},{12,16},{16,12},{20,24},{24,20},{28,32},{32,28},{36,40... | collective-permute-start | bytes 589832 | tf_op jit(solution)/shard_map/ppermute | solution.py:230
  38.0 0.0 collective-permute-done.2.got
  38.0 4.1 %collective-permute-start.4 = (bf16[32,3072]{1,0:T(8,128)(2,1)S(1)}, bf16[32,3072]{1,0:T(8,128)(2,1)S(1)}, u32[]{:S(2)}, u32[]{:S(2)}) collective-permute-start(bf16[32,3072]{1,0:T(8,128)(2,1)S(1)} %shard_map.81), channel_id=1, source_target_pairs={{4,8},{8,4},{12,16},{16,12},{20,24},{24,20},{28,32},{32,28},{36,40... | collective-permute-start | bytes 589832 | tf_op jit(solution)/shard_map/ppermute | solution.py:230
  42.2 0.0 collective-permute-done.1.got
  42.3 1.9 %collective-permute-start.3 = (bf16[32,3072]{1,0:T(8,128)(2,1)S(1)}, bf16[32,3072]{1,0:T(8,128)(2,1)S(1)}, u32[]{:S(2)}, u32[]{:S(2)}) collective-permute-start(bf16[32,3072]{1,0:T(8,128)(2,1)S(1)} %shard_map.80), channel_id=1, source_target_pairs={{0,4},{4,0},{8,12},{12,8},{16,20},{20,16},{24,28},{28,24},{32,36},... | collective-permute-start | bytes 589832 | tf_op jit(solution)/shard_map/ppermute | solution.py:230
  44.2 3.2 %collective-permute-done.4.got = bf16[32,3072]{1,0:T(8,128)(2,1)S(1)} collective-permute-done((bf16[32,3072]{1,0:T(8,128)(2,1)S(1)}, bf16[32,3072]{1,0:T(8,128)(2,1)S(1)}, u32[]{:S(2)}, u32[]{:S(2)}) %collective-permute-start.4) | collective-permute-done | bytes 196640 | tf_op jit(solution)/shard_map/ppermute | solution.py:230
  47.4 1.9 %collective-permute-start.6 = (bf16[32,3072]{1,0:T(8,128)(2,1)S(1)}, bf16[32,3072]{1,0:T(8,128)(2,1)S(1)}, u32[]{:S(2)}, u32[]{:S(2)}) collective-permute-start(bf16[32,3072]{1,0:T(8,128)(2,1)S(1)} %shard_map.83), channel_id=1, source_target_pairs={{0,4},{4,0},{8,12},{12,8},{16,20},{20,16},{24,28},{28,24},{32,36},... | collective-permute-start | bytes 589832 | tf_op jit(solution)/shard_map/ppermute | solution.py:230
  49.3 0.0 collective-permute-done.3.got
  49.4 5.0 %collective-permute-start.5 = (bf16[32,3072]{1,0:T(8,128)(2,1)S(1)}, bf16[32,3072]{1,0:T(8,128)(2,1)S(1)}, u32[]{:S(2)}, u32[]{:S(2)}) collective-permute-start(bf16[32,3072]{1,0:T(8,128)(2,1)S(1)} %shard_map.82), channel_id=1, source_target_pairs={{4,8},{8,4},{12,16},{16,12},{20,24},{24,20},{28,32},{32,28},{36,40... | collective-permute-start | bytes 589832 | tf_op jit(solution)/shard_map/ppermute | solution.py:230
  54.4 1.7 %collective-permute-done.6.got = bf16[32,3072]{1,0:T(8,128)(2,1)S(1)} collective-permute-done((bf16[32,3072]{1,0:T(8,128)(2,1)S(1)}, bf16[32,3072]{1,0:T(8,128)(2,1)S(1)}, u32[]{:S(2)}, u32[]{:S(2)}) %collective-permute-start.6) | collective-permute-done | bytes 196640 | tf_op jit(solution)/shard_map/ppermute | solution.py:230
  56.1 4.7 %collective-permute-start.8 = (bf16[32,3072]{1,0:T(8,128)(2,1)S(1)}, bf16[32,3072]{1,0:T(8,128)(2,1)S(1)}, u32[]{:S(2)}, u32[]{:S(2)}) collective-permute-start(bf16[32,3072]{1,0:T(8,128)(2,1)S(1)} %shard_map.85), channel_id=1, source_target_pairs={{4,8},{8,4},{12,16},{16,12},{20,24},{24,20},{28,32},{32,28},{36,40... | collective-permute-start | bytes 589832 | tf_op jit(solution)/shard_map/ppermute | solution.py:230
  60.8 0.0 collective-permute-done.5.got
  60.9 1.9 %collective-permute-start.7 = (bf16[32,3072]{1,0:T(8,128)(2,1)S(1)}, bf16[32,3072]{1,0:T(8,128)(2,1)S(1)}, u32[]{:S(2)}, u32[]{:S(2)}) collective-permute-start(bf16[32,3072]{1,0:T(8,128)(2,1)S(1)} %shard_map.84), channel_id=1, source_target_pairs={{0,4},{4,0},{8,12},{12,8},{16,20},{20,16},{24,28},{28,24},{32,36},... | collective-permute-start | bytes 589832 | tf_op jit(solution)/shard_map/ppermute | solution.py:230
  62.8 2.4 %collective-permute-done.8.got = bf16[32,3072]{1,0:T(8,128)(2,1)S(1)} collective-permute-done((bf16[32,3072]{1,0:T(8,128)(2,1)S(1)}, bf16[32,3072]{1,0:T(8,128)(2,1)S(1)}, u32[]{:S(2)}, u32[]{:S(2)}) %collective-permute-start.8) | collective-permute-done | bytes 196640 | tf_op jit(solution)/shard_map/ppermute | solution.py:230
  65.3 1.9 %collective-permute-start.10 = (bf16[32,3072]{1,0:T(8,128)(2,1)S(1)}, bf16[32,3072]{1,0:T(8,128)(2,1)S(1)}, u32[]{:S(2)}, u32[]{:S(2)}) collective-permute-start(bf16[32,3072]{1,0:T(8,128)(2,1)S(1)} %shard_map.87), channel_id=1, source_target_pairs={{0,4},{4,0},{8,12},{12,8},{16,20},{20,16},{24,28},{28,24},{32,36},... | collective-permute-start | bytes 589832 | tf_op jit(solution)/shard_map/ppermute | solution.py:230
  67.2 0.1 collective-permute-done.7.got
  67.3 4.2 %collective-permute-start.9 = (bf16[32,3072]{1,0:T(8,128)(2,1)S(1)}, bf16[32,3072]{1,0:T(8,128)(2,1)S(1)}, u32[]{:S(2)}, u32[]{:S(2)}) collective-permute-start(bf16[32,3072]{1,0:T(8,128)(2,1)S(1)} %shard_map.86), channel_id=1, source_target_pairs={{4,8},{8,4},{12,16},{16,12},{20,24},{24,20},{28,32},{32,28},{36,40... | collective-permute-start | bytes 589832 | tf_op jit(solution)/shard_map/ppermute | solution.py:230
  71.6 0.0 all-to-all-done.1.sent
  71.6 2.9 %shard_map.88 = (f32[512,384]{1,0:T(8,128)S(1)}, bf16[512,384]{1,0:T(8,128)(2,1)S(1)}) custom-call(s32[4]{0:T(128)S(1)} %pad_add_fusion.scal, bf16[8,520,384]{2,1,0:T(8,128)(2,1)} %all-to-all-done.1.sent, f32[2,512,128]{2,1,0:T(8,128)S(1)} %get-tuple-element.32.stats, f32[1,3072]{1,0:T(1,128)S(1)} %copy-done, bf16[512,3072]{1,0:T(8,128)(2,1)} %top.1, ...), custom_call_target="tpu_custom_call" | custom-call | flops 500000000 | bytes 6000000 | tf_op jit(solution)/shard_map/pallas_call | solution.py:208
  74.5 9.5 %collective-permute-start.11 = (bf16[512,384]{1,0:T(8,128)(2,1)S(1)}, bf16[512,384]{1,0:T(8,128)(2,1)S(1)}, u32[]{:S(2)}, u32[]{:S(2)}) collective-permute-start(bf16[512,384]{1,0:T(8,128)(2,1)S(1)} %get-tuple-element.42), channel_id=1, source_target_pairs={{384,0},{385,1},{386,2},{387,3},{388,4},{389,5},{390,6},{391,7},{3... | collective-permute-start | bytes 1179656 | tf_op jit(solution)/shard_map/ppermute | solution.py:290
  84.0 0.0 collective-permute-done.10
  84.0 0.0 collective-permute-done.9
  84.0 0.7 fusion.2
  84.8 8.0 %all-to-all-start = ((bf16[4,8,3072]{2,1,0:T(8,128)(2,1)}), bf16[4,8,3072]{2,1,0:T(8,128)(2,1)S(1)}, u32[]{:S(2)}, u32[]{:S(2)}) async-start(bf16[4,8,3072]{2,1,0:T(8,128)(2,1)} %fusion.2), calls=%async_computation | async-start | bytes 393216 | tf_op jit(solution)/shard_map/all_to_all | solution.py:276
  92.7 9.8 %all-to-all-done = bf16[4,8,3072]{2,1,0:T(8,128)(2,1)S(1)} async-done(((bf16[4,8,3072]{2,1,0:T(8,128)(2,1)}), bf16[4,8,3072]{2,1,0:T(8,128)(2,1)S(1)}, u32[]{:S(2)}, u32[]{:S(2)}) %all-to-all-start) | async-done | bytes 196640 | tf_op jit(solution)/shard_map/all_to_all | solution.py:276
  102.6 0.7 reduce_sum.12
  103.2 0.0 collective-permute-done.11
  103.2 0.9 fusion.1
  (9 shorter events, 0.4 us)
Async XLA Ops:
  1.4 6.0 %copy-start = (f32[1,3072]{1,0:T(1,128)S(1)}, f32[1,3072]{1,0:T(1,128)}, u32[]{:S(2)}) copy-start(f32[1,3072]{1,0:T(1,128)} %gain.3) | copy-start | bytes 36868
  1.4 6.0 %copy-start.1 = (bf16[1,384,3072]{2,1,0:T(8,128)(2,1)S(1)}, bf16[1,384,3072]{2,1,0:T(8,128)(2,1)}, u32[]{:S(2)}) copy-start(bf16[1,384,3072]{2,1,0:T(8,128)(2,1)} %param.8) | copy-start | bytes 7077892
  1.4 6.0 %copy-start.2 = (bf16[1,512,384]{2,1,0:T(8,128)(2,1)S(1)}, bf16[1,512,384]{2,1,0:T(8,128)(2,1)}, u32[]{:S(2)}) copy-start(bf16[1,512,384]{2,1,0:T(8,128)(2,1)} %param.6) | copy-start | bytes 1179652
  11.1 60.4 %all-to-all-start.1 = ((bf16[8,520,384]{2,1,0:T(8,128)(2,1)}), bf16[8,520,384]{2,1,0:T(8,128)(2,1)}, u32[]{:S(2)}, u32[]{:S(2)}) async-start(bf16[8,520,384]{2,1,0:T(8,128)(2,1)} %shard_map.79), calls=%async_computation.1 | async-start | bytes 6389760 | tf_op jit(solution)/shard_map/all_to_all | solution.py:288
  16.4 7.0 %collective-permute-start = (bf16[32,3072]{1,0:T(8,128)(2,1)S(1)}, bf16[32,3072]{1,0:T(8,128)(2,1)S(1)}, u32[]{:S(2)}, u32[]{:S(2)}) collective-permute-start(bf16[32,3072]{1,0:T(8,128)(2,1)S(1)} %get-tuple-element.29), channel_id=1, source_target_pairs={{0,4},{4,0},{8,12},{12,8},{16,20},{20,16},{24,28},{28,24},{32,36},... | collective-permute-start | bytes 589832 | tf_op jit(solution)/shard_map/ppermute | solution.py:230
  20.4 17.6 %collective-permute-start.2 = (bf16[32,3072]{1,0:T(8,128)(2,1)S(1)}, bf16[32,3072]{1,0:T(8,128)(2,1)S(1)}, u32[]{:S(2)}, u32[]{:S(2)}) collective-permute-start(bf16[32,3072]{1,0:T(8,128)(2,1)S(1)} %get-tuple-element.33), channel_id=1, source_target_pairs={{0,4},{4,0},{8,12},{12,8},{16,20},{20,16},{24,28},{28,24},{32,36},... | collective-permute-start | bytes 589832 | tf_op jit(solution)/shard_map/ppermute | solution.py:230
  23.5 18.7 %collective-permute-start.1 = (bf16[32,3072]{1,0:T(8,128)(2,1)S(1)}, bf16[32,3072]{1,0:T(8,128)(2,1)S(1)}, u32[]{:S(2)}, u32[]{:S(2)}) collective-permute-start(bf16[32,3072]{1,0:T(8,128)(2,1)S(1)} %shard_map.78), channel_id=1, source_target_pairs={{4,8},{8,4},{12,16},{16,12},{20,24},{24,20},{28,32},{32,28},{36,40... | collective-permute-start | bytes 589832 | tf_op jit(solution)/shard_map/ppermute | solution.py:230
  38.0 9.3 %collective-permute-start.4 = (bf16[32,3072]{1,0:T(8,128)(2,1)S(1)}, bf16[32,3072]{1,0:T(8,128)(2,1)S(1)}, u32[]{:S(2)}, u32[]{:S(2)}) collective-permute-start(bf16[32,3072]{1,0:T(8,128)(2,1)S(1)} %shard_map.81), channel_id=1, source_target_pairs={{4,8},{8,4},{12,16},{16,12},{20,24},{24,20},{28,32},{32,28},{36,40... | collective-permute-start | bytes 589832 | tf_op jit(solution)/shard_map/ppermute | solution.py:230
  42.3 7.1 %collective-permute-start.3 = (bf16[32,3072]{1,0:T(8,128)(2,1)S(1)}, bf16[32,3072]{1,0:T(8,128)(2,1)S(1)}, u32[]{:S(2)}, u32[]{:S(2)}) collective-permute-start(bf16[32,3072]{1,0:T(8,128)(2,1)S(1)} %shard_map.80), channel_id=1, source_target_pairs={{0,4},{4,0},{8,12},{12,8},{16,20},{20,16},{24,28},{28,24},{32,36},... | collective-permute-start | bytes 589832 | tf_op jit(solution)/shard_map/ppermute | solution.py:230
  47.4 8.6 %collective-permute-start.6 = (bf16[32,3072]{1,0:T(8,128)(2,1)S(1)}, bf16[32,3072]{1,0:T(8,128)(2,1)S(1)}, u32[]{:S(2)}, u32[]{:S(2)}) collective-permute-start(bf16[32,3072]{1,0:T(8,128)(2,1)S(1)} %shard_map.83), channel_id=1, source_target_pairs={{0,4},{4,0},{8,12},{12,8},{16,20},{20,16},{24,28},{28,24},{32,36},... | collective-permute-start | bytes 589832 | tf_op jit(solution)/shard_map/ppermute | solution.py:230
  49.4 11.4 %collective-permute-start.5 = (bf16[32,3072]{1,0:T(8,128)(2,1)S(1)}, bf16[32,3072]{1,0:T(8,128)(2,1)S(1)}, u32[]{:S(2)}, u32[]{:S(2)}) collective-permute-start(bf16[32,3072]{1,0:T(8,128)(2,1)S(1)} %shard_map.82), channel_id=1, source_target_pairs={{4,8},{8,4},{12,16},{16,12},{20,24},{24,20},{28,32},{32,28},{36,40... | collective-permute-start | bytes 589832 | tf_op jit(solution)/shard_map/ppermute | solution.py:230
  56.1 9.1 %collective-permute-start.8 = (bf16[32,3072]{1,0:T(8,128)(2,1)S(1)}, bf16[32,3072]{1,0:T(8,128)(2,1)S(1)}, u32[]{:S(2)}, u32[]{:S(2)}) collective-permute-start(bf16[32,3072]{1,0:T(8,128)(2,1)S(1)} %shard_map.85), channel_id=1, source_target_pairs={{4,8},{8,4},{12,16},{16,12},{20,24},{24,20},{28,32},{32,28},{36,40... | collective-permute-start | bytes 589832 | tf_op jit(solution)/shard_map/ppermute | solution.py:230
  60.9 6.4 %collective-permute-start.7 = (bf16[32,3072]{1,0:T(8,128)(2,1)S(1)}, bf16[32,3072]{1,0:T(8,128)(2,1)S(1)}, u32[]{:S(2)}, u32[]{:S(2)}) collective-permute-start(bf16[32,3072]{1,0:T(8,128)(2,1)S(1)} %shard_map.84), channel_id=1, source_target_pairs={{0,4},{4,0},{8,12},{12,8},{16,20},{20,16},{24,28},{28,24},{32,36},... | collective-permute-start | bytes 589832 | tf_op jit(solution)/shard_map/ppermute | solution.py:230
  65.3 18.8 %collective-permute-start.10 = (bf16[32,3072]{1,0:T(8,128)(2,1)S(1)}, bf16[32,3072]{1,0:T(8,128)(2,1)S(1)}, u32[]{:S(2)}, u32[]{:S(2)}) collective-permute-start(bf16[32,3072]{1,0:T(8,128)(2,1)S(1)} %shard_map.87), channel_id=1, source_target_pairs={{0,4},{4,0},{8,12},{12,8},{16,20},{20,16},{24,28},{28,24},{32,36},... | collective-permute-start | bytes 589832 | tf_op jit(solution)/shard_map/ppermute | solution.py:230
  67.3 16.7 %collective-permute-start.9 = (bf16[32,3072]{1,0:T(8,128)(2,1)S(1)}, bf16[32,3072]{1,0:T(8,128)(2,1)S(1)}, u32[]{:S(2)}, u32[]{:S(2)}) collective-permute-start(bf16[32,3072]{1,0:T(8,128)(2,1)S(1)} %shard_map.86), channel_id=1, source_target_pairs={{4,8},{8,4},{12,16},{16,12},{20,24},{24,20},{28,32},{32,28},{36,40... | collective-permute-start | bytes 589832 | tf_op jit(solution)/shard_map/ppermute | solution.py:230
  74.5 28.7 %collective-permute-start.11 = (bf16[512,384]{1,0:T(8,128)(2,1)S(1)}, bf16[512,384]{1,0:T(8,128)(2,1)S(1)}, u32[]{:S(2)}, u32[]{:S(2)}) collective-permute-start(bf16[512,384]{1,0:T(8,128)(2,1)S(1)} %get-tuple-element.42), channel_id=1, source_target_pairs={{384,0},{385,1},{386,2},{387,3},{388,4},{389,5},{390,6},{391,7},{3... | collective-permute-start | bytes 1179656 | tf_op jit(solution)/shard_map/ppermute | solution.py:290
  84.8 17.8 %all-to-all-start = ((bf16[4,8,3072]{2,1,0:T(8,128)(2,1)}), bf16[4,8,3072]{2,1,0:T(8,128)(2,1)S(1)}, u32[]{:S(2)}, u32[]{:S(2)}) async-start(bf16[4,8,3072]{2,1,0:T(8,128)(2,1)} %fusion.2), calls=%async_computation | async-start | bytes 393216 | tf_op jit(solution)/shard_map/all_to_all | solution.py:276

commit v9 on v8

--- a/solution.py
+++ b/solution.py
@@ -29,8 +29,10 @@
     return [pltpu.with_memory_space_constraint(a, pltpu.HBM) for a in arrays]
 
 
-def front_kernel(scal, stream, value_grad_from, gain_from, held, stats, own, *rest):
+def front_kernel(counts, stream, value_grad_from, gain_from, held, stats, own, *rest):
     blocks, (normed, grad, value_grad, gain, sems) = rest[:-5], rest[-5:]
+    place = lax.axis_index("dz")
+    ahead = 1 - 2 * lax.rem(place, 2)
     per = TOK // BLOCK
     gain_here = pltpu.make_async_copy(gain_from, gain, sems.at[per])
     gain_here.start()
@@ -68,13 +70,13 @@
         lax.fori_loop(b * per, (b + 1) * per, chunk, 0, unroll=UNROLL)
     value_grad_here.wait()
     token = lax.broadcasted_iota(jnp.int32, (TOK, SHARE), 0)
-    live = token < scal[3] * TOK_MB
+    live = token < counts[0] * TOK_MB
     left = jnp.where(live, value_grad[...].astype(F32), 0.0).astype(BF16).T
     for n in range(WIDTH // COLS):
         cols = slice(n * COLS, (n + 1) * COLS)
         grad[...] = jnp.dot(left, normed[:, cols], preferred_element_type=F32)
         for r in range(RING):
-            at = lax.rem(scal[0] + r * scal[1] + RING, RING) * ROWS
+            at = lax.rem(place + r * ahead + RING, RING) * ROWS
             piece = grad[pl.ds(pl.multiple_of(at, ROWS), ROWS), :]
             if r == 0:
                 own[:, cols] = piece
@@ -82,7 +84,7 @@
                 blocks[r - 1][:, cols] = piece.astype(BF16)
 
 
-def front(scal, stream, value_grad, gain):
+def front(stream, value_grad, gain, counts):
     vmem = pl.BlockSpec(memory_space=pltpu.VMEM)
     out = [((TOK, WIDTH), BF16), ((2, TOK, 128), F32), ((ROWS, WIDTH), F32)]
     out += [((ROWS, WIDTH), BF16)] * (RING - 1)
@@ -103,7 +105,7 @@
         out_shape=[jax.ShapeDtypeStruct(*o) for o in out],
         compiler_params=pltpu.CompilerParams(vmem_limit_bytes=24 * 1024 * 1024),
         cost_estimate=pl.CostEstimate(flops=2 * TOK * SHARE * WIDTH * 4, transcendentals=0, bytes_accessed=8_000_000),
-    )(scal, *in_hbm(stream, value_grad, gain))
+    )(counts, *in_hbm(stream, value_grad, gain))
 
 
 def parts_kernel(value_grad, weights, held, gain, stats, out, packed, extra, sums, sems):
@@ -161,8 +163,9 @@
     )(value_grad, weights, held, gain, stats)
 
 
-def back_kernel(scal, sent, stats, gain, top, stream, back, above, arrived, top_here, stream_here, columns, sems):
-    share = pl.ds(pl.multiple_of(scal[2] * SHARE, 128), SHARE)
+def back_kernel(sent, stats, gain, top, stream, back, above, arrived, top_here, stream_here, columns, sems):
+    model_index = lax.axis_index("my") * 4 + lax.axis_index("mx")
+    share = pl.ds(pl.multiple_of(model_index * SHARE, 128), SHARE)
     fetches = [
         pltpu.make_async_copy(stream.at[:, share], stream_here, sems.at[0]),
         pltpu.make_async_copy(top.at[:, share], top_here, sems.at[1]),
@@ -202,12 +205,12 @@
         lax.fori_loop(b * per, (b + 1) * per, chunk, 0, unroll=4)
 
 
-def backward(scal, arrived, stats, gain, top, stream):
+def backward(arrived, stats, gain, top, stream):
     vmem = pl.BlockSpec(memory_space=pltpu.VMEM)
     hbm = pl.BlockSpec(memory_space=pl.ANY)
     return pl.pallas_call(
         back_kernel,
-        in_specs=[pl.BlockSpec(memory_space=pltpu.SMEM), hbm, vmem, vmem, hbm, hbm],
+        in_specs=[hbm, vmem, vmem, hbm, hbm],
         out_specs=[vmem, vmem],
         scratch_shapes=[
             pltpu.VMEM((PARTS, TOK + EXTRA, SHARE), BF16),
@@ -219,7 +222,7 @@
         out_shape=[jax.ShapeDtypeStruct((TOK, SHARE), F32), jax.ShapeDtypeStruct((TOK, SHARE), BF16)],
         compiler_params=pltpu.CompilerParams(vmem_limit_bytes=12 * 1024 * 1024),
         cost_estimate=pl.CostEstimate(flops=500_000_000, transcendentals=0, bytes_accessed=6_000_000),
-    )(scal, *in_hbm(arrived), stats, gain, *in_hbm(top, stream))
+    )(*in_hbm(arrived), stats, gain, *in_hbm(top, stream))
 
 
 def swapped(value, link):
@@ -279,14 +282,11 @@
 
 def shards(value_grad, stream, weights, gain, top_grad, counts):
     section_index = lax.axis_index("section")
-    model_index = lax.axis_index(MP)
-    place = lax.axis_index("dz")
-    scal = jnp.stack([place, 1 - 2 * (place % 2), model_index, counts[0]]).astype(jnp.int32)
-    held, stats, own, *blocks = front(scal, stream[0], value_grad[0], gain)
+    held, stats, own, *blocks = front(stream[0], value_grad[0], gain, counts)
     tiles = parts(value_grad[0], weights[0], held, gain, stats)
     weight_grad = sum_over_y(sum_over_z(own, blocks, tiles)).astype(BF16)[None]
     arrived = lax.all_to_all(tiles, MP, split_axis=0, concat_axis=0, tiled=True)
-    norm_back, above_grad = backward(scal, arrived, stats, gain, top_grad, stream[0])
+    norm_back, above_grad = backward(arrived, stats, gain, top_grad, stream[0])
     below_grad = lax.ppermute(above_grad, "section", [(1, 0)])
     lower_grad = (below_grad.astype(F32) + norm_back).astype(BF16)
     result = jnp.where(section_index == 0, lower_grad, above_grad)

time: 105 us -> 103 us (0.981)
  the two profiles are of different devices: /device:TPU:7 before, /device:TPU:6 now
where the time goes in v9:
time: 103 us
  starting transfers between devices  60.2 us (58%)
  waiting for transfers between devices  27.1 us (26%)
  Pallas kernels  11.7 us (11%)
  other arithmetic  2.3 us (2%)
  between operations  1.51 us (1%)
    ppermute x11, starting transfers between devices, swapped(): return lax.ppermute(value, 'dz', pairs)  36.9 us
    ppermute x11, waiting for transfers between devices, swapped(): return lax.ppermute(value, 'dz', pairs)  16.3 us
    all_to_all x1, starting transfers between devices, shards(): arrived = lax.all_to_all(tiles, MP, split_axis=0, concat_axis=0, tiled=True)  13.8 us
    all_to_all x1, waiting for transfers between devices, sum_over_y(): lax.all_to_all(tiles, 'dy', split_axis=0, concat_axis=0, tiled=True)  10.7 us
    all_to_all x1, starting transfers between devices, sum_over_y(): lax.all_to_all(tiles, 'dy', split_axis=0, concat_axis=0, tiled=True)  8.19 us
    pallas_call x1, Pallas kernels, front(): pl.pallas_call(front_kernel, in_specs=[pl.BlockSpec(memory_space=pltpu.SM...  5.21 us
    pallas_call x1, Pallas kernels, parts(): pl.pallas_call(parts_kernel, in_specs=[vmem] * 5, out_specs=pl.BlockSpec(...  3.62 us
    pallas_call x1, Pallas kernels, backward(): pl.pallas_call(back_kernel, in_specs=[hbm, vmem, vmem, hbm, hbm], out_spe...  2.37 us
  transfers between devices with their start and end apart: 14, of which 9 were waited for; matrix products, arithmetic and copies ran while one was open for 1% of the time, Pallas kernels for 3%

profile of v9, /device:TPU:6, one launch (start us, length us, event | category | flops | bytes accessed | tf_op | source)
XLA Modules:
  0.0 102.8 jit_solution(10523086635073204787)
XLA Ops:
  1.3 0.0 copy-start
  1.3 0.0 copy-start.1
  1.3 0.0 copy-start.2
  1.3 5.2 %shard_map.77 = (bf16[512,3072]{1,0:T(8,128)(2,1)S(1)}, f32[2,512,128]{2,1,0:T(8,128)S(1)}, f32[32,3072]{1,0:T(8,128)S(1)}, bf16[32,3072]{1,0:T(8,128)(2,1)S(1)}...) custom-call(s32[1]{0:T(128)S(6)} %copy.8.counts, ...), custom_call_target="tpu_custom_call" | custom-call | flops 4831838208 | bytes 8000000 | tf_op jit(solution)/shard_map/pallas_call | solution.py:91
  6.5 0.0 copy-done
  6.5 0.0 copy-done.1
  6.5 0.0 copy-done.2
  6.6 3.6 %shard_map.79 = bf16[8,520,384]{2,1,0:T(8,128)(2,1)} custom-call(bf16[512,384]{1,0:T(8,128)(2,1)S(1)} %bitcast.10, bf16[384,3072]{1,0:T(8,128)(2,1)S(1)} %bitcast.8, bf16[512,3072]{1,0:T(8,128)(2,1)S(1)} %get-tuple-element.31.held, f32[1,3072]{1,0:T(1,128)S(1)} %copy-done, f32[2,512,128]{2,1,0:T(8,128)S(1)} %get-tuple-element.32.stats), custom_call_target="tpu_custom_call" | custom-call | flops 3623878656 | bytes 9000000 | tf_op jit(solution)/shard_map/pallas_call | solution.py:150
  10.2 13.8 %all-to-all-start.1 = ((bf16[8,520,384]{2,1,0:T(8,128)(2,1)}), bf16[8,520,384]{2,1,0:T(8,128)(2,1)}, u32[]{:S(2)}, u32[]{:S(2)}) async-start(bf16[8,520,384]{2,1,0:T(8,128)(2,1)} %shard_map.79), calls=%async_computation.1 | async-start | bytes 6389760 | tf_op jit(solution)/shard_map/all_to_all | solution.py:288
  24.0 1.9 %collective-permute-start = (bf16[32,3072]{1,0:T(8,128)(2,1)S(1)}, bf16[32,3072]{1,0:T(8,128)(2,1)S(1)}, u32[]{:S(2)}, u32[]{:S(2)}) collective-permute-start(bf16[32,3072]{1,0:T(8,128)(2,1)S(1)} %get-tuple-element.29), channel_id=1, source_target_pairs={{0,4},{4,0},{8,12},{12,8},{16,20},{20,16},{24,28},{28,24},{32,36},... | collective-permute-start | bytes 589832 | tf_op jit(solution)/shard_map/ppermute | solution.py:233
  25.9 3.9 %collective-permute-start.2 = (bf16[32,3072]{1,0:T(8,128)(2,1)S(1)}, bf16[32,3072]{1,0:T(8,128)(2,1)S(1)}, u32[]{:S(2)}, u32[]{:S(2)}) collective-permute-start(bf16[32,3072]{1,0:T(8,128)(2,1)S(1)} %get-tuple-element.33), channel_id=1, source_target_pairs={{0,4},{4,0},{8,12},{12,8},{16,20},{20,16},{24,28},{28,24},{32,36},... | collective-permute-start | bytes 589832 | tf_op jit(solution)/shard_map/ppermute | solution.py:233
  29.8 1.7 %collective-permute-done.got = bf16[32,3072]{1,0:T(8,128)(2,1)S(1)} collective-permute-done((bf16[32,3072]{1,0:T(8,128)(2,1)S(1)}, bf16[32,3072]{1,0:T(8,128)(2,1)S(1)}, u32[]{:S(2)}, u32[]{:S(2)}) %collective-permute-start) | collective-permute-done | bytes 196640 | tf_op jit(solution)/shard_map/ppermute | solution.py:233
  31.5 0.1 shard_map.78
  31.6 8.7 %collective-permute-start.1 = (bf16[32,3072]{1,0:T(8,128)(2,1)S(1)}, bf16[32,3072]{1,0:T(8,128)(2,1)S(1)}, u32[]{:S(2)}, u32[]{:S(2)}) collective-permute-start(bf16[32,3072]{1,0:T(8,128)(2,1)S(1)} %shard_map.78), channel_id=1, source_target_pairs={{4,8},{8,4},{12,16},{16,12},{20,24},{24,20},{28,32},{32,28},{36,40... | collective-permute-start | bytes 589832 | tf_op jit(solution)/shard_map/ppermute | solution.py:233
  40.3 0.0 collective-permute-done.2.got
  40.3 0.1 shard_map.81
  40.3 2.4 %collective-permute-start.4 = (bf16[32,3072]{1,0:T(8,128)(2,1)S(1)}, bf16[32,3072]{1,0:T(8,128)(2,1)S(1)}, u32[]{:S(2)}, u32[]{:S(2)}) collective-permute-start(bf16[32,3072]{1,0:T(8,128)(2,1)S(1)} %shard_map.81), channel_id=1, source_target_pairs={{4,8},{8,4},{12,16},{16,12},{20,24},{24,20},{28,32},{32,28},{36,40... | collective-permute-start | bytes 589832 | tf_op jit(solution)/shard_map/ppermute | solution.py:233
  42.8 2.7 %collective-permute-done.1.got = bf16[32,3072]{1,0:T(8,128)(2,1)S(1)} collective-permute-done((bf16[32,3072]{1,0:T(8,128)(2,1)S(1)}, bf16[32,3072]{1,0:T(8,128)(2,1)S(1)}, u32[]{:S(2)}, u32[]{:S(2)}) %collective-permute-start.1) | collective-permute-done | bytes 196640 | tf_op jit(solution)/shard_map/ppermute | solution.py:233
  45.5 0.1 shard_map.80
  45.5 1.9 %collective-permute-start.3 = (bf16[32,3072]{1,0:T(8,128)(2,1)S(1)}, bf16[32,3072]{1,0:T(8,128)(2,1)S(1)}, u32[]{:S(2)}, u32[]{:S(2)}) collective-permute-start(bf16[32,3072]{1,0:T(8,128)(2,1)S(1)} %shard_map.80), channel_id=1, source_target_pairs={{0,4},{4,0},{8,12},{12,8},{16,20},{20,16},{24,28},{28,24},{32,36},... | collective-permute-start | bytes 589832 | tf_op jit(solution)/shard_map/ppermute | solution.py:233
  47.5 1.7 %collective-permute-done.4.got = bf16[32,3072]{1,0:T(8,128)(2,1)S(1)} collective-permute-done((bf16[32,3072]{1,0:T(8,128)(2,1)S(1)}, bf16[32,3072]{1,0:T(8,128)(2,1)S(1)}, u32[]{:S(2)}, u32[]{:S(2)}) %collective-permute-start.4) | collective-permute-done | bytes 196640 | tf_op jit(solution)/shard_map/ppermute | solution.py:233
  49.1 0.1 shard_map.83
  49.2 2.3 %collective-permute-start.6 = (bf16[32,3072]{1,0:T(8,128)(2,1)S(1)}, bf16[32,3072]{1,0:T(8,128)(2,1)S(1)}, u32[]{:S(2)}, u32[]{:S(2)}) collective-permute-start(bf16[32,3072]{1,0:T(8,128)(2,1)S(1)} %shard_map.83), channel_id=1, source_target_pairs={{0,4},{4,0},{8,12},{12,8},{16,20},{20,16},{24,28},{28,24},{32,36},... | collective-permute-start | bytes 589832 | tf_op jit(solution)/shard_map/ppermute | solution.py:233
  51.5 3.5 %collective-permute-done.3.got = bf16[32,3072]{1,0:T(8,128)(2,1)S(1)} collective-permute-done((bf16[32,3072]{1,0:T(8,128)(2,1)S(1)}, bf16[32,3072]{1,0:T(8,128)(2,1)S(1)}, u32[]{:S(2)}, u32[]{:S(2)}) %collective-permute-start.3) | collective-permute-done | bytes 196640 | tf_op jit(solution)/shard_map/ppermute | solution.py:233
  55.0 0.1 shard_map.82
  55.1 5.2 %collective-permute-start.5 = (bf16[32,3072]{1,0:T(8,128)(2,1)S(1)}, bf16[32,3072]{1,0:T(8,128)(2,1)S(1)}, u32[]{:S(2)}, u32[]{:S(2)}) collective-permute-start(bf16[32,3072]{1,0:T(8,128)(2,1)S(1)} %shard_map.82), channel_id=1, source_target_pairs={{4,8},{8,4},{12,16},{16,12},{20,24},{24,20},{28,32},{32,28},{36,40... | collective-permute-start | bytes 589832 | tf_op jit(solution)/shard_map/ppermute | solution.py:233
  60.3 0.0 collective-permute-done.6.got
  60.3 0.1 shard_map.85
  60.3 2.0 %collective-permute-start.8 = (bf16[32,3072]{1,0:T(8,128)(2,1)S(1)}, bf16[32,3072]{1,0:T(8,128)(2,1)S(1)}, u32[]{:S(2)}, u32[]{:S(2)}) collective-permute-start(bf16[32,3072]{1,0:T(8,128)(2,1)S(1)} %shard_map.85), channel_id=1, source_target_pairs={{4,8},{8,4},{12,16},{16,12},{20,24},{24,20},{28,32},{32,28},{36,40... | collective-permute-start | bytes 589832 | tf_op jit(solution)/shard_map/ppermute | solution.py:233
  62.4 2.5 %collective-permute-done.5.got = bf16[32,3072]{1,0:T(8,128)(2,1)S(1)} collective-permute-done((bf16[32,3072]{1,0:T(8,128)(2,1)S(1)}, bf16[32,3072]{1,0:T(8,128)(2,1)S(1)}, u32[]{:S(2)}, u32[]{:S(2)}) %collective-permute-start.5) | collective-permute-done | bytes 196640 | tf_op jit(solution)/shard_map/ppermute | solution.py:233
  64.9 0.1 shard_map.84
  65.0 1.9 %collective-permute-start.7 = (bf16[32,3072]{1,0:T(8,128)(2,1)S(1)}, bf16[32,3072]{1,0:T(8,128)(2,1)S(1)}, u32[]{:S(2)}, u32[]{:S(2)}) collective-permute-start(bf16[32,3072]{1,0:T(8,128)(2,1)S(1)} %shard_map.84), channel_id=1, source_target_pairs={{0,4},{4,0},{8,12},{12,8},{16,20},{20,16},{24,28},{28,24},{32,36},... | collective-permute-start | bytes 589832 | tf_op jit(solution)/shard_map/ppermute | solution.py:233
  66.9 2.2 %collective-permute-done.8.got = bf16[32,3072]{1,0:T(8,128)(2,1)S(1)} collective-permute-done((bf16[32,3072]{1,0:T(8,128)(2,1)S(1)}, bf16[32,3072]{1,0:T(8,128)(2,1)S(1)}, u32[]{:S(2)}, u32[]{:S(2)}) %collective-permute-start.8) | collective-permute-done | bytes 196640 | tf_op jit(solution)/shard_map/ppermute | solution.py:233
  69.1 0.1 shard_map.87
  69.2 1.9 %collective-permute-start.10 = (bf16[32,3072]{1,0:T(8,128)(2,1)S(1)}, bf16[32,3072]{1,0:T(8,128)(2,1)S(1)}, u32[]{:S(2)}, u32[]{:S(2)}) collective-permute-start(bf16[32,3072]{1,0:T(8,128)(2,1)S(1)} %shard_map.87), channel_id=1, source_target_pairs={{0,4},{4,0},{8,12},{12,8},{16,20},{20,16},{24,28},{28,24},{32,36},... | collective-permute-start | bytes 589832 | tf_op jit(solution)/shard_map/ppermute | solution.py:233
  71.1 1.6 %collective-permute-done.7.got = bf16[32,3072]{1,0:T(8,128)(2,1)S(1)} collective-permute-done((bf16[32,3072]{1,0:T(8,128)(2,1)S(1)}, bf16[32,3072]{1,0:T(8,128)(2,1)S(1)}, u32[]{:S(2)}, u32[]{:S(2)}) %collective-permute-start.7) | collective-permute-done | bytes 196640 | tf_op jit(solution)/shard_map/ppermute | solution.py:233
  72.8 4.7 %collective-permute-start.9 = (bf16[32,3072]{1,0:T(8,128)(2,1)S(1)}, bf16[32,3072]{1,0:T(8,128)(2,1)S(1)}, u32[]{:S(2)}, u32[]{:S(2)}) collective-permute-start(bf16[32,3072]{1,0:T(8,128)(2,1)S(1)} %shard_map.86), channel_id=1, source_target_pairs={{4,8},{8,4},{12,16},{16,12},{20,24},{24,20},{28,32},{32,28},{36,40... | collective-permute-start | bytes 589832 | tf_op jit(solution)/shard_map/ppermute | solution.py:233
  77.4 0.0 all-to-all-done.1.sent
  77.5 2.4 %shard_map.88 = (f32[512,384]{1,0:T(8,128)S(1)}, bf16[512,384]{1,0:T(8,128)(2,1)S(1)}) custom-call(bf16[8,520,384]{2,1,0:T(8,128)(2,1)} %all-to-all-done.1.sent, f32[2,512,128]{2,1,0:T(8,128)S(1)} %get-tuple-element.32.stats, f32[1,3072]{1,0:T(1,128)S(1)} %copy-done, bf16[512,3072]{1,0:T(8,128)(2,1)} %top.1, bf16[512,3072]{1,0:T(8,128)(2,1)} %bitcast.12), custom_call_target="tpu_custom_call" | custom-call | flops 500000000 | bytes 6000000 | tf_op jit(solution)/shard_map/pallas_call | solution.py:211
  79.8 1.3 %collective-permute-start.11 = (bf16[512,384]{1,0:T(8,128)(2,1)S(1)}, bf16[512,384]{1,0:T(8,128)(2,1)S(1)}, u32[]{:S(2)}, u32[]{:S(2)}) collective-permute-start(bf16[512,384]{1,0:T(8,128)(2,1)S(1)} %get-tuple-element.42), channel_id=1, source_target_pairs={{384,0},{385,1},{386,2},{387,3},{388,4},{389,5},{390,6},{391,7},{3... | collective-permute-start | bytes 1179656 | tf_op jit(solution)/shard_map/ppermute | solution.py:290
  81.1 0.0 collective-permute-done.10
  81.1 0.4 collective-permute-done.9
  81.5 0.8 fusion.2
  82.3 8.2 %all-to-all-start = ((bf16[4,8,3072]{2,1,0:T(8,128)(2,1)}), bf16[4,8,3072]{2,1,0:T(8,128)(2,1)S(1)}, u32[]{:S(2)}, u32[]{:S(2)}) async-start(bf16[4,8,3072]{2,1,0:T(8,128)(2,1)} %fusion.2), calls=%async_computation | async-start | bytes 393216 | tf_op jit(solution)/shard_map/all_to_all | solution.py:279
  90.5 10.7 %all-to-all-done = bf16[4,8,3072]{2,1,0:T(8,128)(2,1)S(1)} async-done(((bf16[4,8,3072]{2,1,0:T(8,128)(2,1)}), bf16[4,8,3072]{2,1,0:T(8,128)(2,1)S(1)}, u32[]{:S(2)}, u32[]{:S(2)}) %all-to-all-start) | async-done | bytes 196640 | tf_op jit(solution)/shard_map/all_to_all | solution.py:279
  101.2 0.7 reduce_sum.12
  101.9 0.0 collective-permute-done.11
  101.9 0.9 fusion.1
  (1 shorter events, 0.0 us)
Async XLA Ops:
  1.3 5.2 %copy-start = (f32[1,3072]{1,0:T(1,128)S(1)}, f32[1,3072]{1,0:T(1,128)}, u32[]{:S(2)}) copy-start(f32[1,3072]{1,0:T(1,128)} %gain.3) | copy-start | bytes 36868
  1.3 5.2 %copy-start.1 = (bf16[1,384,3072]{2,1,0:T(8,128)(2,1)S(1)}, bf16[1,384,3072]{2,1,0:T(8,128)(2,1)}, u32[]{:S(2)}) copy-start(bf16[1,384,3072]{2,1,0:T(8,128)(2,1)} %param.8) | copy-start | bytes 7077892
  1.3 5.2 %copy-start.2 = (bf16[1,512,384]{2,1,0:T(8,128)(2,1)S(1)}, bf16[1,512,384]{2,1,0:T(8,128)(2,1)}, u32[]{:S(2)}) copy-start(bf16[1,512,384]{2,1,0:T(8,128)(2,1)} %param.6) | copy-start | bytes 1179652
  10.2 67.3 %all-to-all-start.1 = ((bf16[8,520,384]{2,1,0:T(8,128)(2,1)}), bf16[8,520,384]{2,1,0:T(8,128)(2,1)}, u32[]{:S(2)}, u32[]{:S(2)}) async-start(bf16[8,520,384]{2,1,0:T(8,128)(2,1)} %shard_map.79), calls=%async_computation.1 | async-start | bytes 6389760 | tf_op jit(solution)/shard_map/all_to_all | solution.py:288
  24.0 7.6 %collective-permute-start = (bf16[32,3072]{1,0:T(8,128)(2,1)S(1)}, bf16[32,3072]{1,0:T(8,128)(2,1)S(1)}, u32[]{:S(2)}, u32[]{:S(2)}) collective-permute-start(bf16[32,3072]{1,0:T(8,128)(2,1)S(1)} %get-tuple-element.29), channel_id=1, source_target_pairs={{0,4},{4,0},{8,12},{12,8},{16,20},{20,16},{24,28},{28,24},{32,36},... | collective-permute-start | bytes 589832 | tf_op jit(solution)/shard_map/ppermute | solution.py:233
  25.9 14.4 %collective-permute-start.2 = (bf16[32,3072]{1,0:T(8,128)(2,1)S(1)}, bf16[32,3072]{1,0:T(8,128)(2,1)S(1)}, u32[]{:S(2)}, u32[]{:S(2)}) collective-permute-start(bf16[32,3072]{1,0:T(8,128)(2,1)S(1)} %get-tuple-element.33), channel_id=1, source_target_pairs={{0,4},{4,0},{8,12},{12,8},{16,20},{20,16},{24,28},{28,24},{32,36},... | collective-permute-start | bytes 589832 | tf_op jit(solution)/shard_map/ppermute | solution.py:233
  31.6 13.9 %collective-permute-start.1 = (bf16[32,3072]{1,0:T(8,128)(2,1)S(1)}, bf16[32,3072]{1,0:T(8,128)(2,1)S(1)}, u32[]{:S(2)}, u32[]{:S(2)}) collective-permute-start(bf16[32,3072]{1,0:T(8,128)(2,1)S(1)} %shard_map.78), channel_id=1, source_target_pairs={{4,8},{8,4},{12,16},{16,12},{20,24},{24,20},{28,32},{32,28},{36,40... | collective-permute-start | bytes 589832 | tf_op jit(solution)/shard_map/ppermute | solution.py:233
  40.3 8.8 %collective-permute-start.4 = (bf16[32,3072]{1,0:T(8,128)(2,1)S(1)}, bf16[32,3072]{1,0:T(8,128)(2,1)S(1)}, u32[]{:S(2)}, u32[]{:S(2)}) collective-permute-start(bf16[32,3072]{1,0:T(8,128)(2,1)S(1)} %shard_map.81), channel_id=1, source_target_pairs={{4,8},{8,4},{12,16},{16,12},{20,24},{24,20},{28,32},{32,28},{36,40... | collective-permute-start | bytes 589832 | tf_op jit(solution)/shard_map/ppermute | solution.py:233
  45.5 9.5 %collective-permute-start.3 = (bf16[32,3072]{1,0:T(8,128)(2,1)S(1)}, bf16[32,3072]{1,0:T(8,128)(2,1)S(1)}, u32[]{:S(2)}, u32[]{:S(2)}) collective-permute-start(bf16[32,3072]{1,0:T(8,128)(2,1)S(1)} %shard_map.80), channel_id=1, source_target_pairs={{0,4},{4,0},{8,12},{12,8},{16,20},{20,16},{24,28},{28,24},{32,36},... | collective-permute-start | bytes 589832 | tf_op jit(solution)/shard_map/ppermute | solution.py:233
  49.2 11.1 %collective-permute-start.6 = (bf16[32,3072]{1,0:T(8,128)(2,1)S(1)}, bf16[32,3072]{1,0:T(8,128)(2,1)S(1)}, u32[]{:S(2)}, u32[]{:S(2)}) collective-permute-start(bf16[32,3072]{1,0:T(8,128)(2,1)S(1)} %shard_map.83), channel_id=1, source_target_pairs={{0,4},{4,0},{8,12},{12,8},{16,20},{20,16},{24,28},{28,24},{32,36},... | collective-permute-start | bytes 589832 | tf_op jit(solution)/shard_map/ppermute | solution.py:233
  55.1 9.9 %collective-permute-start.5 = (bf16[32,3072]{1,0:T(8,128)(2,1)S(1)}, bf16[32,3072]{1,0:T(8,128)(2,1)S(1)}, u32[]{:S(2)}, u32[]{:S(2)}) collective-permute-start(bf16[32,3072]{1,0:T(8,128)(2,1)S(1)} %shard_map.82), channel_id=1, source_target_pairs={{4,8},{8,4},{12,16},{16,12},{20,24},{24,20},{28,32},{32,28},{36,40... | collective-permute-start | bytes 589832 | tf_op jit(solution)/shard_map/ppermute | solution.py:233
  60.3 8.8 %collective-permute-start.8 = (bf16[32,3072]{1,0:T(8,128)(2,1)S(1)}, bf16[32,3072]{1,0:T(8,128)(2,1)S(1)}, u32[]{:S(2)}, u32[]{:S(2)}) collective-permute-start(bf16[32,3072]{1,0:T(8,128)(2,1)S(1)} %shard_map.85), channel_id=1, source_target_pairs={{4,8},{8,4},{12,16},{16,12},{20,24},{24,20},{28,32},{32,28},{36,40... | collective-permute-start | bytes 589832 | tf_op jit(solution)/shard_map/ppermute | solution.py:233
  65.0 7.7 %collective-permute-start.7 = (bf16[32,3072]{1,0:T(8,128)(2,1)S(1)}, bf16[32,3072]{1,0:T(8,128)(2,1)S(1)}, u32[]{:S(2)}, u32[]{:S(2)}) collective-permute-start(bf16[32,3072]{1,0:T(8,128)(2,1)S(1)} %shard_map.84), channel_id=1, source_target_pairs={{0,4},{4,0},{8,12},{12,8},{16,20},{20,16},{24,28},{28,24},{32,36},... | collective-permute-start | bytes 589832 | tf_op jit(solution)/shard_map/ppermute | solution.py:233
  69.2 12.0 %collective-permute-start.10 = (bf16[32,3072]{1,0:T(8,128)(2,1)S(1)}, bf16[32,3072]{1,0:T(8,128)(2,1)S(1)}, u32[]{:S(2)}, u32[]{:S(2)}) collective-permute-start(bf16[32,3072]{1,0:T(8,128)(2,1)S(1)} %shard_map.87), channel_id=1, source_target_pairs={{0,4},{4,0},{8,12},{12,8},{16,20},{20,16},{24,28},{28,24},{32,36},... | collective-permute-start | bytes 589832 | tf_op jit(solution)/shard_map/ppermute | solution.py:233
  72.8 8.8 %collective-permute-start.9 = (bf16[32,3072]{1,0:T(8,128)(2,1)S(1)}, bf16[32,3072]{1,0:T(8,128)(2,1)S(1)}, u32[]{:S(2)}, u32[]{:S(2)}) collective-permute-start(bf16[32,3072]{1,0:T(8,128)(2,1)S(1)} %shard_map.86), channel_id=1, source_target_pairs={{4,8},{8,4},{12,16},{16,12},{20,24},{24,20},{28,32},{32,28},{36,40... | collective-permute-start | bytes 589832 | tf_op jit(solution)/shard_map/ppermute | solution.py:233
  79.8 22.0 %collective-permute-start.11 = (bf16[512,384]{1,0:T(8,128)(2,1)S(1)}, bf16[512,384]{1,0:T(8,128)(2,1)S(1)}, u32[]{:S(2)}, u32[]{:S(2)}) collective-permute-start(bf16[512,384]{1,0:T(8,128)(2,1)S(1)} %get-tuple-element.42), channel_id=1, source_target_pairs={{384,0},{385,1},{386,2},{387,3},{388,4},{389,5},{390,6},{391,7},{3... | collective-permute-start | bytes 1179656 | tf_op jit(solution)/shard_map/ppermute | solution.py:290
  82.3 18.9 %all-to-all-start = ((bf16[4,8,3072]{2,1,0:T(8,128)(2,1)}), bf16[4,8,3072]{2,1,0:T(8,128)(2,1)S(1)}, u32[]{:S(2)}, u32[]{:S(2)}) async-start(bf16[4,8,3072]{2,1,0:T(8,128)(2,1)} %fusion.2), calls=%async_computation | async-start | bytes 393216 | tf_op jit(solution)/shard_map/all_to_all | solution.py:279

commit v10 on v9

--- a/solution.py
+++ b/solution.py
@@ -270,12 +270,24 @@
         short = swapped(mine_short, 1 - link)
         mine = joined(block(link, k), long)
         long = swapped(mine, link)
-    return own + long.astype(F32) + short.astype(F32)
-
-
-def sum_over_y(rows_sum):
+    vmem = pl.BlockSpec(memory_space=pltpu.VMEM)
     peers = lax.axis_size("dy")
-    tiles = rows_sum.astype(BF16).reshape(peers, rows_sum.shape[0] // peers, rows_sum.shape[1])
+    return pl.pallas_call(
+        total_kernel,
+        in_specs=[vmem] * 3,
+        out_specs=vmem,
+        out_shape=jax.ShapeDtypeStruct((peers, ROWS // peers, WIDTH), BF16),
+        compiler_params=pltpu.CompilerParams(vmem_limit_bytes=4 * 1024 * 1024),
+    )(own, long, short)
+
+
+def total_kernel(own, long, short, out):
+    for i in range(out.shape[0]):
+        rows = slice(i * out.shape[1], (i + 1) * out.shape[1])
+        out[i] = (own[rows, :] + long[rows, :].astype(F32) + short[rows, :].astype(F32)).astype(BF16)
+
+
+def sum_over_y(tiles):
     arrived = lax.all_to_all(tiles, "dy", split_axis=0, concat_axis=0, tiled=True)
     return arrived.astype(F32).sum(axis=0)
 
@@ -289,8 +301,8 @@
     norm_back, above_grad = backward(arrived, stats, gain, top_grad, stream[0])
     below_grad = lax.ppermute(above_grad, "section", [(1, 0)])
     lower_grad = (below_grad.astype(F32) + norm_back).astype(BF16)
-    result = jnp.where(section_index == 0, lower_grad, above_grad)
-    return (weight_grad, result[None])
+    result = jnp.where(section_index == 0, lower_grad, above_grad)[None]
+    return (weight_grad, result)
 
 
 def solution(mesh):

time: 103 us -> 103 us (level)
  no operation moved by 1% of the time
where the time goes in v10:
time: 103 us
  starting transfers between devices  60.2 us (58%)
  waiting for transfers between devices  27.1 us (26%)
  Pallas kernels  12.4 us (12%)
  other arithmetic  1.55 us (2%)
  between operations  1.51 us (1%)
    ppermute x11, starting transfers between devices, swapped(): return lax.ppermute(value, 'dz', pairs)  36.9 us
    ppermute x11, waiting for transfers between devices, swapped(): return lax.ppermute(value, 'dz', pairs)  16.3 us
    all_to_all x1, starting transfers between devices, shards(): arrived = lax.all_to_all(tiles, MP, split_axis=0, concat_axis=0, tiled=True)  13.8 us
    all_to_all x1, waiting for transfers between devices, sum_over_y(): lax.all_to_all(tiles, 'dy', split_axis=0, concat_axis=0, tiled=True)  10.7 us
    all_to_all x1, starting transfers between devices, sum_over_y(): lax.all_to_all(tiles, 'dy', split_axis=0, concat_axis=0, tiled=True)  8.19 us
    pallas_call x1, Pallas kernels, front(): pl.pallas_call(front_kernel, in_specs=[pl.BlockSpec(memory_space=pltpu.SM...  5.21 us
    pallas_call x1, Pallas kernels, parts(): pl.pallas_call(parts_kernel, in_specs=[vmem] * 5, out_specs=pl.BlockSpec(...  3.62 us
    pallas_call x1, Pallas kernels, backward(): pl.pallas_call(back_kernel, in_specs=[hbm, vmem, vmem, hbm, hbm], out_spe...  2.37 us
  transfers between devices with their start and end apart: 14, of which 9 were waited for; matrix products, arithmetic and copies ran while one was open for 1% of the time, Pallas kernels for 3%

profile of v10, /device:TPU:6, one launch (start us, length us, event | category | flops | bytes accessed | tf_op | source)
XLA Modules:
  0.0 102.8 jit_solution(3623582967964742173)
XLA Ops:
  1.3 0.0 copy-start
  1.3 0.0 copy-start.1
  1.3 0.0 copy-start.2
  1.3 5.2 %shard_map.77 = (bf16[512,3072]{1,0:T(8,128)(2,1)S(1)}, f32[2,512,128]{2,1,0:T(8,128)S(1)}, f32[32,3072]{1,0:T(8,128)S(1)}, bf16[32,3072]{1,0:T(8,128)(2,1)S(1)}...) custom-call(s32[1]{0:T(128)S(6)} %copy.8.counts, ...), custom_call_target="tpu_custom_call" | custom-call | flops 4831838208 | bytes 8000000 | tf_op jit(solution)/shard_map/pallas_call | solution.py:91
  6.5 0.0 copy-done
  6.5 0.0 copy-done.1
  6.5 0.0 copy-done.2
  6.6 3.6 %shard_map.79 = bf16[8,520,384]{2,1,0:T(8,128)(2,1)} custom-call(bf16[512,384]{1,0:T(8,128)(2,1)S(1)} %bitcast.8, bf16[384,3072]{1,0:T(8,128)(2,1)S(1)} %bitcast.6, bf16[512,3072]{1,0:T(8,128)(2,1)S(1)} %get-tuple-element.31.held, f32[1,3072]{1,0:T(1,128)S(1)} %copy-done, f32[2,512,128]{2,1,0:T(8,128)S(1)} %get-tuple-element.32.stats), custom_call_target="tpu_custom_call" | custom-call | flops 3623878656 | bytes 9000000 | tf_op jit(solution)/shard_map/pallas_call | solution.py:150
  10.2 13.8 %all-to-all-start.1 = ((bf16[8,520,384]{2,1,0:T(8,128)(2,1)}), bf16[8,520,384]{2,1,0:T(8,128)(2,1)}, u32[]{:S(2)}, u32[]{:S(2)}) async-start(bf16[8,520,384]{2,1,0:T(8,128)(2,1)} %shard_map.79), calls=%async_computation.1 | async-start | bytes 6389760 | tf_op jit(solution)/shard_map/all_to_all | solution.py:300
  24.0 1.9 %collective-permute-start = (bf16[32,3072]{1,0:T(8,128)(2,1)S(1)}, bf16[32,3072]{1,0:T(8,128)(2,1)S(1)}, u32[]{:S(2)}, u32[]{:S(2)}) collective-permute-start(bf16[32,3072]{1,0:T(8,128)(2,1)S(1)} %get-tuple-element.29), channel_id=1, source_target_pairs={{0,4},{4,0},{8,12},{12,8},{16,20},{20,16},{24,28},{28,24},{32,36},... | collective-permute-start | bytes 589832 | tf_op jit(solution)/shard_map/ppermute | solution.py:233
  25.9 3.9 %collective-permute-start.2 = (bf16[32,3072]{1,0:T(8,128)(2,1)S(1)}, bf16[32,3072]{1,0:T(8,128)(2,1)S(1)}, u32[]{:S(2)}, u32[]{:S(2)}) collective-permute-start(bf16[32,3072]{1,0:T(8,128)(2,1)S(1)} %get-tuple-element.33), channel_id=1, source_target_pairs={{0,4},{4,0},{8,12},{12,8},{16,20},{20,16},{24,28},{28,24},{32,36},... | collective-permute-start | bytes 589832 | tf_op jit(solution)/shard_map/ppermute | solution.py:233
  29.8 1.7 %collective-permute-done.got = bf16[32,3072]{1,0:T(8,128)(2,1)S(1)} collective-permute-done((bf16[32,3072]{1,0:T(8,128)(2,1)S(1)}, bf16[32,3072]{1,0:T(8,128)(2,1)S(1)}, u32[]{:S(2)}, u32[]{:S(2)}) %collective-permute-start) | collective-permute-done | bytes 196640 | tf_op jit(solution)/shard_map/ppermute | solution.py:233
  31.5 0.1 shard_map.78
  31.6 8.7 %collective-permute-start.1 = (bf16[32,3072]{1,0:T(8,128)(2,1)S(1)}, bf16[32,3072]{1,0:T(8,128)(2,1)S(1)}, u32[]{:S(2)}, u32[]{:S(2)}) collective-permute-start(bf16[32,3072]{1,0:T(8,128)(2,1)S(1)} %shard_map.78), channel_id=1, source_target_pairs={{4,8},{8,4},{12,16},{16,12},{20,24},{24,20},{28,32},{32,28},{36,40... | collective-permute-start | bytes 589832 | tf_op jit(solution)/shard_map/ppermute | solution.py:233
  40.3 0.0 collective-permute-done.2.got
  40.3 0.1 shard_map.81
  40.3 2.4 %collective-permute-start.4 = (bf16[32,3072]{1,0:T(8,128)(2,1)S(1)}, bf16[32,3072]{1,0:T(8,128)(2,1)S(1)}, u32[]{:S(2)}, u32[]{:S(2)}) collective-permute-start(bf16[32,3072]{1,0:T(8,128)(2,1)S(1)} %shard_map.81), channel_id=1, source_target_pairs={{4,8},{8,4},{12,16},{16,12},{20,24},{24,20},{28,32},{32,28},{36,40... | collective-permute-start | bytes 589832 | tf_op jit(solution)/shard_map/ppermute | solution.py:233
  42.8 2.7 %collective-permute-done.1.got = bf16[32,3072]{1,0:T(8,128)(2,1)S(1)} collective-permute-done((bf16[32,3072]{1,0:T(8,128)(2,1)S(1)}, bf16[32,3072]{1,0:T(8,128)(2,1)S(1)}, u32[]{:S(2)}, u32[]{:S(2)}) %collective-permute-start.1) | collective-permute-done | bytes 196640 | tf_op jit(solution)/shard_map/ppermute | solution.py:233
  45.5 0.1 shard_map.80
  45.5 1.9 %collective-permute-start.3 = (bf16[32,3072]{1,0:T(8,128)(2,1)S(1)}, bf16[32,3072]{1,0:T(8,128)(2,1)S(1)}, u32[]{:S(2)}, u32[]{:S(2)}) collective-permute-start(bf16[32,3072]{1,0:T(8,128)(2,1)S(1)} %shard_map.80), channel_id=1, source_target_pairs={{0,4},{4,0},{8,12},{12,8},{16,20},{20,16},{24,28},{28,24},{32,36},... | collective-permute-start | bytes 589832 | tf_op jit(solution)/shard_map/ppermute | solution.py:233
  47.5 1.7 %collective-permute-done.4.got = bf16[32,3072]{1,0:T(8,128)(2,1)S(1)} collective-permute-done((bf16[32,3072]{1,0:T(8,128)(2,1)S(1)}, bf16[32,3072]{1,0:T(8,128)(2,1)S(1)}, u32[]{:S(2)}, u32[]{:S(2)}) %collective-permute-start.4) | collective-permute-done | bytes 196640 | tf_op jit(solution)/shard_map/ppermute | solution.py:233
  49.1 0.1 shard_map.83
  49.2 2.3 %collective-permute-start.6 = (bf16[32,3072]{1,0:T(8,128)(2,1)S(1)}, bf16[32,3072]{1,0:T(8,128)(2,1)S(1)}, u32[]{:S(2)}, u32[]{:S(2)}) collective-permute-start(bf16[32,3072]{1,0:T(8,128)(2,1)S(1)} %shard_map.83), channel_id=1, source_target_pairs={{0,4},{4,0},{8,12},{12,8},{16,20},{20,16},{24,28},{28,24},{32,36},... | collective-permute-start | bytes 589832 | tf_op jit(solution)/shard_map/ppermute | solution.py:233
  51.5 3.5 %collective-permute-done.3.got = bf16[32,3072]{1,0:T(8,128)(2,1)S(1)} collective-permute-done((bf16[32,3072]{1,0:T(8,128)(2,1)S(1)}, bf16[32,3072]{1,0:T(8,128)(2,1)S(1)}, u32[]{:S(2)}, u32[]{:S(2)}) %collective-permute-start.3) | collective-permute-done | bytes 196640 | tf_op jit(solution)/shard_map/ppermute | solution.py:233
  55.0 0.1 shard_map.82
  55.1 5.2 %collective-permute-start.5 = (bf16[32,3072]{1,0:T(8,128)(2,1)S(1)}, bf16[32,3072]{1,0:T(8,128)(2,1)S(1)}, u32[]{:S(2)}, u32[]{:S(2)}) collective-permute-start(bf16[32,3072]{1,0:T(8,128)(2,1)S(1)} %shard_map.82), channel_id=1, source_target_pairs={{4,8},{8,4},{12,16},{16,12},{20,24},{24,20},{28,32},{32,28},{36,40... | collective-permute-start | bytes 589832 | tf_op jit(solution)/shard_map/ppermute | solution.py:233
  60.3 0.0 collective-permute-done.6.got
  60.3 0.1 shard_map.85
  60.3 2.0 %collective-permute-start.8 = (bf16[32,3072]{1,0:T(8,128)(2,1)S(1)}, bf16[32,3072]{1,0:T(8,128)(2,1)S(1)}, u32[]{:S(2)}, u32[]{:S(2)}) collective-permute-start(bf16[32,3072]{1,0:T(8,128)(2,1)S(1)} %shard_map.85), channel_id=1, source_target_pairs={{4,8},{8,4},{12,16},{16,12},{20,24},{24,20},{28,32},{32,28},{36,40... | collective-permute-start | bytes 589832 | tf_op jit(solution)/shard_map/ppermute | solution.py:233
  62.4 2.5 %collective-permute-done.5.got = bf16[32,3072]{1,0:T(8,128)(2,1)S(1)} collective-permute-done((bf16[32,3072]{1,0:T(8,128)(2,1)S(1)}, bf16[32,3072]{1,0:T(8,128)(2,1)S(1)}, u32[]{:S(2)}, u32[]{:S(2)}) %collective-permute-start.5) | collective-permute-done | bytes 196640 | tf_op jit(solution)/shard_map/ppermute | solution.py:233
  64.9 0.1 shard_map.84
  65.0 1.9 %collective-permute-start.7 = (bf16[32,3072]{1,0:T(8,128)(2,1)S(1)}, bf16[32,3072]{1,0:T(8,128)(2,1)S(1)}, u32[]{:S(2)}, u32[]{:S(2)}) collective-permute-start(bf16[32,3072]{1,0:T(8,128)(2,1)S(1)} %shard_map.84), channel_id=1, source_target_pairs={{0,4},{4,0},{8,12},{12,8},{16,20},{20,16},{24,28},{28,24},{32,36},... | collective-permute-start | bytes 589832 | tf_op jit(solution)/shard_map/ppermute | solution.py:233
  66.9 2.2 %collective-permute-done.8.got = bf16[32,3072]{1,0:T(8,128)(2,1)S(1)} collective-permute-done((bf16[32,3072]{1,0:T(8,128)(2,1)S(1)}, bf16[32,3072]{1,0:T(8,128)(2,1)S(1)}, u32[]{:S(2)}, u32[]{:S(2)}) %collective-permute-start.8) | collective-permute-done | bytes 196640 | tf_op jit(solution)/shard_map/ppermute | solution.py:233
  69.1 0.1 shard_map.87
  69.2 1.9 %collective-permute-start.10 = (bf16[32,3072]{1,0:T(8,128)(2,1)S(1)}, bf16[32,3072]{1,0:T(8,128)(2,1)S(1)}, u32[]{:S(2)}, u32[]{:S(2)}) collective-permute-start(bf16[32,3072]{1,0:T(8,128)(2,1)S(1)} %shard_map.87), channel_id=1, source_target_pairs={{0,4},{4,0},{8,12},{12,8},{16,20},{20,16},{24,28},{28,24},{32,36},... | collective-permute-start | bytes 589832 | tf_op jit(solution)/shard_map/ppermute | solution.py:233
  71.1 1.6 %collective-permute-done.7.got = bf16[32,3072]{1,0:T(8,128)(2,1)S(1)} collective-permute-done((bf16[32,3072]{1,0:T(8,128)(2,1)S(1)}, bf16[32,3072]{1,0:T(8,128)(2,1)S(1)}, u32[]{:S(2)}, u32[]{:S(2)}) %collective-permute-start.7) | collective-permute-done | bytes 196640 | tf_op jit(solution)/shard_map/ppermute | solution.py:233
  72.8 4.7 %collective-permute-start.9 = (bf16[32,3072]{1,0:T(8,128)(2,1)S(1)}, bf16[32,3072]{1,0:T(8,128)(2,1)S(1)}, u32[]{:S(2)}, u32[]{:S(2)}) collective-permute-start(bf16[32,3072]{1,0:T(8,128)(2,1)S(1)} %shard_map.86), channel_id=1, source_target_pairs={{4,8},{8,4},{12,16},{16,12},{20,24},{24,20},{28,32},{32,28},{36,40... | collective-permute-start | bytes 589832 | tf_op jit(solution)/shard_map/ppermute | solution.py:233
  77.4 0.0 all-to-all-done.1.sent
  77.5 2.4 %shard_map.89 = (f32[512,384]{1,0:T(8,128)S(1)}, bf16[512,384]{1,0:T(8,128)(2,1)S(1)}) custom-call(bf16[8,520,384]{2,1,0:T(8,128)(2,1)} %all-to-all-done.1.sent, f32[2,512,128]{2,1,0:T(8,128)S(1)} %get-tuple-element.32.stats, f32[1,3072]{1,0:T(1,128)S(1)} %copy-done, bf16[512,3072]{1,0:T(8,128)(2,1)} %top.1, bf16[512,3072]{1,0:T(8,128)(2,1)} %bitcast.10), custom_call_target="tpu_custom_call" | custom-call | flops 500000000 | bytes 6000000 | tf_op jit(solution)/shard_map/pallas_call | solution.py:211
  79.8 1.3 %collective-permute-start.11 = (bf16[512,384]{1,0:T(8,128)(2,1)S(1)}, bf16[512,384]{1,0:T(8,128)(2,1)S(1)}, u32[]{:S(2)}, u32[]{:S(2)}) collective-permute-start(bf16[512,384]{1,0:T(8,128)(2,1)S(1)} %get-tuple-element.42), channel_id=1, source_target_pairs={{384,0},{385,1},{386,2},{387,3},{388,4},{389,5},{390,6},{391,7},{3... | collective-permute-start | bytes 1179656 | tf_op jit(solution)/shard_map/ppermute | solution.py:302
  81.1 0.0 collective-permute-done.10.short
  81.1 0.4 collective-permute-done.9.long
  81.5 0.7 shard_map.88
  82.3 8.2 %all-to-all-start = ((bf16[4,8,3072]{2,1,0:T(8,128)(2,1)}), bf16[4,8,3072]{2,1,0:T(8,128)(2,1)S(1)}, u32[]{:S(2)}, u32[]{:S(2)}) async-start(bf16[4,8,3072]{2,1,0:T(8,128)(2,1)} %shard_map.88), calls=%async_computation | async-start | bytes 393216 | tf_op jit(solution)/shard_map/all_to_all | solution.py:291
  90.5 10.7 %all-to-all-done = bf16[4,8,3072]{2,1,0:T(8,128)(2,1)S(1)} async-done(((bf16[4,8,3072]{2,1,0:T(8,128)(2,1)}), bf16[4,8,3072]{2,1,0:T(8,128)(2,1)S(1)}, u32[]{:S(2)}, u32[]{:S(2)}) %all-to-all-start) | async-done | bytes 196640 | tf_op jit(solution)/shard_map/all_to_all | solution.py:291
  101.2 0.7 reduce_sum.12
  101.9 0.0 collective-permute-done.11
  101.9 0.9 fusion.1
  (1 shorter events, 0.0 us)
Async XLA Ops:
  1.3 5.2 %copy-start = (f32[1,3072]{1,0:T(1,128)S(1)}, f32[1,3072]{1,0:T(1,128)}, u32[]{:S(2)}) copy-start(f32[1,3072]{1,0:T(1,128)} %gain.3) | copy-start | bytes 36868
  1.3 5.2 %copy-start.1 = (bf16[1,384,3072]{2,1,0:T(8,128)(2,1)S(1)}, bf16[1,384,3072]{2,1,0:T(8,128)(2,1)}, u32[]{:S(2)}) copy-start(bf16[1,384,3072]{2,1,0:T(8,128)(2,1)} %param.8) | copy-start | bytes 7077892
  1.3 5.2 %copy-start.2 = (bf16[1,512,384]{2,1,0:T(8,128)(2,1)S(1)}, bf16[1,512,384]{2,1,0:T(8,128)(2,1)}, u32[]{:S(2)}) copy-start(bf16[1,512,384]{2,1,0:T(8,128)(2,1)} %param.6) | copy-start | bytes 1179652
  10.2 67.3 %all-to-all-start.1 = ((bf16[8,520,384]{2,1,0:T(8,128)(2,1)}), bf16[8,520,384]{2,1,0:T(8,128)(2,1)}, u32[]{:S(2)}, u32[]{:S(2)}) async-start(bf16[8,520,384]{2,1,0:T(8,128)(2,1)} %shard_map.79), calls=%async_computation.1 | async-start | bytes 6389760 | tf_op jit(solution)/shard_map/all_to_all | solution.py:300
  24.0 7.6 %collective-permute-start = (bf16[32,3072]{1,0:T(8,128)(2,1)S(1)}, bf16[32,3072]{1,0:T(8,128)(2,1)S(1)}, u32[]{:S(2)}, u32[]{:S(2)}) collective-permute-start(bf16[32,3072]{1,0:T(8,128)(2,1)S(1)} %get-tuple-element.29), channel_id=1, source_target_pairs={{0,4},{4,0},{8,12},{12,8},{16,20},{20,16},{24,28},{28,24},{32,36},... | collective-permute-start | bytes 589832 | tf_op jit(solution)/shard_map/ppermute | solution.py:233
  25.9 14.4 %collective-permute-start.2 = (bf16[32,3072]{1,0:T(8,128)(2,1)S(1)}, bf16[32,3072]{1,0:T(8,128)(2,1)S(1)}, u32[]{:S(2)}, u32[]{:S(2)}) collective-permute-start(bf16[32,3072]{1,0:T(8,128)(2,1)S(1)} %get-tuple-element.33), channel_id=1, source_target_pairs={{0,4},{4,0},{8,12},{12,8},{16,20},{20,16},{24,28},{28,24},{32,36},... | collective-permute-start | bytes 589832 | tf_op jit(solution)/shard_map/ppermute | solution.py:233
  31.6 13.9 %collective-permute-start.1 = (bf16[32,3072]{1,0:T(8,128)(2,1)S(1)}, bf16[32,3072]{1,0:T(8,128)(2,1)S(1)}, u32[]{:S(2)}, u32[]{:S(2)}) collective-permute-start(bf16[32,3072]{1,0:T(8,128)(2,1)S(1)} %shard_map.78), channel_id=1, source_target_pairs={{4,8},{8,4},{12,16},{16,12},{20,24},{24,20},{28,32},{32,28},{36,40... | collective-permute-start | bytes 589832 | tf_op jit(solution)/shard_map/ppermute | solution.py:233
  40.3 8.8 %collective-permute-start.4 = (bf16[32,3072]{1,0:T(8,128)(2,1)S(1)}, bf16[32,3072]{1,0:T(8,128)(2,1)S(1)}, u32[]{:S(2)}, u32[]{:S(2)}) collective-permute-start(bf16[32,3072]{1,0:T(8,128)(2,1)S(1)} %shard_map.81), channel_id=1, source_target_pairs={{4,8},{8,4},{12,16},{16,12},{20,24},{24,20},{28,32},{32,28},{36,40... | collective-permute-start | bytes 589832 | tf_op jit(solution)/shard_map/ppermute | solution.py:233
  45.5 9.5 %collective-permute-start.3 = (bf16[32,3072]{1,0:T(8,128)(2,1)S(1)}, bf16[32,3072]{1,0:T(8,128)(2,1)S(1)}, u32[]{:S(2)}, u32[]{:S(2)}) collective-permute-start(bf16[32,3072]{1,0:T(8,128)(2,1)S(1)} %shard_map.80), channel_id=1, source_target_pairs={{0,4},{4,0},{8,12},{12,8},{16,20},{20,16},{24,28},{28,24},{32,36},... | collective-permute-start | bytes 589832 | tf_op jit(solution)/shard_map/ppermute | solution.py:233
  49.2 11.1 %collective-permute-start.6 = (bf16[32,3072]{1,0:T(8,128)(2,1)S(1)}, bf16[32,3072]{1,0:T(8,128)(2,1)S(1)}, u32[]{:S(2)}, u32[]{:S(2)}) collective-permute-start(bf16[32,3072]{1,0:T(8,128)(2,1)S(1)} %shard_map.83), channel_id=1, source_target_pairs={{0,4},{4,0},{8,12},{12,8},{16,20},{20,16},{24,28},{28,24},{32,36},... | collective-permute-start | bytes 589832 | tf_op jit(solution)/shard_map/ppermute | solution.py:233
  55.1 9.9 %collective-permute-start.5 = (bf16[32,3072]{1,0:T(8,128)(2,1)S(1)}, bf16[32,3072]{1,0:T(8,128)(2,1)S(1)}, u32[]{:S(2)}, u32[]{:S(2)}) collective-permute-start(bf16[32,3072]{1,0:T(8,128)(2,1)S(1)} %shard_map.82), channel_id=1, source_target_pairs={{4,8},{8,4},{12,16},{16,12},{20,24},{24,20},{28,32},{32,28},{36,40... | collective-permute-start | bytes 589832 | tf_op jit(solution)/shard_map/ppermute | solution.py:233
  60.3 8.8 %collective-permute-start.8 = (bf16[32,3072]{1,0:T(8,128)(2,1)S(1)}, bf16[32,3072]{1,0:T(8,128)(2,1)S(1)}, u32[]{:S(2)}, u32[]{:S(2)}) collective-permute-start(bf16[32,3072]{1,0:T(8,128)(2,1)S(1)} %shard_map.85), channel_id=1, source_target_pairs={{4,8},{8,4},{12,16},{16,12},{20,24},{24,20},{28,32},{32,28},{36,40... | collective-permute-start | bytes 589832 | tf_op jit(solution)/shard_map/ppermute | solution.py:233
  65.0 7.7 %collective-permute-start.7 = (bf16[32,3072]{1,0:T(8,128)(2,1)S(1)}, bf16[32,3072]{1,0:T(8,128)(2,1)S(1)}, u32[]{:S(2)}, u32[]{:S(2)}) collective-permute-start(bf16[32,3072]{1,0:T(8,128)(2,1)S(1)} %shard_map.84), channel_id=1, source_target_pairs={{0,4},{4,0},{8,12},{12,8},{16,20},{20,16},{24,28},{28,24},{32,36},... | collective-permute-start | bytes 589832 | tf_op jit(solution)/shard_map/ppermute | solution.py:233
  69.2 12.0 %collective-permute-start.10 = (bf16[32,3072]{1,0:T(8,128)(2,1)S(1)}, bf16[32,3072]{1,0:T(8,128)(2,1)S(1)}, u32[]{:S(2)}, u32[]{:S(2)}) collective-permute-start(bf16[32,3072]{1,0:T(8,128)(2,1)S(1)} %shard_map.87), channel_id=1, source_target_pairs={{0,4},{4,0},{8,12},{12,8},{16,20},{20,16},{24,28},{28,24},{32,36},... | collective-permute-start | bytes 589832 | tf_op jit(solution)/shard_map/ppermute | solution.py:233
  72.8 8.8 %collective-permute-start.9 = (bf16[32,3072]{1,0:T(8,128)(2,1)S(1)}, bf16[32,3072]{1,0:T(8,128)(2,1)S(1)}, u32[]{:S(2)}, u32[]{:S(2)}) collective-permute-start(bf16[32,3072]{1,0:T(8,128)(2,1)S(1)} %shard_map.86), channel_id=1, source_target_pairs={{4,8},{8,4},{12,16},{16,12},{20,24},{24,20},{28,32},{32,28},{36,40... | collective-permute-start | bytes 589832 | tf_op jit(solution)/shard_map/ppermute | solution.py:233
  79.8 22.0 %collective-permute-start.11 = (bf16[512,384]{1,0:T(8,128)(2,1)S(1)}, bf16[512,384]{1,0:T(8,128)(2,1)S(1)}, u32[]{:S(2)}, u32[]{:S(2)}) collective-permute-start(bf16[512,384]{1,0:T(8,128)(2,1)S(1)} %get-tuple-element.42), channel_id=1, source_target_pairs={{384,0},{385,1},{386,2},{387,3},{388,4},{389,5},{390,6},{391,7},{3... | collective-permute-start | bytes 1179656 | tf_op jit(solution)/shard_map/ppermute | solution.py:302
  82.3 18.9 %all-to-all-start = ((bf16[4,8,3072]{2,1,0:T(8,128)(2,1)}), bf16[4,8,3072]{2,1,0:T(8,128)(2,1)S(1)}, u32[]{:S(2)}, u32[]{:S(2)}) async-start(bf16[4,8,3072]{2,1,0:T(8,128)(2,1)} %shard_map.88), calls=%async_computation | async-start | bytes 393216 | tf_op jit(solution)/shard_map/all_to_all | solution.py:291
